TPU v7x, 128 devices: a whole 4x4x4 slice. The times are simulated.
128 devices in a mesh: dp: 64 (over y, x, z_lo, core), mp: 2 (over z_hi).
Axes of the slice: x: 4, y: 4, z: 4 (z_hi: 2, z_lo: 2; z = z_hi * 2 + z_lo), core: 2. Of those that a mesh axis runs over, the one named last changes fastest.
Arguments:
- clean_latent: float32 [64, 4096], P('dp'), may hold values from -6 to 6
- noise_draw: float32 [64, 4096], P('dp'), may hold values from -6 to 6
- timestep: int32 [64], P('dp'), may hold values from 1 to 8
- bucket: int32 [64], P('dp'), may hold values from 0 to 7
- bucket_weights: float32 [8], replicated, may hold values from 0.25 to 4
- teacher_embed: float32 [16, 2048], replicated, may hold values from -1.5 to 1.5
- teacher_final: float32 [16, 2048], replicated, may hold values from -0.125 to 0.125
- teacher_mod: float32 [16, 3, 2048], replicated, may hold values from -3 to 3
- teacher_qkv: bfloat16 [2048, 3, 1024], P(None, None, 'mp'), may hold values from -1 to 1
- teacher_out: bfloat16 [2048, 1024], P(None, 'mp'), may hold values from -0.1875 to 0.1875
- student_embed: float32 [16, 2048], replicated, may hold values from -1.5 to 1.5
- student_final: float32 [16, 2048], replicated, may hold values from -0.125 to 0.125
- student_mod: float32 [8, 3, 2048], replicated, may hold values from -3 to 3
- student_qkv: bfloat16 [2048, 3, 1024], P('dp', None, 'mp'), may hold values from -1 to 1
- student_out: bfloat16 [2048, 1024], P('dp', 'mp'), may hold values from -0.1875 to 0.1875
- moment_qkv: float32 [2048, 3, 1024], P('dp', None, 'mp'), may hold values from -2 to 2
- second_qkv: float32 [2048, 3, 1024], P('dp', None, 'mp'), may hold values from 0.05 to 0.5
- moment_out: float32 [2048, 1024], P('dp', 'mp'), may hold values from -2 to 2
- second_out: float32 [2048, 1024], P('dp', 'mp'), may hold values from 0.05 to 0.5
Outputs:
- new_moment_qkv: float32 [2048, 3, 1024], P('dp', None, 'mp')
- new_second_qkv: float32 [2048, 3, 1024], P('dp', None, 'mp')
- update_qkv: float32 [2048, 3, 1024], P('dp', None, 'mp')
- new_moment_out: float32 [2048, 1024], P('dp', 'mp')
- new_second_out: float32 [2048, 1024], P('dp', 'mp')
- update_out: float32 [2048, 1024], P('dp', 'mp')
- loss: float32 [], replicated
All inputs are finite; a program needn't handle non-finite values.
Results may differ from a plain program's by a relative error of at most 0.00035.
Values may be sent and summed in bfloat16 or wider, within the bound.
A program may use at most 128 MiB of HBM per device.

v0:
```python
import math

import jax
import jax.numpy as jnp
from jax import lax
from jax.sharding import Mesh
from jax.sharding import PartitionSpec as P

D = 2048
HS = 64
INNER = 1024
PATCH_CH = 16
SEQ = 256
LATENT = 4096
K = 8
TGRID = 16
NBUCKET = 8
DP = ("dp_0", "dp_1", "dp_2", "dp_3")
DP_MP = ("dp_0", "dp_1", "dp_2", "dp_3", "mp")


LN_EPS = 0.01
BETA_ONE = 0.9
BETA_TWO = 0.99
ADAM_EPS = 1e-08


def in_blocks(shard, dim, devices):
    before, after = (shard.shape[:dim], shard.shape[dim + 1 :])
    return jnp.moveaxis(shard.reshape(*before, devices, -1, *after), dim, 0)


def summed_on_arrival(shard, axis, dim):
    devices = lax.axis_size(axis)
    parts = lax.all_to_all(in_blocks(shard, dim, devices), axis, 0, 0, tiled=True)
    return jnp.sum(parts, axis=0)


def side_by_side(arrays, axis, dim, along):
    widths = [math.prod(a.shape[along:]) for a in arrays]
    both = jnp.concatenate(
        [a.reshape(*a.shape[:along], w) for a, w in zip(arrays, widths)], axis=along
    )
    whole = lax.all_gather(both, axis, axis=dim, tiled=True)
    parts = jnp.split(whole, [sum(widths[:k]) for k in range(1, len(widths))], axis=along)
    return tuple((b.reshape(*whole.shape[:along], *a.shape[along:]) for a, b in zip(arrays, parts)))


def in_order(parts, dim):
    parts = jnp.moveaxis(parts, 0, dim)
    dims = parts.shape
    return parts.reshape(*dims[:dim], dims[dim] * dims[dim + 1], *dims[dim + 2 :])


def sent_to_all(shard, axis):
    copies = jnp.broadcast_to(shard, (lax.axis_size(axis), *shard.shape))
    return lax.all_to_all(copies, axis, split_axis=0, concat_axis=0, tiled=True)


def gathered_copies(shard, axis, dim):
    return in_order(sent_to_all(shard, axis), dim)


def by_axis(shard, axes):
    for axis in axes:
        shard = lax.psum(shard, axis)
    return shard


def summed_rows_2(shard, chips, core, dim):
    sizes = (lax.axis_size(chips), lax.axis_size(core))
    parts = in_blocks(shard, dim, sizes[0] * sizes[1])
    inside = parts.shape[1:]
    parts = parts.reshape(*sizes, *inside).swapaxes(0, 1).reshape(-1, *inside)
    parts = lax.psum_scatter(parts, core, scatter_dimension=0, tiled=True)
    return lax.psum_scatter(parts, chips, scatter_dimension=0, tiled=True)[0]


def plan():
    grid = jnp.arange(TGRID + 1, dtype=jnp.float32)
    lamb = 6.0 - 12.0 * grid / TGRID
    return (jnp.sqrt(jax.nn.sigmoid(lamb)), jnp.sqrt(jax.nn.sigmoid(-lamb)))


def positions():
    index = jnp.arange(SEQ, dtype=jnp.float32)[:, None]
    half = D // 2
    freqs = jnp.exp(-math.log(10000.0) * jnp.arange(half, dtype=jnp.float32) / half)
    angles = index * freqs[None, :]
    return jnp.concatenate([jnp.sin(angles), jnp.cos(angles)], axis=1)


def normalize(values):
    center = values - jnp.mean(values, axis=-1, keepdims=True)
    inverse = lax.rsqrt(jnp.mean(center * center, axis=-1, keepdims=True) + LN_EPS)
    return (center * inverse, inverse)


def norm_back(upstream, normed, inverse):
    first_mean = jnp.mean(upstream, axis=-1, keepdims=True)
    second_mean = jnp.mean(upstream * normed, axis=-1, keepdims=True)
    return (upstream - first_mean - normed * second_mean) * inverse


def one_hot_rows(index, width):
    return (index[:, None] == jnp.arange(width, dtype=jnp.int32)[None, :]).astype(jnp.float32)


def per_device(
    clean_latent,
    noise_draw,
    timestep,
    bucket,
    bucket_weights,
    teacher_embed,
    teacher_final,
    teacher_mod,
    teacher_qkv,
    teacher_out,
    student_embed,
    student_final,
    student_mod,
    student_qkv,
    student_out,
    moment_qkv,
    second_qkv,
    moment_out,
    second_out,
):
    samples = clean_latent.shape[0]
    rows_all = samples * SEQ
    local_inner = teacher_out.shape[1]
    local_heads = local_inner // HS
    count = rows_all // lax.axis_size("mp")
    start = lax.axis_index("mp") * count

    def take(values):
        return lax.dynamic_slice_in_dim(values, start, count, 0)

    alphas, sigmas = plan()
    table = jnp.stack([alphas, sigmas], axis=1)

    def coefficients(tau):
        picked = jnp.dot(one_hot_rows(tau, TGRID + 1), table, precision=lax.Precision.HIGHEST)
        picked = jnp.repeat(picked, SEQ, axis=0)
        return (picked[:, 0:1], picked[:, 1:2])

    def modulation(mod_table, index, length):
        picked = jnp.dot(
            one_hot_rows(index, length),
            mod_table.reshape(length, 3 * D),
            precision=lax.Precision.HIGHEST,
        )
        return picked.reshape(samples, 3, D)

    def gate_rows(modrows):
        return take(jnp.repeat(modrows[:, 2], SEQ, axis=0))

    placed = positions()

    def front(latent, modrows, embed, w_qkv, w_out):
        hidden = (
            jnp.dot(latent, embed, precision=lax.Precision.HIGHEST).reshape(samples, SEQ, D)
            + placed[None]
        )
        normed, unused = normalize(hidden)
        shaped = (
            (normed * (1.0 + modrows[:, None, 1]) + modrows[:, None, 0])
            .astype(jnp.bfloat16)
            .reshape(rows_all, D)
        )
        hidden = hidden.reshape(rows_all, D)
        packed = jnp.dot(
            shaped, w_qkv.reshape(D, 3 * local_inner), preferred_element_type=jnp.float32
        )
        packed = packed.astype(jnp.bfloat16).reshape(samples, SEQ, 3, local_heads, HS)
        queries = packed[:, :, 0]
        keys_all = packed[:, :, 1]
        values = packed[:, :, 2]
        scores = jnp.einsum(
            "sqhd,skhd->shqk", queries, keys_all, preferred_element_type=jnp.float32
        ) / math.sqrt(HS)
        highest = jnp.max(scores, axis=-1, keepdims=True)
        expos = jnp.exp(scores - highest)
        weights = expos / jnp.sum(expos, axis=-1, keepdims=True)
        rounded = weights.astype(jnp.bfloat16)
        attended = jnp.einsum(
            "shqk,skhd->sqhd", rounded, values, preferred_element_type=jnp.float32
        )
        attended = attended.astype(jnp.bfloat16).reshape(rows_all, local_inner)
        projected = lax.dot_general(
            attended, w_out, (((1,), (1,)), ((), ())), preferred_element_type=jnp.float32
        )
        return (hidden, shaped, queries, keys_all, values, weights, rounded, attended, projected)

    def reduce_heads(projected):
        return summed_on_arrival(projected, "mp", 0)

    def tail(hidden, modrows, projected, final):
        mixed = take(hidden) + gate_rows(modrows) * reduce_heads(projected)
        normed, inverse = normalize(mixed)
        predicted = lax.dot_general(
            normed, final, (((1,), (1,)), ((), ())), precision=lax.Precision.HIGHEST
        )
        return (predicted, normed, inverse)

    def teacher_eps(latent, modrows):
        parts = front(latent, modrows, teacher_embed, teacher_qkv, teacher_out)
        return tail(parts[0], modrows, parts[8], teacher_final)[0]

    whole_qkv, whole_out = side_by_side((student_qkv, student_out), DP, 0, 1)
    first = 2 * timestep
    middle = first - 1
    last = first - 2
    a_first, s_first = coefficients(first)
    a_middle, s_middle = coefficients(middle)
    a_last, s_last = coefficients(last)
    clean_rows = clean_latent.reshape(rows_all, PATCH_CH)
    noise_rows = noise_draw.reshape(rows_all, PATCH_CH)
    latent0 = a_first * clean_rows + s_first * noise_rows
    mine0 = take(latent0)
    af_mine, sf_mine = (take(a_first), take(s_first))
    am_mine, sm_mine = (take(a_middle), take(s_middle))
    al_mine, sl_mine = (take(a_last), take(s_last))
    eps_zero = teacher_eps(latent0, modulation(teacher_mod, first - 1, TGRID))
    next_mine = am_mine * (mine0 - sf_mine * eps_zero) / af_mine + sm_mine * eps_zero
    latent1 = gathered_copies(next_mine, "mp", 0)
    eps_one = teacher_eps(latent1, modulation(teacher_mod, middle - 1, TGRID))
    latent2 = al_mine * (take(latent1) - sm_mine * eps_one) / am_mine + sl_mine * eps_one
    target = (mine0 - af_mine / al_mine * latent2) / (sf_mine - af_mine * sl_mine / al_mine)
    student_rows_mod = modulation(student_mod, timestep - 1, K)
    hidden, shaped, queries, keys_all, values, weights, rounded, attended, projected = front(
        latent0, student_rows_mod, student_embed, whole_qkv, whole_out
    )
    predicted, normed, inverse = tail(hidden, student_rows_mod, projected, student_final)
    sample_weight = jnp.dot(
        one_hot_rows(bucket, NBUCKET), bucket_weights, precision=lax.Precision.HIGHEST
    )
    row_weight = take(jnp.repeat(sample_weight, SEQ, axis=0)[:, None])
    error = predicted - target
    loss_part = jnp.sum(row_weight * error * error)
    d_pred = 2.0 * row_weight * error
    d_normed = jnp.dot(d_pred, student_final, precision=lax.Precision.HIGHEST)
    d_mixed = norm_back(d_normed, normed, inverse)
    d_proj_mine = (gate_rows(student_rows_mod) * d_mixed).astype(jnp.bfloat16)
    d_proj = gathered_copies(d_proj_mine, "mp", 0)
    loss_sum = by_axis(loss_part, DP_MP)
    d_attn = jnp.dot(d_proj, whole_out, preferred_element_type=jnp.float32).astype(jnp.bfloat16)
    d_attn = d_attn.reshape(samples, SEQ, local_heads, HS)
    d_prob = jnp.einsum("sqhd,skhd->shqk", d_attn, values, preferred_element_type=jnp.float32)
    d_score = (
        weights * (d_prob - jnp.sum(weights * d_prob, axis=-1, keepdims=True)) / math.sqrt(HS)
    ).astype(jnp.bfloat16)
    d_query = jnp.einsum(
        "shqk,skhd->sqhd", d_score, keys_all, preferred_element_type=jnp.float32
    ).astype(jnp.bfloat16)
    d_key = jnp.einsum(
        "shqk,sqhd->skhd", d_score, queries, preferred_element_type=jnp.float32
    ).astype(jnp.bfloat16)
    d_value = jnp.einsum(
        "shqk,sqhd->skhd", rounded, d_attn, preferred_element_type=jnp.float32
    ).astype(jnp.bfloat16)
    d_pack = jnp.stack([d_query, d_key, d_value], axis=2).reshape(rows_all, 3 * local_inner)
    own_rows = D // lax.axis_size(DP)
    piece = shaped
    grad_qkv = lax.psum_scatter(
        lax.dot_general(
            piece, d_pack, (((0,), (0,)), ((), ())), preferred_element_type=jnp.float32
        ),
        DP,
        scatter_dimension=0,
        tiled=True,
    ).reshape(own_rows, 3, local_inner)
    piece = d_proj
    grad_out = summed_rows_2(
        lax.dot_general(
            piece, attended, (((0,), (0,)), ((), ())), preferred_element_type=jnp.float32
        ),
        ("dp_0", "dp_1", "dp_2"),
        "dp_3",
        0,
    )
    squares = jnp.sum(grad_qkv * grad_qkv) + jnp.sum(grad_out * grad_out)
    squares = by_axis(squares, DP_MP)
    rms_value = jnp.sqrt(squares / (4 * D * INNER))
    factor = 1.0 / jnp.maximum(rms_value, 1.0)

    def adam(moment, second, grad):
        normed_grad = grad * factor
        new_moment = BETA_ONE * moment + (1.0 - BETA_ONE) * normed_grad
        new_second = BETA_TWO * second + (1.0 - BETA_TWO) * normed_grad * normed_grad
        return (new_moment, new_second, new_moment / (jnp.sqrt(new_second) + ADAM_EPS))

    mq, vq, uq = adam(moment_qkv, second_qkv, grad_qkv)
    mo, vo, uo = adam(moment_out, second_out, grad_out)
    loss = loss_sum / (samples * lax.axis_size(DP) * LATENT)
    return (mq, vq, uq, mo, vo, uo, loss)


def solution(mesh):
    torus = Mesh(
        mesh.devices.reshape(4, 4, 2, 2, mesh.shape["mp"]), ("dp_0", "dp_1", "dp_2", "dp_3", "mp")
    )
    in_specs = (
        P(DP, None),
        P(DP, None),
        P(DP),
        P(DP),
        P(),
        P(),
        P(),
        P(),
        P(None, None, "mp"),
        P(None, "mp"),
        P(),
        P(),
        P(),
        P(DP, None, "mp"),
        P(DP, "mp"),
        P(DP, None, "mp"),
        P(DP, None, "mp"),
        P(DP, "mp"),
        P(DP, "mp"),
    )
    out_specs = (
        P(DP, None, "mp"),
        P(DP, None, "mp"),
        P(DP, None, "mp"),
        P(DP, "mp"),
        P(DP, "mp"),
        P(DP, "mp"),
        P(),
    )
    return jax.shard_map(
        per_device, mesh=torus, in_specs=in_specs, out_specs=out_specs, check_vma=False
    )
```

profile of v0, /device:TPU:1, one launch (start us, length us, event | category | flops | bytes accessed | tf_op | source)
XLA Modules:
  0.0 785.2 jit_solution(3109990404546934198)
XLA Ops:
  13.3 8.9 %copy.110 = bf16[2048,3,512]{0,2,1:T(8,128)(2,1)} copy(bf16[2048,3,512]{2,0,1:T(8,128)(2,1)} %param.27) | data formatting | bytes 12582912 | tf_op args[8]
  22.2 3.7 fusion.66
  42.9 6.1 all-to-all-start.1
  57.3 38.5 %all-to-all-done.1 = f32[2,128,2048]{2,1,0:T(8,128)} async-done(((f32[2,128,2048]{2,1,0:T(8,128)}), f32[2,128,2048]{2,1,0:T(8,128)}, u32[]{:S(2)}, u32[]{:S(2)}) %all-to-all-start.1) | async-done | bytes 2097184 | tf_op jit(solution)/shard_map/all_to_all | solution.py:35
  118.0 4.7 convolution_convert_fusion
  129.1 5.1 all-to-all-start.3
  135.4 23.7 %all-to-all-done.3 = f32[2,128,2048]{2,1,0:T(8,128)} async-done(((f32[2,128,2048]{2,1,0:T(8,128)}), f32[2,128,2048]{2,1,0:T(8,128)}, u32[]{:S(2)}, u32[]{:S(2)}) %all-to-all-start.3) | async-done | bytes 2097184 | tf_op jit(solution)/shard_map/all_to_all | solution.py:35
  162.0 5.6 fusion.6
  173.2 3.7 fusion.13
  176.9 4.8 all-to-all-start
  185.5 20.4 %all-to-all-done = f32[2,128,2048]{2,1,0:T(8,128)} async-done(((f32[2,128,2048]{2,1,0:T(8,128)}), f32[2,128,2048]{2,1,0:T(8,128)}, u32[]{:S(2)}, u32[]{:S(2)}) %all-to-all-start) | async-done | bytes 2097184 | tf_op jit(solution)/shard_map/all_to_all | solution.py:35
  210.6 4.7 fusion.104
  221.4 15.2 %all_to_all.25 = bf16[2,128,2048]{1,2,0:T(8,128)(2,1)} all-to-all(bf16[2,128,2048]{1,2,0:T(8,128)(2,1)S(1)} %broadcast_in_dim.5), channel_id=1, replica_groups=mesh['dp_0'=4,'dp_1'=4,'dp_2'=2,'dp_3'=2,'mp'=2] {'mp'}, dimensions={0} | all-to-all | bytes 2097152 | tf_op jit(solution)/shard_map/all_to_all | solution.py:57
  244.0 14.5 %reduce-scatter.6.cloned.1.call-done = f32[32,32,512]{2,1,0:T(8,128)} async-done(((f32[64,32,512]{2,1,0:T(8,128)}), f32[32,32,512]{2,1,0:T(8,128)}) %reduce-scatter.6.cloned.1.call-update) | async-done | bytes 2097168 | tf_op jit(solution)/shard_map/reduce_scatter | solution.py:75
  264.2 4.5 fusion.42
  268.6 5.2 fusion.39
  276.0 6.5 fusion.145
  282.6 120.6 %reduce-scatter.8.cloned.1.call-done = f32[1,32,512]{2,1,0:T(8,128)} async-done(((f32[32,32,512]{2,1,0:T(8,128)}), f32[1,32,512]{2,1,0:T(8,128)}) %reduce-scatter.8.cloned.1.call-update) | async-done | bytes 65552 | tf_op jit(solution)/shard_map/reduce_scatter | solution.py:76
  404.8 324.9 %reduce-scatter.4.cloned.1.call-done = f32[32,1536]{1,0:T(8,128)} async-done(((f32[2048,1536]{1,0:T(8,128)}), f32[32,1536]{1,0:T(8,128)}) %reduce-scatter.4.cloned.1.call-update) | async-done | bytes 196624 | tf_op jit(solution)/shard_map/reduce_scatter | solution.py:266
  732.7 6.6 all-reduce.1
  739.3 7.3 all-reduce
  746.6 9.4 %all-reduce.4 = (f32[]{:T(128)}, f32[]{:T(128)}) all-reduce(f32[]{:T(128)} %get-tuple-element.30, f32[]{:T(128)} %get-tuple-element.31), channel_id=1, replica_groups=mesh['dp_0'=4,'dp_1'=4,'dp_2'=2,'dp_3'=2,'mp'=2] {'dp_2'}, use_global_device_ids=true, to_apply=%region_31.0 | all-reduce | flops 2 | bytes 16 | tf_op jit(solution)/shard_map/psum | solution.py:66
  756.0 8.3 %all-reduce.3 = (f32[]{:T(128)}, f32[]{:T(128)}) all-reduce(f32[]{:T(128)} %get-tuple-element.38, f32[]{:T(128)} %get-tuple-element.39), channel_id=1, replica_groups=mesh['dp_0'=4,'dp_1'=4,'dp_2'=2,'dp_3'=2,'mp'=2] {'dp_3'}, use_global_device_ids=true, to_apply=%region_32.0 | all-reduce | flops 2 | bytes 16 | tf_op jit(solution)/shard_map/psum | solution.py:66
  764.3 6.0 all-reduce.2
  (177 shorter events, 101.8 us)
Async XLA Ops:
  7.2 33.6 %copy-start = (bf16[2048,512]{1,0:T(8,128)(2,1)S(1)}, bf16[2048,512]{1,0:T(8,128)(2,1)}, u32[]{:S(2)}) copy-start(bf16[2048,512]{1,0:T(8,128)(2,1)} %param.28) | copy-start | bytes 6291460
  7.2 154.8 %all-gather.2.cloned.1.call-start = ((), (), s32[]{:S(2)}) async-start(), calls=%async_computation.8 | async-start | bytes 8519680 | tf_op jit(solution)/shard_map/all_gather | solution.py:44
  25.9 4.0 copy-start.7
  42.9 6.3 copy-start.21
  42.9 52.9 %all-to-all-start.1 = ((f32[2,128,2048]{2,1,0:T(8,128)}), f32[2,128,2048]{2,1,0:T(8,128)}, u32[]{:S(2)}, u32[]{:S(2)}) async-start(f32[2,128,2048]{2,1,0:T(8,128)} %fusion.11), calls=%async_computation.1 | async-start | bytes 4194304 | tf_op jit(solution)/shard_map/all_to_all | solution.py:35
  52.4 109.6 %copy-start.29 = (f32[256]{0:T(256)}, f32[256]{0:T(256)S(1)}, u32[]{:S(2)}) copy-start(f32[256]{0:T(256)S(1)} %broadcast_multiply_fusion.3) | copy-start | bytes 3076
  54.1 107.9 %copy-start.31 = (f32[256]{0:T(256)}, f32[256]{0:T(256)S(1)}, u32[]{:S(2)}) copy-start(f32[256]{0:T(256)S(1)} %add_rsqrt_fusion.2) | copy-start | bytes 3076
  55.3 45.4 %copy-start.22 = (f32[128,16]{0,1:T(8,128)}, f32[128,16]{0,1:T(8,128)S(1)}, u32[]{:S(2)}) copy-start(f32[128,16]{0,1:T(8,128)S(1)} %copy.148) | copy-start | bytes 24580
  98.6 9.6 %copy-start.33 = (f32[8]{0:T(128)S(1)}, f32[8]{0:T(128)}, u32[]{:S(2)}) copy-start(f32[8]{0:T(128)} %param.23) | copy-start | bytes 100
  98.6 14.7 %copy-start.14 = (f32[16,2048]{1,0:T(8,128)S(1)}, f32[16,2048]{1,0:T(8,128)}, u32[]{:S(2)}) copy-start(f32[16,2048]{1,0:T(8,128)} %param.24) | copy-start | bytes 393220
  104.9 8.4 %all-to-all-start.2 = ((f32[2,128,16]{1,2,0:T(8,128)}), f32[2,128,16]{1,2,0:T(8,128)S(1)}, u32[]{:S(2)}, u32[]{:S(2)}) async-start(f32[2,128,16]{1,2,0:T(8,128)} %broadcast_in_dim.4), calls=%async_computation.2 | async-start | bytes 32768 | tf_op jit(solution)/shard_map/all_to_all | solution.py:57
  129.1 30.1 %all-to-all-start.3 = ((f32[2,128,2048]{2,1,0:T(8,128)}), f32[2,128,2048]{2,1,0:T(8,128)}, u32[]{:S(2)}, u32[]{:S(2)}) async-start(f32[2,128,2048]{2,1,0:T(8,128)} %fusion.9), calls=%async_computation.3 | async-start | bytes 4194304 | tf_op jit(solution)/shard_map/all_to_all | solution.py:35
  134.2 27.8 %copy-start.3 = (f32[256,2048]{1,0:T(8,128)S(1)}, f32[256,2048]{1,0:T(8,128)}, u32[]{:S(2)}) copy-start(f32[256,2048]{1,0:T(8,128)} %copy-done.2) | copy-start | bytes 6291460
  169.0 4.1 copy-start.10
  176.9 29.0 %all-to-all-start = ((f32[2,128,2048]{2,1,0:T(8,128)}), f32[2,128,2048]{2,1,0:T(8,128)}, u32[]{:S(2)}, u32[]{:S(2)}) async-start(f32[2,128,2048]{2,1,0:T(8,128)} %fusion.13), calls=%async_computation | async-start | bytes 4194304 | tf_op jit(solution)/shard_map/all_to_all | solution.py:35
  181.7 76.8 %reduce-scatter.6.cloned.1.call-start = ((), (), s32[]{:S(2)}) async-start(), calls=%async_computation.10 | async-start | bytes 6291456 | tf_op jit(solution)/shard_map/reduce_scatter | solution.py:75
  185.5 23.3 %copy-start.24 = (f32[1,1,2048]{2,0,1:T(1,128)S(1)}, f32[1,1,2048]{2,0,1:T(1,128)}, u32[]{:S(2)}) copy-start(f32[1,1,2048]{2,0,1:T(1,128)} %get-tuple-element.56) | copy-start | bytes 24580
  244.0 159.3 %reduce-scatter.8.cloned.1.call-start = ((), (), s32[]{:S(2)}) async-start(), calls=%async_computation.11 | async-start | bytes 2162688 | tf_op jit(solution)/shard_map/reduce_scatter | solution.py:76
  258.5 471.1 %reduce-scatter.4.cloned.1.call-start = ((), (), s32[]{:S(2)}) async-start(), calls=%async_computation.9 | async-start | bytes 12779520 | tf_op jit(solution)/shard_map/reduce_scatter | solution.py:266
  282.6 489.5 %copy-start.20 = (f32[32,3,512]{2,0,1:T(8,128)S(1)}, f32[32,3,512]{2,0,1:T(8,128)}, u32[]{:S(2)}) copy-start(f32[32,3,512]{2,0,1:T(8,128)} %param.35) | copy-start | bytes 589828
  282.6 493.8 %copy-start.25 = (f32[32,512]{1,0:T(8,128)S(1)}, f32[32,512]{1,0:T(8,128)}, u32[]{:S(2)}) copy-start(f32[32,512]{1,0:T(8,128)} %param.37) | copy-start | bytes 196612
  282.6 493.8 %copy-start.26 = (f32[32,512]{1,0:T(8,128)S(1)}, f32[32,512]{1,0:T(8,128)}, u32[]{:S(2)}) copy-start(f32[32,512]{1,0:T(8,128)} %param.36) | copy-start | bytes 196612
  403.3 373.2 %copy-start.17 = (f32[1,32,512]{2,1,0:T(8,128)S(1)}, f32[1,32,512]{2,1,0:T(8,128)}, u32[]{:S(2)}) copy-start(f32[1,32,512]{2,1,0:T(8,128)} %reduce-scatter.8.cloned.1.call-done) | copy-start | bytes 196612
  729.7 47.5 %copy-start.1 = (bf16[2048,512]{1,0:T(8,128)(2,1)S(1)}, bf16[2048,512]{1,0:T(8,128)(2,1)}, u32[]{:S(2)}) copy-start(bf16[2048,512]{1,0:T(8,128)(2,1)} %param.28) | copy-start | bytes 6291460
  (20 other events, 41.6 us)
Sparse Core Ops, SparseCore 0:
  10.3 115.7 all-gather.1
  244.1 14.3 reduce-scatter.5
  260.9 142.3 reduce-scatter.7
  405.5 324.0 reduce-scatter.3
where the time goes:
time: 795 us; the launch traced here: 785 us
  waiting for transfers between devices  543 us (68%)
  matrix products  79 us (10%)
  blocking collectives  52.8 us (7%)
  local copies, waits for them, and re-layouts  35.3 us (4%)
  other arithmetic  31.2 us (4%)
  between operations  24.5 us (3%)
  starting transfers between devices  19.7 us (2%)
    reduce_scatter x1, waiting for transfers between devices, per_device(): lax.psum_scatter(lax.dot_general(piece, d_pack, (((0,), (0,)), ((), ())),...  325 us
    reduce_scatter x1, waiting for transfers between devices, summed_rows_2(): return lax.psum_scatter(parts, chips, scatter_dimension=0, tiled=True)[0]  121 us
    all_to_all x3, waiting for transfers between devices, summed_on_arrival(): lax.all_to_all(in_blocks(shard, dim, devices), axis, 0, 0, tiled=True)  82.6 us
    psum x5, blocking collectives, by_axis(): shard = lax.psum(shard, axis)  37.6 us
    all_to_all x3, starting transfers between devices, summed_on_arrival(): lax.all_to_all(in_blocks(shard, dim, devices), axis, 0, 0, tiled=True)  16 us
  transfers between devices with their start and end apart: 8, of which 6 were waited for; matrix products, arithmetic and copies ran while one was open for 12% of the time, Pallas kernels for 0%

commit v1 on v0

--- a/solution.py
+++ b/solution.py
@@ -3,6 +3,8 @@
 import jax
 import jax.numpy as jnp
 from jax import lax
+from jax.experimental import pallas as pl
+from jax.experimental.pallas import tpu as pltpu
 from jax.sharding import Mesh
 from jax.sharding import PartitionSpec as P
 
@@ -25,55 +27,225 @@
 ADAM_EPS = 1e-08
 
 
-def in_blocks(shard, dim, devices):
-    before, after = (shard.shape[:dim], shard.shape[dim + 1 :])
-    return jnp.moveaxis(shard.reshape(*before, devices, -1, *after), dim, 0)
-
-
-def summed_on_arrival(shard, axis, dim):
-    devices = lax.axis_size(axis)
-    parts = lax.all_to_all(in_blocks(shard, dim, devices), axis, 0, 0, tiled=True)
-    return jnp.sum(parts, axis=0)
-
-
-def side_by_side(arrays, axis, dim, along):
-    widths = [math.prod(a.shape[along:]) for a in arrays]
-    both = jnp.concatenate(
-        [a.reshape(*a.shape[:along], w) for a, w in zip(arrays, widths)], axis=along
-    )
-    whole = lax.all_gather(both, axis, axis=dim, tiled=True)
-    parts = jnp.split(whole, [sum(widths[:k]) for k in range(1, len(widths))], axis=along)
-    return tuple((b.reshape(*whole.shape[:along], *a.shape[along:]) for a, b in zip(arrays, parts)))
-
-
-def in_order(parts, dim):
-    parts = jnp.moveaxis(parts, 0, dim)
-    dims = parts.shape
-    return parts.reshape(*dims[:dim], dims[dim] * dims[dim + 1], *dims[dim + 2 :])
-
-
-def sent_to_all(shard, axis):
-    copies = jnp.broadcast_to(shard, (lax.axis_size(axis), *shard.shape))
-    return lax.all_to_all(copies, axis, split_axis=0, concat_axis=0, tiled=True)
-
-
-def gathered_copies(shard, axis, dim):
-    return in_order(sent_to_all(shard, axis), dim)
-
-
-def by_axis(shard, axes):
-    for axis in axes:
-        shard = lax.psum(shard, axis)
-    return shard
-
-
-def summed_rows_2(shard, chips, core, dim):
-    sizes = (lax.axis_size(chips), lax.axis_size(core))
-    parts = in_blocks(shard, dim, sizes[0] * sizes[1])
-    inside = parts.shape[1:]
-    parts = parts.reshape(*sizes, *inside).swapaxes(0, 1).reshape(-1, *inside)
-    parts = lax.psum_scatter(parts, core, scatter_dimension=0, tiled=True)
-    return lax.psum_scatter(parts, chips, scatter_dimension=0, tiled=True)[0]
+ROWS = 1024
+HALF = 1024
+AXES = ("dp_0", "dp_1", "dp_2", "dp_3", "mp")
+
+
+def remote(src, dst, send, recv, axis, target):
+    return pltpu.make_async_remote_copy(
+        src_ref=src,
+        dst_ref=dst,
+        send_sem=send,
+        recv_sem=recv,
+        device_id={axis: target},
+        device_id_type=pl.DeviceIdType.MESH,
+    )
+
+
+def ring_start(axis, part, relay, direct, send, recv):
+    me = lax.axis_index(axis)
+    right, left, far = (lax.rem(me + k, 4) for k in (1, 3, 2))
+    half = part.shape[1] // 2
+    top, low = pl.ds(0, half), pl.ds(half, half)
+    copies = [
+        remote(part.at[far, top], relay.at[0], send.at[0], recv.at[0], axis, right),
+        remote(part.at[far, low], relay.at[1], send.at[1], recv.at[1], axis, left),
+        remote(part.at[right, low], direct.at[0], send.at[2], recv.at[2], axis, right),
+        remote(part.at[left, top], direct.at[1], send.at[3], recv.at[3], axis, left),
+    ]
+    for c in copies:
+        c.start()
+    return copies
+
+
+def ring_relay(axis, copies, part, relay, passed, summed, send, recv):
+    me = lax.axis_index(axis)
+    right, left = (lax.rem(me + k, 4) for k in (1, 3))
+    half = part.shape[1] // 2
+    top, low = pl.ds(0, half), pl.ds(half, half)
+    copies[0].wait_recv()
+    passed[0] = relay[0] + part[right, top]
+    first = remote(passed.at[0], summed.at[0], send.at[4], recv.at[4], axis, right)
+    first.start()
+    copies[1].wait_recv()
+    passed[1] = relay[1] + part[left, low]
+    second = remote(passed.at[1], summed.at[1], send.at[5], recv.at[5], axis, left)
+    second.start()
+    return [first, second]
+
+
+def ring_finish(axis, copies, more, part, direct, summed):
+    me = lax.axis_index(axis)
+    half = part.shape[1] // 2
+    copies[3].wait_recv()
+    more[0].wait_recv()
+    upper = part[me, pl.ds(0, half)] + direct[1] + summed[0]
+    copies[2].wait_recv()
+    more[1].wait_recv()
+    lower = part[me, pl.ds(half, half)] + direct[0] + summed[1]
+    for c in [*copies, *more]:
+        c.wait_send()
+    return upper, lower
+
+
+def reduce_kernel(
+    shaped_own,
+    shaped_other,
+    proj_own,
+    proj_other,
+    packed,
+    out,
+    shaped_in,
+    proj_in,
+    packed_in,
+    part_a,
+    part_b,
+    part_c,
+    part_d,
+    *rest,
+):
+    boxes_a, boxes_b, boxes_c, boxes_d = rest[0:4], rest[4:8], rest[8:12], rest[12:16]
+    last, last_in, pair_send, pair_recv, send, recv, z_send, z_recv = rest[16:]
+    y, x, z, core = (lax.axis_index(a) for a in AXES[:4])
+    barrier = pltpu.get_barrier_semaphore()
+    friends = [("dp_3", 1 - core), ("dp_2", 1 - z)]
+    friends += [("dp_1", lax.rem(x + k, 4)) for k in (1, 3)]
+    friends += [("dp_0", lax.rem(y + k, 4)) for k in (1, 3)]
+    for axis, target in friends:
+        pl.semaphore_signal(
+            barrier, inc=1, device_id={axis: target}, device_id_type=pl.DeviceIdType.MESH
+        )
+    pl.semaphore_wait(barrier, len(friends))
+
+    pair = [
+        remote(a, b, pair_send.at[k], pair_recv.at[k], "dp_3", 1 - core)
+        for k, (a, b) in enumerate(
+            [(packed, packed_in), (shaped_other, shaped_in), (proj_other, proj_in)]
+        )
+    ]
+    for c in pair:
+        c.start()
+
+    def products(s_ref, p_ref, b_ref, add):
+        def step(k, carry):
+            rows = pl.ds(pl.multiple_of(k * 256, 256), 256)
+            s, p = s_ref[rows], p_ref[rows]
+            g = jnp.dot(s, b_ref[:, :HALF], preferred_element_type=jnp.float32)
+            for j in range(4):
+                block = g[64 * j : 64 * j + 64]
+                spot = pl.ds(pl.multiple_of(k * 64, 64), 64)
+                part_a[j, spot] = part_a[j, spot] + block if add else block
+            h = jnp.dot(s, b_ref[:, HALF : HALF + 512], preferred_element_type=jnp.float32)
+            part_b[k, :, 0:512] = part_b[k, :, 0:512] + h if add else h
+            o = jnp.dot(p, b_ref[:, HALF + 512 :], preferred_element_type=jnp.float32)
+            part_b[k, :, 512:1024] = part_b[k, :, 512:1024] + o if add else o
+            return carry
+
+        lax.fori_loop(0, 4, step, 0)
+
+    products(shaped_own, proj_own, packed, False)
+    for c in pair:
+        c.wait_recv()
+    products(shaped_in, proj_in, packed_in, True)
+
+    first_a = ring_start("dp_1", part_a, boxes_a[0], boxes_a[1], send.at[0], recv.at[0])
+    first_b = ring_start("dp_0", part_b, boxes_b[0], boxes_b[1], send.at[1], recv.at[1])
+    more_a = ring_relay(
+        "dp_1", first_a, part_a, boxes_a[0], boxes_a[2], boxes_a[3], send.at[0], recv.at[0]
+    )
+    more_b = ring_relay(
+        "dp_0", first_b, part_b, boxes_b[0], boxes_b[2], boxes_b[3], send.at[1], recv.at[1]
+    )
+    upper, lower = ring_finish("dp_1", first_a, more_a, part_a, boxes_a[1], boxes_a[3])
+    for k in range(2):
+        part_c[k] = upper[64 * k : 64 * k + 64]
+        part_c[2 + k] = lower[64 * k : 64 * k + 64]
+    first_c = ring_start("dp_0", part_c, boxes_c[0], boxes_c[1], send.at[2], recv.at[2])
+    upper, lower = ring_finish("dp_0", first_b, more_b, part_b, boxes_b[1], boxes_b[3])
+    for k in range(2):
+        part_d[k] = upper[64 * k : 64 * k + 64]
+        part_d[2 + k] = lower[64 * k : 64 * k + 64]
+    first_d = ring_start("dp_1", part_d, boxes_d[0], boxes_d[1], send.at[3], recv.at[3])
+    more_c = ring_relay(
+        "dp_0", first_c, part_c, boxes_c[0], boxes_c[2], boxes_c[3], send.at[2], recv.at[2]
+    )
+    more_d = ring_relay(
+        "dp_1", first_d, part_d, boxes_d[0], boxes_d[2], boxes_d[3], send.at[3], recv.at[3]
+    )
+    z_copies = []
+    for k, (axis, first, more, part, boxes) in enumerate(
+        [
+            ("dp_0", first_c, more_c, part_c, boxes_c),
+            ("dp_1", first_d, more_d, part_d, boxes_d),
+        ]
+    ):
+        upper, lower = ring_finish(axis, first, more, part, boxes[1], boxes[3])
+        last[k, 0] = upper
+        last[k, 1] = lower
+        c = remote(
+            last.at[k, 1 - z], last_in.at[k], z_send.at[k], z_recv.at[k], "dp_2", 1 - z
+        )
+        c.start()
+        z_copies.append(c)
+    for k, c in enumerate(z_copies):
+        c.wait_recv()
+        out[:, k * HALF : (k + 1) * HALF] = last[k, z] + last_in[k]
+    for c in [*pair, *z_copies]:
+        c.wait_send()
+
+
+def reduce_gradients(shaped, d_proj, packed):
+    core = lax.axis_index("dp_3")
+
+    def split(values):
+        rows = values.T.reshape(ROWS // 32, 2, 32, SEQ)
+        own = lax.dynamic_index_in_dim(rows, core, 1, keepdims=False)
+        other = lax.dynamic_index_in_dim(rows, 1 - core, 1, keepdims=False)
+        return own.reshape(ROWS, SEQ), other.reshape(ROWS, SEQ)
+
+    shaped_own, shaped_other = split(shaped)
+    proj_own, proj_other = split(d_proj)
+    vmem = pl.BlockSpec(memory_space=pltpu.VMEM)
+    wire = jnp.float32
+
+    def boxes(half):
+        return [pltpu.VMEM((2, half, HALF), wire)] * 4
+
+    return pl.pallas_call(
+        reduce_kernel,
+        out_shape=jax.ShapeDtypeStruct((32, 2 * HALF), jnp.float32),
+        in_specs=[vmem] * 5,
+        out_specs=vmem,
+        scratch_shapes=[
+            pltpu.VMEM((ROWS, SEQ), jnp.bfloat16),
+            pltpu.VMEM((ROWS, SEQ), jnp.bfloat16),
+            pltpu.VMEM((SEQ, 2 * HALF), jnp.bfloat16),
+            pltpu.VMEM((4, 256, HALF), jnp.float32),
+            pltpu.VMEM((4, 256, HALF), jnp.float32),
+            pltpu.VMEM((4, 64, HALF), jnp.float32),
+            pltpu.VMEM((4, 64, HALF), jnp.float32),
+            *boxes(128),
+            *boxes(128),
+            *boxes(32),
+            *boxes(32),
+            pltpu.VMEM((2, 2, 32, HALF), jnp.float32),
+            pltpu.VMEM((2, 32, HALF), jnp.float32),
+            pltpu.SemaphoreType.DMA((3,)),
+            pltpu.SemaphoreType.DMA((3,)),
+            pltpu.SemaphoreType.DMA((4, 6)),
+            pltpu.SemaphoreType.DMA((4, 6)),
+            pltpu.SemaphoreType.DMA((2,)),
+            pltpu.SemaphoreType.DMA((2,)),
+        ],
+        compiler_params=pltpu.CompilerParams(
+            collective_id=1, has_side_effects=True, vmem_limit_bytes=60 * 2**20
+        ),
+    )(shaped_own, shaped_other, proj_own, proj_other, packed)
+
+
+def swapped(values):
+    return lax.ppermute(values, "mp", [(0, 1), (1, 0)])
 
 
 def plan():
@@ -131,12 +303,6 @@
     rows_all = samples * SEQ
     local_inner = teacher_out.shape[1]
     local_heads = local_inner // HS
-    count = rows_all // lax.axis_size("mp")
-    start = lax.axis_index("mp") * count
-
-    def take(values):
-        return lax.dynamic_slice_in_dim(values, start, count, 0)
-
     alphas, sigmas = plan()
     table = jnp.stack([alphas, sigmas], axis=1)
 
@@ -154,11 +320,11 @@
         return picked.reshape(samples, 3, D)
 
     def gate_rows(modrows):
-        return take(jnp.repeat(modrows[:, 2], SEQ, axis=0))
+        return jnp.repeat(modrows[:, 2], SEQ, axis=0)
 
     placed = positions()
 
-    def front(latent, modrows, embed, w_qkv, w_out):
+    def front(latent, modrows, embed, w_qkv, w_out, other_out):
         hidden = (
             jnp.dot(latent, embed, precision=lax.Precision.HIGHEST).reshape(samples, SEQ, D)
             + placed[None]
@@ -188,16 +354,16 @@
             "shqk,skhd->sqhd", rounded, values, preferred_element_type=jnp.float32
         )
         attended = attended.astype(jnp.bfloat16).reshape(rows_all, local_inner)
+        contract = (((1,), (1,)), ((), ()))
         projected = lax.dot_general(
-            attended, w_out, (((1,), (1,)), ((), ())), preferred_element_type=jnp.float32
+            attended, w_out, contract, preferred_element_type=jnp.float32
+        ) + lax.dot_general(
+            swapped(attended), other_out, contract, preferred_element_type=jnp.float32
         )
         return (hidden, shaped, queries, keys_all, values, weights, rounded, attended, projected)
 
-    def reduce_heads(projected):
-        return summed_on_arrival(projected, "mp", 0)
-
     def tail(hidden, modrows, projected, final):
-        mixed = take(hidden) + gate_rows(modrows) * reduce_heads(projected)
+        mixed = hidden + gate_rows(modrows) * projected
         normed, inverse = normalize(mixed)
         predicted = lax.dot_general(
             normed, final, (((1,), (1,)), ((), ())), precision=lax.Precision.HIGHEST
@@ -205,10 +371,17 @@
         return (predicted, normed, inverse)
 
     def teacher_eps(latent, modrows):
-        parts = front(latent, modrows, teacher_embed, teacher_qkv, teacher_out)
+        parts = front(latent, modrows, teacher_embed, teacher_qkv, teacher_out, teacher_other)
         return tail(parts[0], modrows, parts[8], teacher_final)[0]
 
-    whole_qkv, whole_out = side_by_side((student_qkv, student_out), DP, 0, 1)
+    teacher_other = swapped(teacher_out)
+    flat = jnp.concatenate(
+        [student_qkv.reshape(-1, 3 * local_inner), student_out, swapped(student_out)], axis=1
+    )
+    whole = lax.all_gather(flat, DP, axis=0, tiled=True)
+    whole_qkv = whole[:, : 3 * local_inner]
+    whole_out = whole[:, 3 * local_inner : 4 * local_inner]
+    whole_other = whole[:, 4 * local_inner :]
     first = 2 * timestep
     middle = first - 1
     last = first - 2
@@ -218,33 +391,26 @@
     clean_rows = clean_latent.reshape(rows_all, PATCH_CH)
     noise_rows = noise_draw.reshape(rows_all, PATCH_CH)
     latent0 = a_first * clean_rows + s_first * noise_rows
-    mine0 = take(latent0)
-    af_mine, sf_mine = (take(a_first), take(s_first))
-    am_mine, sm_mine = (take(a_middle), take(s_middle))
-    al_mine, sl_mine = (take(a_last), take(s_last))
     eps_zero = teacher_eps(latent0, modulation(teacher_mod, first - 1, TGRID))
-    next_mine = am_mine * (mine0 - sf_mine * eps_zero) / af_mine + sm_mine * eps_zero
-    latent1 = gathered_copies(next_mine, "mp", 0)
+    latent1 = a_middle * (latent0 - s_first * eps_zero) / a_first + s_middle * eps_zero
     eps_one = teacher_eps(latent1, modulation(teacher_mod, middle - 1, TGRID))
-    latent2 = al_mine * (take(latent1) - sm_mine * eps_one) / am_mine + sl_mine * eps_one
-    target = (mine0 - af_mine / al_mine * latent2) / (sf_mine - af_mine * sl_mine / al_mine)
+    latent2 = a_last * (latent1 - s_middle * eps_one) / a_middle + s_last * eps_one
+    target = (latent0 - a_first / a_last * latent2) / (s_first - a_first * s_last / a_last)
     student_rows_mod = modulation(student_mod, timestep - 1, K)
     hidden, shaped, queries, keys_all, values, weights, rounded, attended, projected = front(
-        latent0, student_rows_mod, student_embed, whole_qkv, whole_out
+        latent0, student_rows_mod, student_embed, whole_qkv, whole_out, whole_other
     )
     predicted, normed, inverse = tail(hidden, student_rows_mod, projected, student_final)
     sample_weight = jnp.dot(
         one_hot_rows(bucket, NBUCKET), bucket_weights, precision=lax.Precision.HIGHEST
     )
-    row_weight = take(jnp.repeat(sample_weight, SEQ, axis=0)[:, None])
+    row_weight = jnp.repeat(sample_weight, SEQ, axis=0)[:, None]
     error = predicted - target
     loss_part = jnp.sum(row_weight * error * error)
     d_pred = 2.0 * row_weight * error
     d_normed = jnp.dot(d_pred, student_final, precision=lax.Precision.HIGHEST)
     d_mixed = norm_back(d_normed, normed, inverse)
-    d_proj_mine = (gate_rows(student_rows_mod) * d_mixed).astype(jnp.bfloat16)
-    d_proj = gathered_copies(d_proj_mine, "mp", 0)
-    loss_sum = by_axis(loss_part, DP_MP)
+    d_proj = (gate_rows(student_rows_mod) * d_mixed).astype(jnp.bfloat16)
     d_attn = jnp.dot(d_proj, whole_out, preferred_element_type=jnp.float32).astype(jnp.bfloat16)
     d_attn = d_attn.reshape(samples, SEQ, local_heads, HS)
     d_prob = jnp.einsum("sqhd,skhd->shqk", d_attn, values, preferred_element_type=jnp.float32)
@@ -260,28 +426,15 @@
     d_value = jnp.einsum(
         "shqk,sqhd->skhd", rounded, d_attn, preferred_element_type=jnp.float32
     ).astype(jnp.bfloat16)
-    d_pack = jnp.stack([d_query, d_key, d_value], axis=2).reshape(rows_all, 3 * local_inner)
-    own_rows = D // lax.axis_size(DP)
-    piece = shaped
-    grad_qkv = lax.psum_scatter(
-        lax.dot_general(
-            piece, d_pack, (((0,), (0,)), ((), ())), preferred_element_type=jnp.float32
-        ),
-        DP,
-        scatter_dimension=0,
-        tiled=True,
-    ).reshape(own_rows, 3, local_inner)
-    piece = d_proj
-    grad_out = summed_rows_2(
-        lax.dot_general(
-            piece, attended, (((0,), (0,)), ((), ())), preferred_element_type=jnp.float32
-        ),
-        ("dp_0", "dp_1", "dp_2"),
-        "dp_3",
-        0,
-    )
-    squares = jnp.sum(grad_qkv * grad_qkv) + jnp.sum(grad_out * grad_out)
-    squares = by_axis(squares, DP_MP)
+    packed = jnp.concatenate(
+        [v.reshape(rows_all, local_inner) for v in (d_query, d_key, d_value, attended)], axis=1
+    )
+    grads = reduce_gradients(shaped, d_proj, packed)
+    grad_qkv = grads[:, : 3 * local_inner].reshape(-1, 3, local_inner)
+    grad_out = grads[:, 3 * local_inner :]
+    squares, loss_sum = lax.psum(
+        jnp.stack([jnp.sum(grads * grads), loss_part / lax.axis_size("mp")]), DP_MP
+    )
     rms_value = jnp.sqrt(squares / (4 * D * INNER))
     factor = 1.0 / jnp.maximum(rms_value, 1.0)
 

time: 795 us -> 382 us (0.48)
  waiting for transfers between devices: 543 us -> 82.3 us
  Pallas kernels: 0 us -> 66.6 us
  other arithmetic: 31.2 us -> 19.5 us
  blocking collectives: 52.8 us -> 63 us
    reduce_scatter x3 -> x0, waiting for transfers between devices: 460 us -> none  [the longest x1 325 us: per_device(): lax.psum_scatter(lax.dot_general(piece, d_pack, (((0,), (0,)), ((), ())),...]
    all_to_all x4 -> x0, waiting for transfers between devices: 82.6 us -> none  [the longest x3 82.6 us: summed_on_arrival(): lax.all_to_all(in_blocks(shard, dim, devices), axis, 0, 0, tiled=True)]
    ppermute x0 -> x5, waiting for transfers between devices: none -> 82.2 us  [swapped(): return lax.ppermute(values, 'mp', [(0, 1), (1, 0)])]
    pallas_call x0 -> x1, Pallas kernels: none -> 66.6 us  [reduce_gradients(): pl.pallas_call(reduce_kernel, out_shape=jax.ShapeDtypeStruct((32, 2 * HAL...]
    psum x5 -> x1, blocking collectives: 37.6 us -> 63 us  [per_device(): lax.psum(jnp.stack([jnp.sum(grads * grads), loss_part / lax.axis_size('mp...]
    ppermute x0 -> x5, starting transfers between devices: none -> 19.9 us  [swapped(): return lax.ppermute(values, 'mp', [(0, 1), (1, 0)])]
    all_to_all x4 -> x0, starting transfers between devices: 19.3 us -> none  [the longest x3 16 us: summed_on_arrival(): lax.all_to_all(in_blocks(shard, dim, devices), axis, 0, 0, tiled=True)]
    all_to_all x1 -> x0, blocking collectives: 15.2 us -> none  [sent_to_all(): return lax.all_to_all(copies, axis, split_axis=0, concat_axis=0, tiled=True)]
  transfers between devices with their start and end apart: 8 -> 6, of which waited for: 6 -> 4; matrix products, arithmetic and copies ran while one was open for 12% -> 17% of each run, Pallas kernels for 0% -> 0%
where the time goes in v1:
time: 382 us; the launch traced here: 378 us
  waiting for transfers between devices  82.3 us (22%)
  matrix products  71.1 us (19%)
  Pallas kernels  66.6 us (17%)
  blocking collectives  63 us (16%)
  local copies, waits for them, and re-layouts  31.9 us (8%)
  between operations  24.1 us (6%)
  starting transfers between devices  19.9 us (5%)
  other arithmetic  19.5 us (5%)
    ppermute x5, waiting for transfers between devices, swapped(): return lax.ppermute(values, 'mp', [(0, 1), (1, 0)])  82.2 us
    pallas_call x1, Pallas kernels, reduce_gradients(): pl.pallas_call(reduce_kernel, out_shape=jax.ShapeDtypeStruct((32, 2 * HAL...  66.6 us
    psum x1, blocking collectives, per_device(): lax.psum(jnp.stack([jnp.sum(grads * grads), loss_part / lax.axis_size('mp...  63 us
    ppermute x5, starting transfers between devices, swapped(): return lax.ppermute(values, 'mp', [(0, 1), (1, 0)])  19.9 us
    unnamed x84, local copies, waits for them, and re-layouts  16.2 us
    dot_general x3, matrix products, tail(): lax.dot_general(normed, final, (((1,), (1,)), ((), ())), precision=lax.Pr...  12.1 us
    dot_general x3, matrix products, front(): jnp.dot(shaped, w_qkv.reshape(D, 3 * local_inner), preferred_element_type...  9.35 us
    dot_general x3, matrix products, front(): lax.dot_general(swapped(attended), other_out, contract, preferred_element...  7.69 us
  transfers between devices with their start and end apart: 6, of which 4 were waited for; matrix products, arithmetic and copies ran while one was open for 17% of the time, Pallas kernels for 0%

profile of v1, /device:TPU:1, one launch (start us, length us, event | category | flops | bytes accessed | tf_op | source)
XLA Modules:
  0.0 378.4 jit_solution(16860713660458355321)
XLA Ops:
  7.2 4.5 %collective-permute-start = (bf16[32,512]{1,0:T(8,128)(2,1)}, bf16[32,512]{1,0:T(8,128)(2,1)S(1)}, u32[]{:S(2)}, u32[]{:S(2)}) collective-permute-start(bf16[32,512]{1,0:T(8,128)(2,1)} %param.33), channel_id=1, source_target_pairs={{0,1},{1,0},{2,3},{3,2},{4,5},{5,4},{6,7},{7,6},{8,9},{9,8},{10,11... | collective-permute-start | bytes 98312 | tf_op jit(solution)/shard_map/ppermute | solution.py:248
  18.4 8.9 %copy.86 = bf16[2048,3,512]{0,2,1:T(8,128)(2,1)} copy(bf16[2048,3,512]{2,0,1:T(8,128)(2,1)} %param.27) | data formatting | bytes 12582912 | tf_op args[8]
  27.3 3.7 fusion.69
  39.7 3.0 collective-permute-start.2
  48.5 3.3 fusion.148
  61.3 2.3 constant_dynamic-slice_fusion.2
  63.9 2.6 fusion.157
  66.5 73.7 %collective-permute-done.3 = bf16[2048,512]{1,0:T(8,128)(2,1)} collective-permute-done((bf16[2048,512]{1,0:T(8,128)(2,1)}, bf16[2048,512]{1,0:T(8,128)(2,1)}, u32[]{:S(2)}, u32[]{:S(2)}) %collective-permute-start.3) | collective-permute-done | bytes 2097184 | tf_op jit(solution)/shard_map/ppermute | solution.py:248
  140.2 2.8 fusion.153
  143.9 4.6 %multiply_add_fusion.1 = f32[256,16]{0,1:T(8,128)S(1)} fusion(f32[256,16]{0,1:T(8,128)S(1)} %copy.92, f32[16,2048]{1,0:T(8,128)S(1)} %copy-done.17, f32[256,2048]{1,0:T(8,128)S(1)} %get-tuple-element.58, f32[256]{0:T(256)S(1)} %add_rsqrt_fusion.2, f32[256]{0:T(256)S(1)} %broadcast_multiply_fusion.4, f32[]{:T(128)} %bitcast.55, f32[]{:T(128)} %bitcast.3, ...), kind=kOutput, calls=%fused_computation.138 | convolution fusion | flops 101736448 | bytes 2263056 | tf_op jit(solution)/shard_map/dot_general | solution.py:368
  158.0 11.4 %collective-permute-start.4 = (bf16[256,512]{0,1:T(8,128)(2,1)S(1)}, bf16[256,512]{0,1:T(8,128)(2,1)S(1)}, u32[]{:S(2)}, u32[]{:S(2)}) collective-permute-start(bf16[256,512]{0,1:T(8,128)(2,1)S(1)} %bitcast.303), channel_id=1, source_target_pairs={{0,1},{1,0},{2,3},{3,2},{4,5},{5,4},{6,7},{7,6},{8,9},{9,8},{10,11... | collective-permute-start | bytes 786440 | tf_op jit(solution)/shard_map/ppermute | solution.py:248
  169.4 2.3 fusion.158
  171.7 4.5 %collective-permute-done.4 = bf16[256,512]{0,1:T(8,128)(2,1)S(1)} collective-permute-done((bf16[256,512]{0,1:T(8,128)(2,1)S(1)}, bf16[256,512]{0,1:T(8,128)(2,1)S(1)}, u32[]{:S(2)}, u32[]{:S(2)}) %collective-permute-start.4) | collective-permute-done | bytes 262176 | tf_op jit(solution)/shard_map/ppermute | solution.py:248
  176.2 2.5 fusion.156
  180.6 5.5 %fusion.12 = bf16[256,1536]{1,0:T(8,128)(2,1)} fusion(bf16[2048,2560]{1,0:T(8,128)(2,1)} %all-gather.2.cloned.1.call-done, f32[256,2048]{1,0:T(8,128)S(1)} %get-tuple-element.50, f32[2048]{0:T(1024)S(1)} %bitcast.314, f32[2048]{0:T(1024)S(1)} %bitcast.312, f32[256]{0:T(256)S(1)} %copy-done.35, f32[256]{0:T(256)S(1)} %copy-done.33), kind=kOutput, calls=%fused_computation.18 | convolution fusion | flops 1613627392 | bytes 9193472 | tf_op jit(solution)/shard_map/dot_general | solution.py:339
  195.1 3.4 collective-permute-done.1
  198.5 2.3 fusion.15
  200.9 2.6 fusion.150
  204.3 5.7 %fusion.95 = (f32[]{:T(128)}, f32[256,16]{0,1:T(8,128)S(1)}) fusion(f32[]{:T(128)} %fusion.112, f32[]{:T(128)S(6)} %sub.173, f32[256,16]{0,1:T(8,128)S(1)} %copy.92, f32[256,16]{0,1:T(8,128)S(1)} %fusion.18, f32[]{:T(128)} %bitcast.71, f32[]{:T(128)} %bitcast.37, f32[256,16]{0,1:T(8,128)S(1)} %multiply_add_fusion.1, f32[]{:T(128)} %bitcast.55, ...), kind=kOutput, calls=%fused_computation.135 | convolution fusion | flops 101765120 | bytes 2295840 | tf_op jit(solution)/shard_map/dot_general | solution.py:368
  213.2 2.3 fusion.45
  217.1 3.8 fusion.39
  220.9 3.7 fusion.42
  230.2 66.6 %shard_map.234 = f32[32,2048]{1,0:T(8,128)} custom-call(bf16[1024,256]{1,0:T(8,128)(2,1)} %bitcast.285, bf16[1024,256]{1,0:T(8,128)(2,1)} %bitcast.284, bf16[1024,256]{1,0:T(8,128)(2,1)} %bitcast.287, bf16[1024,256]{1,0:T(8,128)(2,1)} %bitcast.286, bf16[256,2048]{1,0:T(8,128)(2,1)} %pad_maximum_fusion.1.packed), custom_call_target="tpu_custom_call" | custom-call | tf_op jit(solution)/shard_map/pallas_call | solution.py:215
  299.9 63.0 %psum.7 = f32[2]{0:T(128)S(1)} all-reduce(f32[2]{0:T(128)S(1)} %pad_maximum_fusion.4), channel_id=1, replica_groups=mesh['dp_0'=4,'dp_1'=4,'dp_2'=2,'dp_3'=2,'mp'=2] {'dp_0','dp_1','dp_2','..., use_global_device_ids=true, to_apply=%region_23.24 | all-reduce | flops 2 | bytes 16 | tf_op jit(solution)/shard_map/psum | solution.py:435
  (169 shorter events, 65.3 us)
Async XLA Ops:
  7.2 26.2 %copy-start = (f32[16,3,2048]{2,0,1:T(8,128)S(1)}, f32[16,3,2048]{2,0,1:T(8,128)}, u32[]{:S(2)}) copy-start(f32[16,3,2048]{2,0,1:T(8,128)} %param.26) | copy-start | bytes 1179652
  7.2 173.4 %all-gather.2.cloned.1.call-start = ((), (), s32[]{:S(2)}) async-start(), calls=%async_computation | async-start | bytes 10649600 | tf_op jit(solution)/shard_map/all_gather | solution.py:381
  7.2 6.0 %collective-permute-start = (bf16[32,512]{1,0:T(8,128)(2,1)}, bf16[32,512]{1,0:T(8,128)(2,1)S(1)}, u32[]{:S(2)}, u32[]{:S(2)}) collective-permute-start(bf16[32,512]{1,0:T(8,128)(2,1)} %param.33), channel_id=1, source_target_pairs={{0,1},{1,0},{2,3},{3,2},{4,5},{5,4},{6,7},{7,6},{8,9},{9,8},{10,11... | collective-permute-start | bytes 98312 | tf_op jit(solution)/shard_map/ppermute | solution.py:248
  15.4 27.7 %copy-start.36 = (f32[17,1]{0,1:T(1,128)}, f32[17,1]{0,1:T(1,128)S(1)}, u32[]{:S(2)}) copy-start(f32[17,1]{0,1:T(1,128)S(1)} %get-tuple-element.66) | copy-start | bytes 208
  15.4 27.7 %copy-start.37 = (f32[17,1]{0,1:T(1,128)}, f32[17,1]{0,1:T(1,128)S(1)}, u32[]{:S(2)}) copy-start(f32[17,1]{0,1:T(1,128)S(1)} %get-tuple-element.67) | copy-start | bytes 208
  18.4 24.6 %copy-start.11 = (f32[256,16]{1,0:T(8,128)}, f32[256,16]{1,0:T(8,128)S(1)}, u32[]{:S(2)}) copy-start(f32[256,16]{1,0:T(8,128)S(1)} %add.197) | copy-start | bytes 49156
  39.7 26.8 %collective-permute-start.2 = (bf16[256,512]{0,1:T(8,128)(2,1)}, bf16[256,512]{0,1:T(8,128)(2,1)}, u32[]{:S(2)}, u32[]{:S(2)}) collective-permute-start(bf16[256,512]{0,1:T(8,128)(2,1)} %bitcast.52), channel_id=1, source_target_pairs={{0,1},{1,0},{2,3},{3,2},{4,5},{5,4},{6,7},{7,6},{8,9},{9,8},{10,11... | collective-permute-start | bytes 786440 | tf_op jit(solution)/shard_map/ppermute | solution.py:248
  42.7 97.5 %collective-permute-start.3 = (bf16[2048,512]{1,0:T(8,128)(2,1)}, bf16[2048,512]{1,0:T(8,128)(2,1)}, u32[]{:S(2)}, u32[]{:S(2)}) collective-permute-start(bf16[2048,512]{1,0:T(8,128)(2,1)} %param.28), channel_id=1, source_target_pairs={{0,1},{1,0},{2,3},{3,2},{4,5},{5,4},{6,7},{7,6},{8,9},{9,8},{10,11... | collective-permute-start | bytes 6291464 | tf_op jit(solution)/shard_map/ppermute | solution.py:248
  63.9 76.3 %copy-start.3 = (f32[256,2048]{1,0:T(8,128)S(1)}, f32[256,2048]{1,0:T(8,128)}, u32[]{:S(2)}) copy-start(f32[256,2048]{1,0:T(8,128)} %copy-done.2) | copy-start | bytes 6291460
  63.9 76.3 %copy-start.31 = (f32[1,1,2048]{2,0,1:T(1,128)S(1)}, f32[1,1,2048]{2,0,1:T(1,128)}, u32[]{:S(2)}) copy-start(f32[1,1,2048]{2,0,1:T(1,128)} %get-tuple-element.35) | copy-start | bytes 24580
  140.2 11.7 %slice-start = ((s8[6291456]{0:T(1024)(128)(4,1)}), s8[4194304]{0:T(1024)(128)(4,1)S(1)}, s32[]{:S(2)}) async-start(s8[6291456]{0:T(1024)(128)(4,1)} %bitcast.278), calls=%async_computation.1 | async-start | bytes 8388608
  143.0 5.5 %copy-start.9 = (f32[256,1024]{1,0:T(8,128)S(1)}, f32[256,1024]{1,0:T(8,128)}, u32[]{:S(2)}) copy-start(f32[256,1024]{1,0:T(8,128)} %copy-done.8) | copy-start | bytes 3145732
  143.0 5.5 %copy-start.16 = (f32[16,2048]{1,0:T(8,128)S(1)}, f32[16,2048]{1,0:T(8,128)}, u32[]{:S(2)}) copy-start(f32[16,2048]{1,0:T(8,128)} %param.24) | copy-start | bytes 393220
  143.0 8.8 %slice-start.1 = ((s8[6291456]{0:T(1024)(128)(4,1)}), s8[2097152]{0:T(1024)(128)(4,1)S(1)}, s32[]{:S(2)}) async-start(s8[6291456]{0:T(1024)(128)(4,1)} %bitcast.278), calls=%async_computation.2 | async-start | bytes 4194304
  158.0 18.3 %copy-start.5 = (f32[256,2048]{1,0:T(8,128)S(1)}, f32[256,2048]{1,0:T(8,128)}, u32[]{:S(2)}) copy-start(f32[256,2048]{1,0:T(8,128)} %copy-done.4) | copy-start | bytes 6291460
  158.0 18.2 %collective-permute-start.4 = (bf16[256,512]{0,1:T(8,128)(2,1)S(1)}, bf16[256,512]{0,1:T(8,128)(2,1)S(1)}, u32[]{:S(2)}, u32[]{:S(2)}) collective-permute-start(bf16[256,512]{0,1:T(8,128)(2,1)S(1)} %bitcast.303), channel_id=1, source_target_pairs={{0,1},{1,0},{2,3},{3,2},{4,5},{5,4},{6,7},{7,6},{8,9},{9,8},{10,11... | collective-permute-start | bytes 786440 | tf_op jit(solution)/shard_map/ppermute | solution.py:248
  187.5 4.2 %copy-start.12 = (bf16[256,1536]{0,1:T(8,128)(2,1)}, bf16[256,1536]{0,1:T(8,128)(2,1)S(1)}, u32[]{:S(2)}) copy-start(bf16[256,1536]{0,1:T(8,128)(2,1)S(1)} %copy.83) | copy-start | bytes 2359300
  191.7 6.8 %collective-permute-start.1 = (bf16[256,512]{0,1:T(8,128)(2,1)S(1)}, bf16[256,512]{0,1:T(8,128)(2,1)S(1)}, u32[]{:S(2)}, u32[]{:S(2)}) collective-permute-start(bf16[256,512]{0,1:T(8,128)(2,1)S(1)} %bitcast.295), channel_id=1, source_target_pairs={{0,1},{1,0},{2,3},{3,2},{4,5},{5,4},{6,7},{7,6},{8,9},{9,8},{10,11... | collective-permute-start | bytes 786440 | tf_op jit(solution)/shard_map/ppermute | solution.py:248
  195.1 5.8 %copy-start.24 = (f32[1,1,2048]{2,0,1:T(1,128)S(1)}, f32[1,1,2048]{2,0,1:T(1,128)}, u32[]{:S(2)}) copy-start(f32[1,1,2048]{2,0,1:T(1,128)} %get-tuple-element.37) | copy-start | bytes 24580
  230.2 135.1 %copy-start.22 = (f32[32,3,512]{2,0,1:T(8,128)S(1)}, f32[32,3,512]{2,0,1:T(8,128)}, u32[]{:S(2)}) copy-start(f32[32,3,512]{2,0,1:T(8,128)} %param.35) | copy-start | bytes 589828
  230.2 135.1 %copy-start.23 = (f32[32,3,512]{2,0,1:T(8,128)S(1)}, f32[32,3,512]{2,0,1:T(8,128)}, u32[]{:S(2)}) copy-start(f32[32,3,512]{2,0,1:T(8,128)} %param.34) | copy-start | bytes 589828
  296.8 71.3 %copy-start.25 = (f32[32,512]{1,0:T(8,128)S(1)}, f32[32,512]{1,0:T(8,128)}, u32[]{:S(2)}) copy-start(f32[32,512]{1,0:T(8,128)} %param.37) | copy-start | bytes 196612
  296.8 71.2 %copy-start.26 = (f32[32,512]{1,0:T(8,128)S(1)}, f32[32,512]{1,0:T(8,128)}, u32[]{:S(2)}) copy-start(f32[32,512]{1,0:T(8,128)} %param.36) | copy-start | bytes 196612
  296.8 73.4 %copy-start.1 = (f32[16,3,2048]{2,0,1:T(8,128)S(1)}, f32[16,3,2048]{2,0,1:T(8,128)}, u32[]{:S(2)}) copy-start(f32[16,3,2048]{2,0,1:T(8,128)} %param.26) | copy-start | bytes 1179652
  (22 other events, 38.7 us)
Sparse Core Ops, SparseCore 0:
  14.8 124.4 all-gather.1

commit v2 on v1

--- a/solution.py
+++ b/solution.py
@@ -38,9 +38,57 @@
         dst_ref=dst,
         send_sem=send,
         recv_sem=recv,
-        device_id={axis: target},
+        device_id={axis: target} if isinstance(axis, str) else dict(zip(axis, target)),
         device_id_type=pl.DeviceIdType.MESH,
     )
+
+
+def greet(friends):
+    barrier = pltpu.get_barrier_semaphore()
+    for axis, target in friends:
+        pl.semaphore_signal(
+            barrier,
+            inc=1,
+            device_id={axis: target} if isinstance(axis, str) else dict(zip(axis, target)),
+            device_id_type=pl.DeviceIdType.MESH,
+        )
+    pl.semaphore_wait(barrier, len(friends))
+
+
+def all_places():
+    y, x, z, core, mp = (lax.axis_index(a) for a in AXES)
+    return [
+        (core, [("dp_3", 1 - core)]),
+        (2 * mp + z, [("dp_2", 1 - z), ("mp", 1 - mp), (("dp_2", "mp"), (1 - z, 1 - mp))]),
+        (x, [("dp_1", lax.rem(x + k, 4)) for k in (1, 2, 3)]),
+        (y, [("dp_0", lax.rem(y + k, 4)) for k in (1, 2, 3)]),
+    ]
+
+
+def sum_over_all(value, inbox, send, recv):
+    for stage, (slot, partners) in enumerate(all_places()):
+        inbox[stage, slot] = value
+        copies = [
+            remote(
+                inbox.at[stage, slot],
+                inbox.at[stage, slot],
+                send.at[stage, k],
+                recv.at[stage, k],
+                axis,
+                target,
+            )
+            for k, (axis, target) in enumerate(partners)
+        ]
+        for c in copies:
+            c.start()
+        for c in copies:
+            c.wait_recv()
+        value = inbox[stage, 0]
+        for k in range(1, len(partners) + 1):
+            value = value + inbox[stage, k]
+        for c in copies:
+            c.wait_send()
+    return value
 
 
 def ring_start(axis, part, relay, direct, send, recv):
@@ -95,7 +143,9 @@
     proj_own,
     proj_other,
     packed,
+    loss_part,
     out,
+    totals,
     shaped_in,
     proj_in,
     packed_in,
@@ -106,18 +156,10 @@
     *rest,
 ):
     boxes_a, boxes_b, boxes_c, boxes_d = rest[0:4], rest[4:8], rest[8:12], rest[12:16]
-    last, last_in, pair_send, pair_recv, send, recv, z_send, z_recv = rest[16:]
+    last, last_in, pair_send, pair_recv, send, recv, z_send, z_recv = rest[16:24]
+    inbox, sum_send, sum_recv = rest[24:]
     y, x, z, core = (lax.axis_index(a) for a in AXES[:4])
-    barrier = pltpu.get_barrier_semaphore()
-    friends = [("dp_3", 1 - core), ("dp_2", 1 - z)]
-    friends += [("dp_1", lax.rem(x + k, 4)) for k in (1, 3)]
-    friends += [("dp_0", lax.rem(y + k, 4)) for k in (1, 3)]
-    for axis, target in friends:
-        pl.semaphore_signal(
-            barrier, inc=1, device_id={axis: target}, device_id_type=pl.DeviceIdType.MESH
-        )
-    pl.semaphore_wait(barrier, len(friends))
-
+    greet([friend for _, partners in all_places() for friend in partners])
     pair = [
         remote(a, b, pair_send.at[k], pair_recv.at[k], "dp_3", 1 - core)
         for k, (a, b) in enumerate(
@@ -190,12 +232,18 @@
         z_copies.append(c)
     for k, c in enumerate(z_copies):
         c.wait_recv()
-        out[:, k * HALF : (k + 1) * HALF] = last[k, z] + last_in[k]
+        both = last[k, z] + last_in[k]
+        out[2 * k] = both[:, :512]
+        out[2 * k + 1] = both[:, 512:]
     for c in [*pair, *z_copies]:
         c.wait_send()
-
-
-def reduce_gradients(shaped, d_proj, packed):
+    squares = jnp.sum(out[...] * out[...])
+    row = lax.broadcasted_iota(jnp.int32, (8, 128), 0)
+    value = jnp.where(row == 0, squares, loss_part[...])
+    totals[...] = sum_over_all(value, inbox, sum_send, sum_recv)
+
+
+def reduce_gradients(shaped, d_proj, packed, loss_part):
     core = lax.axis_index("dp_3")
 
     def split(values):
@@ -214,9 +262,12 @@
 
     return pl.pallas_call(
         reduce_kernel,
-        out_shape=jax.ShapeDtypeStruct((32, 2 * HALF), jnp.float32),
-        in_specs=[vmem] * 5,
-        out_specs=vmem,
+        out_shape=(
+            jax.ShapeDtypeStruct((4, 32, 512), jnp.float32),
+            jax.ShapeDtypeStruct((8, 128), jnp.float32),
+        ),
+        in_specs=[vmem] * 6,
+        out_specs=(vmem, vmem),
         scratch_shapes=[
             pltpu.VMEM((ROWS, SEQ), jnp.bfloat16),
             pltpu.VMEM((ROWS, SEQ), jnp.bfloat16),
@@ -237,11 +288,14 @@
             pltpu.SemaphoreType.DMA((4, 6)),
             pltpu.SemaphoreType.DMA((2,)),
             pltpu.SemaphoreType.DMA((2,)),
+            pltpu.VMEM((4, 4, 8, 128), jnp.float32),
+            pltpu.SemaphoreType.DMA((4, 3)),
+            pltpu.SemaphoreType.DMA((4, 3)),
         ],
         compiler_params=pltpu.CompilerParams(
             collective_id=1, has_side_effects=True, vmem_limit_bytes=60 * 2**20
         ),
-    )(shaped_own, shaped_other, proj_own, proj_other, packed)
+    )(shaped_own, shaped_other, proj_own, proj_other, packed, loss_part)
 
 
 def swapped(values):
@@ -429,12 +483,12 @@
     packed = jnp.concatenate(
         [v.reshape(rows_all, local_inner) for v in (d_query, d_key, d_value, attended)], axis=1
     )
-    grads = reduce_gradients(shaped, d_proj, packed)
-    grad_qkv = grads[:, : 3 * local_inner].reshape(-1, 3, local_inner)
-    grad_out = grads[:, 3 * local_inner :]
-    squares, loss_sum = lax.psum(
-        jnp.stack([jnp.sum(grads * grads), loss_part / lax.axis_size("mp")]), DP_MP
-    )
+    grads, totals = reduce_gradients(
+        shaped, d_proj, packed, jnp.full((8, 128), loss_part / lax.axis_size("mp"))
+    )
+    grad_qkv = jnp.moveaxis(grads[:3], 0, 1)
+    grad_out = grads[3]
+    squares, loss_sum = totals[0, 0], totals[1, 0]
     rms_value = jnp.sqrt(squares / (4 * D * INNER))
     factor = 1.0 / jnp.maximum(rms_value, 1.0)
 

time: 382 us -> 328 us (0.86)
  blocking collectives: 63 us -> 0 us
  Pallas kernels: 66.6 us -> 77.2 us
    psum x1 -> x0, blocking collectives: 63 us -> none  [per_device(): lax.psum(jnp.stack([jnp.sum(grads * grads), loss_part / lax.axis_size('mp...]
    pallas_call x1, Pallas kernels: 66.6 us -> 77.2 us  [reduce_gradients(): pl.pallas_call(reduce_kernel, out_shape=(jax.ShapeDtypeStruct((4, 32, 512...]
    unnamed x84 -> x81, local copies, waits for them, and re-layouts: 16.2 us -> 14 us
  transfers between devices with their start and end apart: 6 -> 6, of which waited for: 4 -> 4; matrix products, arithmetic and copies ran while one was open for 17% -> 20% of each run, Pallas kernels for 0% -> 0%
where the time goes in v2:
time: 328 us; the launch traced here: 323 us
  waiting for transfers between devices  82.3 us (25%)
  Pallas kernels  77.2 us (24%)
  matrix products  71.1 us (22%)
  local copies, waits for them, and re-layouts  30.9 us (9%)
  between operations  24.1 us (7%)
  starting transfers between devices  19.9 us (6%)
  other arithmetic  17.5 us (5%)
    ppermute x5, waiting for transfers between devices, swapped(): return lax.ppermute(values, 'mp', [(0, 1), (1, 0)])  82.2 us
    pallas_call x1, Pallas kernels, reduce_gradients(): pl.pallas_call(reduce_kernel, out_shape=(jax.ShapeDtypeStruct((4, 32, 512...  77.2 us
    ppermute x5, starting transfers between devices, swapped(): return lax.ppermute(values, 'mp', [(0, 1), (1, 0)])  19.9 us
    unnamed x81, local copies, waits for them, and re-layouts  14 us
    dot_general x3, matrix products, tail(): lax.dot_general(normed, final, (((1,), (1,)), ((), ())), precision=lax.Pr...  12.1 us
    dot_general x3, matrix products, front(): jnp.dot(shaped, w_qkv.reshape(D, 3 * local_inner), preferred_element_type...  9.35 us
    dot_general x3, matrix products, front(): lax.dot_general(swapped(attended), other_out, contract, preferred_element...  7.69 us
    dot_general x3, matrix products, front(): lax.dot_general(attended, w_out, contract, preferred_element_type=jnp.flo...  7.48 us
  transfers between devices with their start and end apart: 6, of which 4 were waited for; matrix products, arithmetic and copies ran while one was open for 20% of the time, Pallas kernels for 0%

profile of v2, /device:TPU:1, one launch (start us, length us, event | category | flops | bytes accessed | tf_op | source)
XLA Modules:
  0.0 322.8 jit_solution(8919583409891938533)
XLA Ops:
  7.2 4.5 %collective-permute-start = (bf16[32,512]{1,0:T(8,128)(2,1)}, bf16[32,512]{1,0:T(8,128)(2,1)S(1)}, u32[]{:S(2)}, u32[]{:S(2)}) collective-permute-start(bf16[32,512]{1,0:T(8,128)(2,1)} %param.33), channel_id=1, source_target_pairs={{0,1},{1,0},{2,3},{3,2},{4,5},{5,4},{6,7},{7,6},{8,9},{9,8},{10,11... | collective-permute-start | bytes 98312 | tf_op jit(solution)/shard_map/ppermute | solution.py:302
  18.4 8.9 %copy.77 = bf16[2048,3,512]{0,2,1:T(8,128)(2,1)} copy(bf16[2048,3,512]{2,0,1:T(8,128)(2,1)} %param.27) | data formatting | bytes 12582912 | tf_op args[8]
  27.3 3.7 %fusion.69 = (f32[256,1024]{1,0:T(8,128)S(1)}, f32[256,1024]{1,0:T(8,128)S(1)}) fusion(f32[1024]{0:T(1024)S(1)} %multiply_exponential_fusion), kind=kLoop, calls=%fused_computation.96 | loop fusion | flops 262144 | bytes 2101248 | tf_op jit(solution)/shard_map/sin | solution.py:316
  39.7 3.0 collective-permute-start.2
  48.5 3.3 %fusion.150 = (f32[256]{0:T(256)S(1)}, f32[256,2048]{1,0:T(8,128)S(1)}) fusion(f32[256,1024]{1,0:T(8,128)} %copy-done.8, f32[256,1024]{1,0:T(8,128)S(1)} %get-tuple-element.31, f32[256,16]{1,0:T(8,128)} %copy-done.11, f32[16,2048]{1,0:T(8,128)} %param.29), kind=kOutput, calls=%fused_computation.212 | convolution fusion | flops 102235904 | bytes 4342784 | tf_op jit(solution)/shard_map/dot_general | solution.py:383
  61.3 2.3 constant_dynamic-slice_fusion.2
  63.9 2.6 fusion.159
  66.5 73.7 %collective-permute-done.3 = bf16[2048,512]{1,0:T(8,128)(2,1)} collective-permute-done((bf16[2048,512]{1,0:T(8,128)(2,1)}, bf16[2048,512]{1,0:T(8,128)(2,1)}, u32[]{:S(2)}, u32[]{:S(2)}) %collective-permute-start.3) | collective-permute-done | bytes 2097184 | tf_op jit(solution)/shard_map/ppermute | solution.py:302
  140.2 2.8 fusion.155
  143.9 4.6 %multiply_add_fusion = f32[256,16]{0,1:T(8,128)S(1)} fusion(f32[256,16]{0,1:T(8,128)S(1)} %copy.83, f32[16,2048]{1,0:T(8,128)S(1)} %copy-done.17, f32[256,2048]{1,0:T(8,128)S(1)} %get-tuple-element.48, f32[256]{0:T(256)S(1)} %add_rsqrt_fusion.2, f32[256]{0:T(256)S(1)} %broadcast_multiply_fusion.4, f32[]{:T(128)} %bitcast.55, f32[]{:T(128)} %bitcast.3, ...), kind=kOutput, calls=%fused_computation.137 | convolution fusion | flops 101736448 | bytes 2263056 | tf_op jit(solution)/shard_map/dot_general | solution.py:422
  158.0 11.4 %collective-permute-start.4 = (bf16[256,512]{0,1:T(8,128)(2,1)S(1)}, bf16[256,512]{0,1:T(8,128)(2,1)S(1)}, u32[]{:S(2)}, u32[]{:S(2)}) collective-permute-start(bf16[256,512]{0,1:T(8,128)(2,1)S(1)} %bitcast.315), channel_id=1, source_target_pairs={{0,1},{1,0},{2,3},{3,2},{4,5},{5,4},{6,7},{7,6},{8,9},{9,8},{10,11... | collective-permute-start | bytes 786440 | tf_op jit(solution)/shard_map/ppermute | solution.py:302
  169.4 2.3 fusion.160
  171.7 4.5 %collective-permute-done.4 = bf16[256,512]{0,1:T(8,128)(2,1)S(1)} collective-permute-done((bf16[256,512]{0,1:T(8,128)(2,1)S(1)}, bf16[256,512]{0,1:T(8,128)(2,1)S(1)}, u32[]{:S(2)}, u32[]{:S(2)}) %collective-permute-start.4) | collective-permute-done | bytes 262176 | tf_op jit(solution)/shard_map/ppermute | solution.py:302
  176.2 2.5 fusion.158
  180.6 5.5 %fusion.12 = bf16[256,1536]{1,0:T(8,128)(2,1)} fusion(bf16[2048,2560]{1,0:T(8,128)(2,1)} %all-gather.2.cloned.1.call-done, f32[256,2048]{1,0:T(8,128)S(1)} %get-tuple-element.40, f32[2048]{0:T(1024)S(1)} %bitcast.326, f32[2048]{0:T(1024)S(1)} %bitcast.324, f32[256]{0:T(256)S(1)} %copy-done.35, f32[256]{0:T(256)S(1)} %copy-done.33), kind=kOutput, calls=%fused_computation.18 | convolution fusion | flops 1613627392 | bytes 9193472 | tf_op jit(solution)/shard_map/dot_general | solution.py:393
  195.1 3.4 %collective-permute-done.1 = bf16[256,512]{0,1:T(8,128)(2,1)S(1)} collective-permute-done((bf16[256,512]{0,1:T(8,128)(2,1)S(1)}, bf16[256,512]{0,1:T(8,128)(2,1)S(1)}, u32[]{:S(2)}, u32[]{:S(2)}) %collective-permute-start.1) | collective-permute-done | bytes 262176 | tf_op jit(solution)/shard_map/ppermute | solution.py:302
  198.5 2.3 fusion.15
  200.9 2.6 fusion.152
  204.3 5.7 %fusion.96 = (f32[]{:T(128)}, f32[256,16]{0,1:T(8,128)S(1)}) fusion(f32[]{:T(128)} %fusion.113, f32[]{:T(128)S(6)} %sub.173, f32[256,16]{0,1:T(8,128)S(1)} %copy.83, f32[256,16]{0,1:T(8,128)S(1)} %fusion.18, f32[]{:T(128)} %bitcast.71, f32[]{:T(128)} %bitcast.37, f32[256,16]{0,1:T(8,128)S(1)} %multiply_add_fusion, f32[]{:T(128)} %bitcast.55, f32[]{:T(128)} %bitcast.33, ...), kind=kOutput, calls=%fused_computation.134 | convolution fusion | flops 101765120 | bytes 2295840 | tf_op jit(solution)/shard_map/dot_general | solution.py:422
  210.0 2.3 fusion.138
  213.2 2.3 fusion.45
  217.1 3.8 %fusion.39 = bf16[8,64,256]{2,1,0:T(8,128)(2,1)} fusion(f32[8,256,256]{1,2,0:T(8,128)S(1)} %fusion.80, bf16[1,256,3,8,64]{1,4,3,2,0:T(8,128)(2,1)} %bitcast.303, f32[8,256,256]{1,2,0:T(8,128)} %get-tuple-element.42, f32[8,256]{1,0:T(8,128)S(1)} %get-tuple-element.41), kind=kOutput, calls=%fused_computation.62 | convolution fusion | flops 70912256 | bytes 8929280 | tf_op jit(solution)/shard_map/shqk,skhd->sqhd/dot_general | solution.py:474
  220.9 3.7 %fusion.42 = bf16[8,64,256]{2,1,0:T(8,128)(2,1)} fusion(f32[8,256,256]{1,2,0:T(8,128)S(1)} %fusion.80, bf16[1,256,3,8,64]{1,4,3,2,0:T(8,128)(2,1)} %bitcast.304, f32[8,256,256]{1,2,0:T(8,128)} %get-tuple-element.42, f32[8,256]{1,0:T(8,128)S(1)} %get-tuple-element.41), kind=kOutput, calls=%fused_computation.63 | convolution fusion | flops 70912256 | bytes 8929280 | tf_op jit(solution)/shard_map/shqk,sqhd->skhd/dot_general | solution.py:477
  231.5 77.2 %shard_map.234 = (f32[4,32,512]{2,1,0:T(8,128)}, f32[8,128]{1,0:T(8,128)}) custom-call(bf16[1024,256]{1,0:T(8,128)(2,1)} %bitcast.297, bf16[1024,256]{1,0:T(8,128)(2,1)} %bitcast.296, bf16[1024,256]{1,0:T(8,128)(2,1)} %bitcast.299, bf16[1024,256]{1,0:T(8,128)(2,1)} %bitcast.298, bf16[256,2048]{1,0:T(8,128)(2,1)} %pad_maximum_fusion.1.packed, ...), custom_call_target="tpu_custom_call" | custom-call | tf_op jit(solution)/shard_map/pallas_call | solution.py:263
  (162 shorter events, 59.9 us)
Async XLA Ops:
  7.2 26.2 %copy-start = (f32[16,3,2048]{2,0,1:T(8,128)S(1)}, f32[16,3,2048]{2,0,1:T(8,128)}, u32[]{:S(2)}) copy-start(f32[16,3,2048]{2,0,1:T(8,128)} %param.26) | copy-start | bytes 1179652
  7.2 173.4 %all-gather.2.cloned.1.call-start = ((), (), s32[]{:S(2)}) async-start(), calls=%async_computation | async-start | bytes 10649600 | tf_op jit(solution)/shard_map/all_gather | solution.py:435
  7.2 6.0 %collective-permute-start = (bf16[32,512]{1,0:T(8,128)(2,1)}, bf16[32,512]{1,0:T(8,128)(2,1)S(1)}, u32[]{:S(2)}, u32[]{:S(2)}) collective-permute-start(bf16[32,512]{1,0:T(8,128)(2,1)} %param.33), channel_id=1, source_target_pairs={{0,1},{1,0},{2,3},{3,2},{4,5},{5,4},{6,7},{7,6},{8,9},{9,8},{10,11... | collective-permute-start | bytes 98312 | tf_op jit(solution)/shard_map/ppermute | solution.py:302
  15.4 27.7 %copy-start.36 = (f32[17,1]{0,1:T(1,128)}, f32[17,1]{0,1:T(1,128)S(1)}, u32[]{:S(2)}) copy-start(f32[17,1]{0,1:T(1,128)S(1)} %get-tuple-element.56) | copy-start | bytes 208
  15.4 27.7 %copy-start.37 = (f32[17,1]{0,1:T(1,128)}, f32[17,1]{0,1:T(1,128)S(1)}, u32[]{:S(2)}) copy-start(f32[17,1]{0,1:T(1,128)S(1)} %get-tuple-element.57) | copy-start | bytes 208
  18.4 24.6 %copy-start.11 = (f32[256,16]{1,0:T(8,128)}, f32[256,16]{1,0:T(8,128)S(1)}, u32[]{:S(2)}) copy-start(f32[256,16]{1,0:T(8,128)S(1)} %add.195) | copy-start | bytes 49156
  39.7 26.8 %collective-permute-start.2 = (bf16[256,512]{0,1:T(8,128)(2,1)}, bf16[256,512]{0,1:T(8,128)(2,1)}, u32[]{:S(2)}, u32[]{:S(2)}) collective-permute-start(bf16[256,512]{0,1:T(8,128)(2,1)} %bitcast.52), channel_id=1, source_target_pairs={{0,1},{1,0},{2,3},{3,2},{4,5},{5,4},{6,7},{7,6},{8,9},{9,8},{10,11... | collective-permute-start | bytes 786440 | tf_op jit(solution)/shard_map/ppermute | solution.py:302
  42.7 97.5 %collective-permute-start.3 = (bf16[2048,512]{1,0:T(8,128)(2,1)}, bf16[2048,512]{1,0:T(8,128)(2,1)}, u32[]{:S(2)}, u32[]{:S(2)}) collective-permute-start(bf16[2048,512]{1,0:T(8,128)(2,1)} %param.28), channel_id=1, source_target_pairs={{0,1},{1,0},{2,3},{3,2},{4,5},{5,4},{6,7},{7,6},{8,9},{9,8},{10,11... | collective-permute-start | bytes 6291464 | tf_op jit(solution)/shard_map/ppermute | solution.py:302
  63.9 76.3 %copy-start.3 = (f32[256,2048]{1,0:T(8,128)S(1)}, f32[256,2048]{1,0:T(8,128)}, u32[]{:S(2)}) copy-start(f32[256,2048]{1,0:T(8,128)} %copy-done.2) | copy-start | bytes 6291460
  63.9 76.3 %copy-start.31 = (f32[1,1,2048]{2,0,1:T(1,128)S(1)}, f32[1,1,2048]{2,0,1:T(1,128)}, u32[]{:S(2)}) copy-start(f32[1,1,2048]{2,0,1:T(1,128)} %get-tuple-element.25) | copy-start | bytes 24580
  140.2 11.7 %slice-start = ((s8[6291456]{0:T(1024)(128)(4,1)}), s8[4194304]{0:T(1024)(128)(4,1)S(1)}, s32[]{:S(2)}) async-start(s8[6291456]{0:T(1024)(128)(4,1)} %bitcast.290), calls=%async_computation.1 | async-start | bytes 8388608
  143.0 5.5 %copy-start.9 = (f32[256,1024]{1,0:T(8,128)S(1)}, f32[256,1024]{1,0:T(8,128)}, u32[]{:S(2)}) copy-start(f32[256,1024]{1,0:T(8,128)} %copy-done.8) | copy-start | bytes 3145732
  143.0 5.5 %copy-start.16 = (f32[16,2048]{1,0:T(8,128)S(1)}, f32[16,2048]{1,0:T(8,128)}, u32[]{:S(2)}) copy-start(f32[16,2048]{1,0:T(8,128)} %param.24) | copy-start | bytes 393220
  143.0 8.8 %slice-start.1 = ((s8[6291456]{0:T(1024)(128)(4,1)}), s8[2097152]{0:T(1024)(128)(4,1)S(1)}, s32[]{:S(2)}) async-start(s8[6291456]{0:T(1024)(128)(4,1)} %bitcast.290), calls=%async_computation.2 | async-start | bytes 4194304
  158.0 18.3 %copy-start.5 = (f32[256,2048]{1,0:T(8,128)S(1)}, f32[256,2048]{1,0:T(8,128)}, u32[]{:S(2)}) copy-start(f32[256,2048]{1,0:T(8,128)} %copy-done.4) | copy-start | bytes 6291460
  158.0 18.2 %collective-permute-start.4 = (bf16[256,512]{0,1:T(8,128)(2,1)S(1)}, bf16[256,512]{0,1:T(8,128)(2,1)S(1)}, u32[]{:S(2)}, u32[]{:S(2)}) collective-permute-start(bf16[256,512]{0,1:T(8,128)(2,1)S(1)} %bitcast.315), channel_id=1, source_target_pairs={{0,1},{1,0},{2,3},{3,2},{4,5},{5,4},{6,7},{7,6},{8,9},{9,8},{10,11... | collective-permute-start | bytes 786440 | tf_op jit(solution)/shard_map/ppermute | solution.py:302
  187.5 4.2 %copy-start.12 = (bf16[256,1536]{0,1:T(8,128)(2,1)}, bf16[256,1536]{0,1:T(8,128)(2,1)S(1)}, u32[]{:S(2)}) copy-start(bf16[256,1536]{0,1:T(8,128)(2,1)S(1)} %copy.74) | copy-start | bytes 2359300
  191.7 6.8 %collective-permute-start.1 = (bf16[256,512]{0,1:T(8,128)(2,1)S(1)}, bf16[256,512]{0,1:T(8,128)(2,1)S(1)}, u32[]{:S(2)}, u32[]{:S(2)}) collective-permute-start(bf16[256,512]{0,1:T(8,128)(2,1)S(1)} %bitcast.307), channel_id=1, source_target_pairs={{0,1},{1,0},{2,3},{3,2},{4,5},{5,4},{6,7},{7,6},{8,9},{9,8},{10,11... | collective-permute-start | bytes 786440 | tf_op jit(solution)/shard_map/ppermute | solution.py:302
  195.1 5.8 %copy-start.24 = (f32[1,1,2048]{2,0,1:T(1,128)S(1)}, f32[1,1,2048]{2,0,1:T(1,128)}, u32[]{:S(2)}) copy-start(f32[1,1,2048]{2,0,1:T(1,128)} %get-tuple-element.27) | copy-start | bytes 24580
  230.9 79.8 %copy-start.25 = (f32[32,512]{1,0:T(8,128)S(1)}, f32[32,512]{1,0:T(8,128)}, u32[]{:S(2)}) copy-start(f32[32,512]{1,0:T(8,128)} %param.37) | copy-start | bytes 196612
  230.9 79.8 %copy-start.26 = (f32[32,512]{1,0:T(8,128)S(1)}, f32[32,512]{1,0:T(8,128)}, u32[]{:S(2)}) copy-start(f32[32,512]{1,0:T(8,128)} %param.36) | copy-start | bytes 196612
  230.9 81.3 %copy-start.22 = (f32[32,3,512]{2,0,1:T(8,128)S(1)}, f32[32,3,512]{2,0,1:T(8,128)}, u32[]{:S(2)}) copy-start(f32[32,3,512]{2,0,1:T(8,128)} %param.35) | copy-start | bytes 589828
  230.9 81.3 %copy-start.23 = (f32[32,3,512]{2,0,1:T(8,128)S(1)}, f32[32,3,512]{2,0,1:T(8,128)}, u32[]{:S(2)}) copy-start(f32[32,3,512]{2,0,1:T(8,128)} %param.34) | copy-start | bytes 589828
  231.5 83.2 %copy-start.1 = (f32[16,3,2048]{2,0,1:T(8,128)S(1)}, f32[16,3,2048]{2,0,1:T(8,128)}, u32[]{:S(2)}) copy-start(f32[16,3,2048]{2,0,1:T(8,128)} %param.26) | copy-start | bytes 1179652
  (22 other events, 39.3 us)
Sparse Core Ops, SparseCore 0:
  14.8 124.4 all-gather.1

commit v3 on v2

--- a/solution.py
+++ b/solution.py
@@ -138,10 +138,8 @@
 
 
 def reduce_kernel(
-    shaped_own,
-    shaped_other,
-    proj_own,
-    proj_other,
+    shaped,
+    proj,
     packed,
     loss_part,
     out,
@@ -163,7 +161,7 @@
     pair = [
         remote(a, b, pair_send.at[k], pair_recv.at[k], "dp_3", 1 - core)
         for k, (a, b) in enumerate(
-            [(packed, packed_in), (shaped_other, shaped_in), (proj_other, proj_in)]
+            [(packed, packed_in), (shaped.at[:, 1 - core], shaped_in), (proj.at[:, 1 - core], proj_in)]
         )
     ]
     for c in pair:
@@ -171,8 +169,8 @@
 
     def products(s_ref, p_ref, b_ref, add):
         def step(k, carry):
-            rows = pl.ds(pl.multiple_of(k * 256, 256), 256)
-            s, p = s_ref[rows], p_ref[rows]
+            rows = pl.ds(pl.multiple_of(k * 8, 8), 8)
+            s, p = (r[rows].reshape(256, SEQ) for r in (s_ref, p_ref))
             g = jnp.dot(s, b_ref[:, :HALF], preferred_element_type=jnp.float32)
             for j in range(4):
                 block = g[64 * j : 64 * j + 64]
@@ -186,7 +184,7 @@
 
         lax.fori_loop(0, 4, step, 0)
 
-    products(shaped_own, proj_own, packed, False)
+    products(shaped.at[:, core], proj.at[:, core], packed, False)
     for c in pair:
         c.wait_recv()
     products(shaped_in, proj_in, packed_in, True)
@@ -243,17 +241,7 @@
     totals[...] = sum_over_all(value, inbox, sum_send, sum_recv)
 
 
-def reduce_gradients(shaped, d_proj, packed, loss_part):
-    core = lax.axis_index("dp_3")
-
-    def split(values):
-        rows = values.T.reshape(ROWS // 32, 2, 32, SEQ)
-        own = lax.dynamic_index_in_dim(rows, core, 1, keepdims=False)
-        other = lax.dynamic_index_in_dim(rows, 1 - core, 1, keepdims=False)
-        return own.reshape(ROWS, SEQ), other.reshape(ROWS, SEQ)
-
-    shaped_own, shaped_other = split(shaped)
-    proj_own, proj_other = split(d_proj)
+def reduce_gradients(shaped, proj, packed, loss_part):
     vmem = pl.BlockSpec(memory_space=pltpu.VMEM)
     wire = jnp.float32
 
@@ -266,11 +254,11 @@
             jax.ShapeDtypeStruct((4, 32, 512), jnp.float32),
             jax.ShapeDtypeStruct((8, 128), jnp.float32),
         ),
-        in_specs=[vmem] * 6,
+        in_specs=[vmem] * 4,
         out_specs=(vmem, vmem),
         scratch_shapes=[
-            pltpu.VMEM((ROWS, SEQ), jnp.bfloat16),
-            pltpu.VMEM((ROWS, SEQ), jnp.bfloat16),
+            pltpu.VMEM((32, 32, SEQ), jnp.bfloat16),
+            pltpu.VMEM((32, 32, SEQ), jnp.bfloat16),
             pltpu.VMEM((SEQ, 2 * HALF), jnp.bfloat16),
             pltpu.VMEM((4, 256, HALF), jnp.float32),
             pltpu.VMEM((4, 256, HALF), jnp.float32),
@@ -295,11 +283,435 @@
         compiler_params=pltpu.CompilerParams(
             collective_id=1, has_side_effects=True, vmem_limit_bytes=60 * 2**20
         ),
-    )(shaped_own, shaped_other, proj_own, proj_other, packed, loss_part)
-
-
-def swapped(values):
-    return lax.ppermute(values, "mp", [(0, 1), (1, 0)])
+    )(shaped, proj, packed, loss_part)
+
+
+TOKENS = 256
+WIDE = 256
+NT = (((1,), (1,)), ((), ()))
+TN = (((0,), (0,)), ((), ()))
+
+
+def dot(a, b, dims=(((1,), (0,)), ((), ()))):
+    return lax.dot_general(a, b, dims, preferred_element_type=jnp.float32)
+
+
+def gather_stream(held, slabs, send, recv):
+    y, x, z, core = (lax.axis_index(a) for a in AXES[:4])
+    near = {"dp_0": [lax.rem(y + k, 4) for k in (1, 3)], "dp_1": [lax.rem(x + k, 4) for k in (1, 3)]}
+    every = slice(None)
+    live = []
+
+    def go(spot, k, axis, target):
+        ref = held.at[(slabs, *spot)]
+        c = remote(ref, ref, send.at[k], recv.at[k], axis, target)
+        c.start()
+        live.append(c)
+        return c
+
+    def ring_direct(first):
+        for half, axis in enumerate(("dp_1", "dp_0") if first else ("dp_0", "dp_1")):
+            if first:
+                spot = (y, x, every, core, half)
+            elif half == 0:
+                spot = (y, every, every, core, half)
+            else:
+                spot = (every, x, every, core, half)
+            for side in range(2):
+                k = (1 if first else 9) + 4 * half + side
+                go(spot, k, axis, near[axis][side])
+
+    def ring_relay(first):
+        base = 1 if first else 9
+        direct = live[-4:]
+        for half, axis in enumerate(("dp_1", "dp_0") if first else ("dp_0", "dp_1")):
+            for side in range(2):
+                direct[2 * half + side].wait_recv()
+                back = near[axis][1 - side]
+                if first:
+                    spot = (y, back) if axis == "dp_1" else (back, x)
+                else:
+                    spot = (every, back) if axis == "dp_1" else (back, every)
+                go((*spot, side, core, half), base + 4 * half + 2 + side, axis, near[axis][side])
+
+    def step(k):
+        if k == 0:
+            go((y, x, z, core), 0, "dp_2", 1 - z)
+        elif k == 1:
+            live[-1].wait_recv()
+            ring_direct(True)
+        elif k == 2:
+            ring_relay(True)
+        elif k == 3:
+            for c in live[-4:]:
+                c.wait_recv()
+            ring_direct(False)
+        elif k == 4:
+            ring_relay(False)
+        elif k == 5:
+            for c in live[-4:]:
+                c.wait_recv()
+            go((every, every, every, core), 17, "dp_3", 1 - core)
+        else:
+            live[-1].wait_recv()
+            for c in live:
+                c.wait_send()
+
+    return step
+
+
+def three_terms(v8):
+    high = v8.astype(jnp.bfloat16).astype(jnp.float32)
+    rest = v8 - high
+    middle = rest.astype(jnp.bfloat16).astype(jnp.float32)
+    low = rest - middle
+    group = lax.broadcasted_iota(jnp.int32, v8.shape, 1) // 16
+    picked = jnp.where(
+        (group == 0) | (group == 1) | (group == 3),
+        high,
+        jnp.where((group == 2) | (group == 5), middle, jnp.where(group == 4, low, 0.0)),
+    )
+    return picked.astype(jnp.bfloat16)
+
+
+def step_kernel(
+    coef,
+    latent8,
+    mods,
+    placed,
+    teacher_embed,
+    teacher_final,
+    student_embed,
+    student_final,
+    student_back,
+    teacher_qkv,
+    teacher_out,
+    student_qkv,
+    student_out,
+    shaped_t,
+    proj_t,
+    packed,
+    loss_part,
+    held,
+    near_qkv,
+    hidden,
+    hidden_s,
+    mixed,
+    shaped,
+    shaped_s,
+    qkv,
+    heads,
+    heads_in,
+    weights,
+    terms,
+    inverses,
+    d_attn,
+    qkv_sem,
+    swap_send,
+    swap_recv,
+    t_send,
+    t_recv,
+    s_send,
+    s_recv,
+):
+    y, x, z, core, mp = (lax.axis_index(a) for a in AXES)
+    load = pltpu.make_async_copy(teacher_qkv, near_qkv, qkv_sem)
+    load.start()
+    held[0:3, y, x, z, core] = student_qkv[...]
+    held[3, y, x, z, core] = student_out[...]
+    friends = [("dp_3", 1 - core), ("dp_2", 1 - z), ("mp", 1 - mp)]
+    friends += [("dp_1", lax.rem(x + k, 4)) for k in (1, 3)]
+    friends += [("dp_0", lax.rem(y + k, 4)) for k in (1, 3)]
+    greet(friends)
+
+    def swap(src, dst, k):
+        c = remote(src, dst, swap_send.at[k], swap_recv.at[k], "mp", 1 - mp)
+        c.start()
+        return c
+
+    spot = (y, x, z, core)
+    swaps = [
+        swap(teacher_out.at[spot], held.at[(5, *spot)], 0),
+        swap(student_out, held.at[(4, *spot)], 1),
+    ]
+    t_step = gather_stream(held, pl.ds(5, 1), t_send, t_recv)
+    s_step = gather_stream(held, pl.ds(0, 5), s_send, s_recv)
+
+    def columns(k, width):
+        return pl.ds(pl.multiple_of(k * width, width), width)
+
+    def spread(v8, b_ref, out, base=None):
+        terms8 = three_terms(v8)
+
+        def body(n, carry):
+            cols = columns(n, WIDE)
+            h = dot(terms8, b_ref[:, cols])
+            out[:, cols] = h if base is None else h + base[:, cols]
+            return carry
+
+        lax.fori_loop(0, D // WIDE, body, 0)
+
+    def shape(hid, which, out):
+        def body(n, carry):
+            rows = columns(n, 16)
+            v = hid[rows]
+            c = v - jnp.mean(v, axis=-1, keepdims=True)
+            inv = lax.rsqrt(jnp.mean(c * c, axis=-1, keepdims=True) + LN_EPS)
+            s = c * inv * (1.0 + mods[which, 1:2]) + mods[which, 0:1]
+            out[rows] = s.astype(jnp.bfloat16)
+            return carry
+
+        lax.fori_loop(0, TOKENS // 16, body, 0)
+
+    def project(src, weight):
+        def body(j, carry):
+            qkv[j] = dot(src[...], weight(j)).astype(jnp.bfloat16)
+            return carry
+
+        lax.fori_loop(0, 3, body, 0)
+
+    lane = lax.broadcasted_iota(jnp.int32, (1, 128), 1)
+    low_f = jnp.where(lane < 64, 1.0, 0.0)
+    sides = [low_f.astype(jnp.bfloat16), (1.0 - low_f).astype(jnp.bfloat16)]
+    is_low = lax.broadcasted_iota(jnp.int32, (TOKENS, 128), 1) < 64
+
+    def attend(out, keep):
+        def body(hp, carry):
+            cols = columns(hp, 128)
+            q, k, v = qkv[0, :, cols], qkv[1, :, cols], qkv[2, :, cols]
+            outs = []
+            for h in range(2):
+                s = dot(q * sides[h], k, NT) * 0.125
+                e = jnp.exp(s - jnp.max(s, axis=-1, keepdims=True))
+                w = e / jnp.sum(e, axis=-1, keepdims=True)
+                if keep:
+                    weights[2 * hp + h] = w
+                outs.append(dot(w.astype(jnp.bfloat16), v))
+            out[:, cols] = jnp.where(is_low, outs[0], outs[1]).astype(jnp.bfloat16)
+            return carry
+
+        lax.fori_loop(0, 4, body, 0)
+
+    def mix(att, weight, which, base):
+        def body(n, carry):
+            cols = columns(n, 512)
+            p = dot(att[...], weight(n), NT)
+            mixed[:, cols] = base[:, cols] + mods[which, 2:3, cols] * p
+            return carry
+
+        lax.fori_loop(0, 4, body, 0)
+
+    def predict(final, keep):
+        def body(n, carry):
+            rows = columns(n, 16)
+            v = mixed[rows]
+            c = v - jnp.mean(v, axis=-1, keepdims=True)
+            inv = lax.rsqrt(jnp.mean(c * c, axis=-1, keepdims=True) + LN_EPS)
+            u = c * inv
+            if keep:
+                mixed[rows] = u
+                inverses[rows] = jnp.broadcast_to(inv, (16, 128))
+            high = u.astype(jnp.bfloat16)
+            rest = u - high.astype(jnp.float32)
+            middle = rest.astype(jnp.bfloat16)
+            terms[0, rows] = high
+            terms[1, rows] = middle
+            terms[2, rows] = (rest - middle.astype(jnp.float32)).astype(jnp.bfloat16)
+            return carry
+
+        lax.fori_loop(0, TOKENS // 16, body, 0)
+        r = dot(terms[0], final[...], NT)
+        m = dot(terms[1], final[0:256], NT)
+        small = dot(terms[2], final[0:128], NT)
+        return (
+            r[:, 0:128]
+            + (r[:, 128:256] + m[:, 0:128])
+            + (r[:, 256:384] + m[:, 128:256] + small)
+        )
+
+    def other_rows(slab):
+        return lambda n: held[slab, n].reshape(512, 512)
+
+    a_f, s_f, a_m, s_m, a_l, s_l, row_weight = (coef[k] for k in range(7))
+
+    lat0 = latent8[...]
+    spread(lat0, teacher_embed, hidden, placed)
+    shape(hidden, 0, shaped)
+    for c in swaps:
+        c.wait_recv()
+    t_step(0)
+    s_step(0)
+    load.wait()
+    project(shaped, lambda j: near_qkv[j])
+    t_step(1)
+    attend(heads.at[0], False)
+    swaps.append(swap(heads.at[0], heads_in.at[0], 2))
+    t_step(2)
+    spread(lat0, student_embed, hidden_s, placed)
+    t_step(3)
+    s_step(1)
+    shape(hidden_s, 2, shaped_s)
+    t_step(4)
+    s_step(2)
+    mix(heads.at[0], lambda n: teacher_out[n].reshape(512, 512), 0, hidden)
+    t_step(5)
+    s_step(3)
+    t_step(6)
+    swaps[2].wait_recv()
+    mix(heads_in.at[0], other_rows(5), 0, mixed)
+    eps0 = predict(teacher_final, False)
+    lat1 = a_m * (lat0 - s_f * eps0) / a_f + s_m * eps0
+
+    spread(lat1, teacher_embed, hidden, placed)
+    shape(hidden, 1, shaped)
+    project(shaped, lambda j: near_qkv[j])
+    attend(heads.at[1], False)
+    swaps.append(swap(heads.at[1], heads_in.at[1], 3))
+    s_step(4)
+    mix(heads.at[1], lambda n: teacher_out[n].reshape(512, 512), 1, hidden)
+    swaps[3].wait_recv()
+    mix(heads_in.at[1], other_rows(5), 1, mixed)
+    eps1 = predict(teacher_final, False)
+    lat2 = a_l * (lat1 - s_m * eps1) / a_m + s_l * eps1
+    target = (lat0 - a_f / a_l * lat2) / (s_f - a_f * s_l / a_l)
+
+    s_step(5)
+
+    def turn(src, out):
+        def body(n, carry):
+            t = src[:, columns(n, 128)].astype(jnp.float32).T.astype(jnp.bfloat16)
+            out[pl.ds(2 * n, 2)] = t.reshape(2, 2, 32, TOKENS)
+            return carry
+
+        lax.fori_loop(0, D // 128, body, 0)
+
+    turn(shaped_s, shaped_t)
+    s_step(6)
+    project(shaped_s, lambda j: held[j].reshape(D, 512))
+    attend(heads.at[2], True)
+    swaps.append(swap(heads.at[2], heads_in.at[2], 4))
+    mix(heads.at[2], other_rows(3), 2, hidden_s)
+    swaps[4].wait_recv()
+    mix(heads_in.at[2], other_rows(4), 2, mixed)
+    error = predict(student_final, True) - target
+    lanes = lax.broadcasted_iota(jnp.int32, error.shape, 1)
+    loss_part[...] = jnp.full(
+        (8, 128), 0.5 * row_weight * jnp.sum(jnp.where(lanes < 16, error * error, 0.0))
+    )
+
+    spread(2.0 * row_weight * error, student_back, hidden)
+
+    def back(n, carry):
+        rows = columns(n, 16)
+        up, u = hidden[rows], mixed[rows]
+        first_mean = jnp.mean(up, axis=-1, keepdims=True)
+        second_mean = jnp.mean(up * u, axis=-1, keepdims=True)
+        d = (up - first_mean - u * second_mean) * inverses[rows, 0:1]
+        shaped[rows] = (mods[2, 2:3] * d).astype(jnp.bfloat16)
+        return carry
+
+    lax.fori_loop(0, TOKENS // 16, back, 0)
+    d_attn[...] = dot(shaped[...], held[3].reshape(D, 512)).astype(jnp.bfloat16)
+
+    def back_heads(hp, carry):
+        cols = columns(hp, 128)
+        q, k, v, da = qkv[0, :, cols], qkv[1, :, cols], qkv[2, :, cols], d_attn[:, cols]
+        outs = []
+        for h in range(2):
+            w = weights[2 * hp + h]
+            dp = dot(da * sides[h], v, NT)
+            ds = w * (dp - jnp.sum(w * dp, axis=-1, keepdims=True)) * 0.125
+            ds = ds.astype(jnp.bfloat16)
+            outs.append((dot(ds, k), dot(ds, q, TN), dot(w.astype(jnp.bfloat16), da, TN)))
+        for j in range(3):
+            spot = pl.ds(pl.multiple_of(j * 512 + hp * 128, 128), 128)
+            both = jnp.where(is_low, outs[0][j], outs[1][j])
+            packed[:, spot] = both.astype(jnp.bfloat16)
+        packed[:, pl.ds(pl.multiple_of(1536 + hp * 128, 128), 128)] = heads[2, :, cols]
+        return carry
+
+    lax.fori_loop(0, 4, back_heads, 0)
+    turn(shaped, proj_t)
+    for c in swaps:
+        c.wait_send()
+
+
+def three_parts(values):
+    high = lax.reduce_precision(values, 8, 7)
+    rest = values - high
+    middle = lax.reduce_precision(rest, 8, 7)
+    return high, middle, rest - middle
+
+
+def stacked(values):
+    h, m, l = three_parts(values)
+    zero = jnp.zeros_like(h)
+    return jnp.concatenate([h, m, h, l, h, m, zero, zero], axis=0).astype(jnp.bfloat16)
+
+
+def repeated(values):
+    return jnp.concatenate([jnp.tile(t, (8, 1)) for t in three_parts(values)], axis=0).astype(
+        jnp.bfloat16
+    )
+
+
+def whole_step(coef, latent8, mods, placed, teacher, student, qkv_t, out_t, qkv_s, out_s):
+    vmem = pl.BlockSpec(memory_space=pltpu.VMEM)
+    bf16, f32 = jnp.bfloat16, jnp.float32
+    return pl.pallas_call(
+        step_kernel,
+        out_shape=(
+            jax.ShapeDtypeStruct((32, 2, 32, TOKENS), bf16),
+            jax.ShapeDtypeStruct((32, 2, 32, TOKENS), bf16),
+            jax.ShapeDtypeStruct((TOKENS, D), bf16),
+            jax.ShapeDtypeStruct((8, 128), f32),
+        ),
+        in_specs=[pl.BlockSpec(memory_space=pltpu.SMEM)]
+        + [vmem] * 8
+        + [pl.BlockSpec(memory_space=pl.ANY)]
+        + [vmem] * 3,
+        out_specs=(vmem,) * 4,
+        scratch_shapes=[
+            pltpu.VMEM((6, 4, 4, 2, 2, 2, 16, 512), bf16),
+            pltpu.VMEM((3, D, 512), bf16),
+            pltpu.VMEM((TOKENS, D), f32),
+            pltpu.VMEM((TOKENS, D), f32),
+            pltpu.VMEM((TOKENS, D), f32),
+            pltpu.VMEM((TOKENS, D), bf16),
+            pltpu.VMEM((TOKENS, D), bf16),
+            pltpu.VMEM((3, TOKENS, 512), bf16),
+            pltpu.VMEM((3, TOKENS, 512), bf16),
+            pltpu.VMEM((3, TOKENS, 512), bf16),
+            pltpu.VMEM((8, TOKENS, TOKENS), f32),
+            pltpu.VMEM((3, TOKENS, D), bf16),
+            pltpu.VMEM((TOKENS, 128), f32),
+            pltpu.VMEM((TOKENS, 512), bf16),
+            pltpu.SemaphoreType.DMA,
+            pltpu.SemaphoreType.DMA((5,)),
+            pltpu.SemaphoreType.DMA((5,)),
+            pltpu.SemaphoreType.DMA((18,)),
+            pltpu.SemaphoreType.DMA((18,)),
+            pltpu.SemaphoreType.DMA((18,)),
+            pltpu.SemaphoreType.DMA((18,)),
+        ],
+        compiler_params=pltpu.CompilerParams(
+            collective_id=2, has_side_effects=True, vmem_limit_bytes=62 * 2**20
+        ),
+    )(
+        coef,
+        latent8,
+        mods,
+        placed,
+        stacked(teacher[0]),
+        repeated(teacher[1]),
+        stacked(student[0]),
+        repeated(student[1]),
+        stacked(student[1]),
+        jnp.moveaxis(qkv_t, 1, 0),
+        out_t.reshape(4, 4, 2, 2, 2, 16, 512),
+        jnp.moveaxis(qkv_s, 1, 0).reshape(3, 2, 16, 512),
+        out_s.reshape(2, 16, 512),
+    )
 
 
 def plan():
@@ -309,23 +721,14 @@
 
 
 def positions():
-    index = jnp.arange(SEQ, dtype=jnp.float32)[:, None]
     half = D // 2
     freqs = jnp.exp(-math.log(10000.0) * jnp.arange(half, dtype=jnp.float32) / half)
-    angles = index * freqs[None, :]
-    return jnp.concatenate([jnp.sin(angles), jnp.cos(angles)], axis=1)
-
-
-def normalize(values):
-    center = values - jnp.mean(values, axis=-1, keepdims=True)
-    inverse = lax.rsqrt(jnp.mean(center * center, axis=-1, keepdims=True) + LN_EPS)
-    return (center * inverse, inverse)
-
-
-def norm_back(upstream, normed, inverse):
-    first_mean = jnp.mean(upstream, axis=-1, keepdims=True)
-    second_mean = jnp.mean(upstream * normed, axis=-1, keepdims=True)
-    return (upstream - first_mean - normed * second_mean) * inverse
+    steps = jnp.arange(16, dtype=jnp.float32)[:, None]
+    coarse, fine = 16.0 * steps * freqs[None], steps * freqs[None]
+    sin_a, cos_a = jnp.sin(coarse)[:, None], jnp.cos(coarse)[:, None]
+    sin_b, cos_b = jnp.sin(fine)[None], jnp.cos(fine)[None]
+    both = [sin_a * cos_b + cos_a * sin_b, cos_a * cos_b - sin_a * sin_b]
+    return jnp.concatenate(both, axis=2).reshape(SEQ, D)
 
 
 def one_hot_rows(index, width):
@@ -354,138 +757,40 @@
     second_out,
 ):
     samples = clean_latent.shape[0]
-    rows_all = samples * SEQ
-    local_inner = teacher_out.shape[1]
-    local_heads = local_inner // HS
     alphas, sigmas = plan()
     table = jnp.stack([alphas, sigmas], axis=1)
-
-    def coefficients(tau):
-        picked = jnp.dot(one_hot_rows(tau, TGRID + 1), table, precision=lax.Precision.HIGHEST)
-        picked = jnp.repeat(picked, SEQ, axis=0)
-        return (picked[:, 0:1], picked[:, 1:2])
-
-    def modulation(mod_table, index, length):
-        picked = jnp.dot(
-            one_hot_rows(index, length),
-            mod_table.reshape(length, 3 * D),
-            precision=lax.Precision.HIGHEST,
-        )
-        return picked.reshape(samples, 3, D)
-
-    def gate_rows(modrows):
-        return jnp.repeat(modrows[:, 2], SEQ, axis=0)
-
-    placed = positions()
-
-    def front(latent, modrows, embed, w_qkv, w_out, other_out):
-        hidden = (
-            jnp.dot(latent, embed, precision=lax.Precision.HIGHEST).reshape(samples, SEQ, D)
-            + placed[None]
-        )
-        normed, unused = normalize(hidden)
-        shaped = (
-            (normed * (1.0 + modrows[:, None, 1]) + modrows[:, None, 0])
-            .astype(jnp.bfloat16)
-            .reshape(rows_all, D)
-        )
-        hidden = hidden.reshape(rows_all, D)
-        packed = jnp.dot(
-            shaped, w_qkv.reshape(D, 3 * local_inner), preferred_element_type=jnp.float32
-        )
-        packed = packed.astype(jnp.bfloat16).reshape(samples, SEQ, 3, local_heads, HS)
-        queries = packed[:, :, 0]
-        keys_all = packed[:, :, 1]
-        values = packed[:, :, 2]
-        scores = jnp.einsum(
-            "sqhd,skhd->shqk", queries, keys_all, preferred_element_type=jnp.float32
-        ) / math.sqrt(HS)
-        highest = jnp.max(scores, axis=-1, keepdims=True)
-        expos = jnp.exp(scores - highest)
-        weights = expos / jnp.sum(expos, axis=-1, keepdims=True)
-        rounded = weights.astype(jnp.bfloat16)
-        attended = jnp.einsum(
-            "shqk,skhd->sqhd", rounded, values, preferred_element_type=jnp.float32
-        )
-        attended = attended.astype(jnp.bfloat16).reshape(rows_all, local_inner)
-        contract = (((1,), (1,)), ((), ()))
-        projected = lax.dot_general(
-            attended, w_out, contract, preferred_element_type=jnp.float32
-        ) + lax.dot_general(
-            swapped(attended), other_out, contract, preferred_element_type=jnp.float32
-        )
-        return (hidden, shaped, queries, keys_all, values, weights, rounded, attended, projected)
-
-    def tail(hidden, modrows, projected, final):
-        mixed = hidden + gate_rows(modrows) * projected
-        normed, inverse = normalize(mixed)
-        predicted = lax.dot_general(
-            normed, final, (((1,), (1,)), ((), ())), precision=lax.Precision.HIGHEST
-        )
-        return (predicted, normed, inverse)
-
-    def teacher_eps(latent, modrows):
-        parts = front(latent, modrows, teacher_embed, teacher_qkv, teacher_out, teacher_other)
-        return tail(parts[0], modrows, parts[8], teacher_final)[0]
-
-    teacher_other = swapped(teacher_out)
-    flat = jnp.concatenate(
-        [student_qkv.reshape(-1, 3 * local_inner), student_out, swapped(student_out)], axis=1
-    )
-    whole = lax.all_gather(flat, DP, axis=0, tiled=True)
-    whole_qkv = whole[:, : 3 * local_inner]
-    whole_out = whole[:, 3 * local_inner : 4 * local_inner]
-    whole_other = whole[:, 4 * local_inner :]
     first = 2 * timestep
-    middle = first - 1
-    last = first - 2
-    a_first, s_first = coefficients(first)
-    a_middle, s_middle = coefficients(middle)
-    a_last, s_last = coefficients(last)
-    clean_rows = clean_latent.reshape(rows_all, PATCH_CH)
-    noise_rows = noise_draw.reshape(rows_all, PATCH_CH)
-    latent0 = a_first * clean_rows + s_first * noise_rows
-    eps_zero = teacher_eps(latent0, modulation(teacher_mod, first - 1, TGRID))
-    latent1 = a_middle * (latent0 - s_first * eps_zero) / a_first + s_middle * eps_zero
-    eps_one = teacher_eps(latent1, modulation(teacher_mod, middle - 1, TGRID))
-    latent2 = a_last * (latent1 - s_middle * eps_one) / a_middle + s_last * eps_one
-    target = (latent0 - a_first / a_last * latent2) / (s_first - a_first * s_last / a_last)
-    student_rows_mod = modulation(student_mod, timestep - 1, K)
-    hidden, shaped, queries, keys_all, values, weights, rounded, attended, projected = front(
-        latent0, student_rows_mod, student_embed, whole_qkv, whole_out, whole_other
-    )
-    predicted, normed, inverse = tail(hidden, student_rows_mod, projected, student_final)
-    sample_weight = jnp.dot(
+    taus = jnp.concatenate([first, first - 1, first - 2])
+    picked = jnp.dot(one_hot_rows(taus, TGRID + 1), table, precision=lax.Precision.HIGHEST)
+    weight = jnp.dot(
         one_hot_rows(bucket, NBUCKET), bucket_weights, precision=lax.Precision.HIGHEST
     )
-    row_weight = jnp.repeat(sample_weight, SEQ, axis=0)[:, None]
-    error = predicted - target
-    loss_part = jnp.sum(row_weight * error * error)
-    d_pred = 2.0 * row_weight * error
-    d_normed = jnp.dot(d_pred, student_final, precision=lax.Precision.HIGHEST)
-    d_mixed = norm_back(d_normed, normed, inverse)
-    d_proj = (gate_rows(student_rows_mod) * d_mixed).astype(jnp.bfloat16)
-    d_attn = jnp.dot(d_proj, whole_out, preferred_element_type=jnp.float32).astype(jnp.bfloat16)
-    d_attn = d_attn.reshape(samples, SEQ, local_heads, HS)
-    d_prob = jnp.einsum("sqhd,skhd->shqk", d_attn, values, preferred_element_type=jnp.float32)
-    d_score = (
-        weights * (d_prob - jnp.sum(weights * d_prob, axis=-1, keepdims=True)) / math.sqrt(HS)
-    ).astype(jnp.bfloat16)
-    d_query = jnp.einsum(
-        "shqk,skhd->sqhd", d_score, keys_all, preferred_element_type=jnp.float32
-    ).astype(jnp.bfloat16)
-    d_key = jnp.einsum(
-        "shqk,sqhd->skhd", d_score, queries, preferred_element_type=jnp.float32
-    ).astype(jnp.bfloat16)
-    d_value = jnp.einsum(
-        "shqk,sqhd->skhd", rounded, d_attn, preferred_element_type=jnp.float32
-    ).astype(jnp.bfloat16)
-    packed = jnp.concatenate(
-        [v.reshape(rows_all, local_inner) for v in (d_query, d_key, d_value, attended)], axis=1
-    )
-    grads, totals = reduce_gradients(
-        shaped, d_proj, packed, jnp.full((8, 128), loss_part / lax.axis_size("mp"))
-    )
+    coef = jnp.concatenate([picked.reshape(-1), weight, jnp.zeros((1,), jnp.float32)])
+    steps = one_hot_rows(jnp.concatenate([first - 1, first - 2]), TGRID)
+    mods = jnp.concatenate(
+        [
+            jnp.dot(steps, teacher_mod.reshape(TGRID, 3 * D), precision=lax.Precision.HIGHEST),
+            jnp.dot(
+                one_hot_rows(timestep - 1, K),
+                student_mod.reshape(K, 3 * D),
+                precision=lax.Precision.HIGHEST,
+            ),
+        ]
+    ).reshape(3, 3, D)
+    latent0 = (coef[0] * clean_latent + coef[1] * noise_draw).reshape(SEQ, PATCH_CH)
+    shaped, proj, packed, loss_part = whole_step(
+        coef,
+        jnp.tile(latent0, (1, 8)),
+        mods,
+        positions(),
+        (teacher_embed, teacher_final),
+        (student_embed, student_final),
+        teacher_qkv,
+        teacher_out,
+        student_qkv,
+        student_out,
+    )
+    grads, totals = reduce_gradients(shaped, proj, packed, loss_part)
     grad_qkv = jnp.moveaxis(grads[:3], 0, 1)
     grad_out = grads[3]
     squares, loss_sum = totals[0, 0], totals[1, 0]

time: 328 us -> 212 us (0.65); the launches traced: 323 us -> 211 us
  Pallas kernels: 77.2 us -> 186 us
  waiting for transfers between devices: 82.3 us -> 0 us
  matrix products: 71.1 us -> 1.63 us
  local copies, waits for them, and re-layouts: 30.9 us -> 3.71 us
  starting transfers between devices: 19.9 us -> 0 us
  between operations: 24.1 us -> 4.9 us
  other arithmetic: 17.5 us -> 14.1 us
    pallas_call x0 -> x1, Pallas kernels: none -> 111 us  [whole_step(): pl.pallas_call(step_kernel, out_shape=(jax.ShapeDtypeStruct((32, 2, 32, T...]
    ppermute x5 -> x0, waiting for transfers between devices: 82.2 us -> none  [swapped(): return lax.ppermute(values, 'mp', [(0, 1), (1, 0)])]
    dot_general x30 -> x3, matrix products: 66.2 us -> 1.63 us  [the longest x1 1.15 us: per_device(): jnp.dot(one_hot_rows(timestep - 1, K), student_mod.reshape(K, 3 * D), pre...]
    ppermute x5 -> x0, starting transfers between devices: 19.9 us -> none  [swapped(): return lax.ppermute(values, 'mp', [(0, 1), (1, 0)])]
    unnamed x81 -> x25, local copies, waits for them, and re-layouts: 14 us -> 0.51 us
    sub x3 -> x0, matrix products: 4.88 us -> none  [front(): expos = jnp.exp(scores - highest)]
    dynamic_slice x2 -> x0, local copies, waits for them, and re-layouts: 3.43 us -> none  [split(): other = lax.dynamic_index_in_dim(rows, 1 - core, 1, keepdims=False)]
  transfers between devices with their start and end apart: 6 -> 0, of which waited for: 4 -> 0; matrix products, arithmetic and copies ran while one was open for 20% -> 0% of each run, Pallas kernels for 0% -> 0%
where the time goes in v3:
time: 212 us; the launch traced here: 211 us
  Pallas kernels  186 us (88%)
  other arithmetic  14.1 us (7%)
  between operations  4.9 us (2%)
  local copies, waits for them, and re-layouts  3.71 us (2%)
    pallas_call x1, Pallas kernels, whole_step(): pl.pallas_call(step_kernel, out_shape=(jax.ShapeDtypeStruct((32, 2, 32, T...  111 us
    pallas_call x1, Pallas kernels, reduce_gradients(): pl.pallas_call(reduce_kernel, out_shape=(jax.ShapeDtypeStruct((4, 32, 512...  75.3 us

profile of v3, /device:TPU:1, one launch (start us, length us, event | category | flops | bytes accessed | tf_op | source)
XLA Modules:
  0.0 210.6 jit_solution(5371462094433137597)
XLA Ops:
  2.0 0.1 pad_add_fusion
  2.1 0.1 pad_add_fusion.1
  2.1 1.3 fusion.27
  3.4 0.2 fusion.17
  3.6 0.1 reshape.265
  3.7 1.2 pad_maximum_fusion.4.coef
  5.0 0.6 fusion.38
  5.6 2.1 add_reduce_fusion
  7.6 1.1 fusion.4
  8.8 0.3 fusion
  9.2 0.7 pad_maximum_fusion.3.mods
  9.8 0.1 tile.70
  10.0 0.8 copy.39.latent8
  10.8 0.9 reduce-precision_convert_fusion.5
  11.7 0.5 multiply_sine_fusion
  12.7 0.4 copy-done.3
  13.4 1.9 pad_maximum_fusion.1
  15.3 0.3 multiply_add_fusion
  15.6 1.5 pad_maximum_fusion.placed
  17.1 111.0 %shard_map.234 = (bf16[32,2,32,256]{3,2,1,0:T(8,128)(2,1)}, bf16[32,2,32,256]{3,2,1,0:T(8,128)(2,1)}, bf16[256,2048]{1,0:T(8,128)(2,1)}, f32[8,128]{1,0:T(8,128)}) custom-call(f32[8]{0:T(128)} %pad_maximum_fusion.4.coef, f32[256,128]{1,0:T(8,128)} %copy.39.latent8, f32[3,3,2048]{2,1,0:T(4,128)} %pad_maximum_fusion.3.mods, ...), custom_call_target="tpu_custom_call" | custom-call | tf_op jit(solution)/shard_map/pallas_call | solution.py:661
  128.1 75.3 %shard_map.235 = (f32[4,32,512]{2,1,0:T(8,128)}, f32[8,128]{1,0:T(8,128)}) custom-call(bf16[32,2,32,256]{3,2,1,0:T(8,128)(2,1)} %get-tuple-element.13.shaped, bf16[32,2,32,256]{3,2,1,0:T(8,128)(2,1)} %get-tuple-element.14.proj, bf16[256,2048]{1,0:T(8,128)(2,1)} %get-tuple-element.15.packed, f32[8,128]{1,0:T(8,128)} %get-tuple-element.16.loss_part), custom_call_target="tpu_custom_call" | custom-call | tf_op jit(solution)/shard_map/pallas_call | solution.py:251
  203.5 1.3 fusion.37
  206.1 1.5 add_divide_fusion.1
  207.7 1.8 add_divide_fusion
  (54 shorter events, 0.8 us)
Async XLA Ops:
  0.6 8.2 %copy-start = (f32[16,3,2048]{2,0,1:T(8,128)S(1)}, f32[16,3,2048]{2,0,1:T(8,128)}, u32[]{:S(2)}) copy-start(f32[16,3,2048]{2,0,1:T(8,128)} %param.26) | copy-start | bytes 1179652
  3.6 8.8 %copy-start.1 = (f32[16,2048]{1,0:T(8,128)S(1)}, f32[16,2048]{1,0:T(8,128)}, u32[]{:S(2)}) copy-start(f32[16,2048]{1,0:T(8,128)} %param.24) | copy-start | bytes 393220
  9.9 2.6 %copy-start.2 = (f32[16,2048]{1,0:T(8,128)S(1)}, f32[16,2048]{1,0:T(8,128)}, u32[]{:S(2)}) copy-start(f32[16,2048]{1,0:T(8,128)} %param.29) | copy-start | bytes 393220
  12.2 0.9 copy-start.3
  12.6 0.9 copy-start.4
  13.3 2.1 copy-start.5
  13.3 2.1 copy-start.6
  128.1 78.0 %copy-start.9 = (f32[32,512]{1,0:T(8,128)S(1)}, f32[32,512]{1,0:T(8,128)}, u32[]{:S(2)}) copy-start(f32[32,512]{1,0:T(8,128)} %param.37) | copy-start | bytes 196612
  128.1 78.0 %copy-start.10 = (f32[32,512]{1,0:T(8,128)S(1)}, f32[32,512]{1,0:T(8,128)}, u32[]{:S(2)}) copy-start(f32[32,512]{1,0:T(8,128)} %param.36) | copy-start | bytes 196612
  128.1 79.5 %copy-start.7 = (f32[32,3,512]{2,0,1:T(8,128)S(1)}, f32[32,3,512]{2,0,1:T(8,128)}, u32[]{:S(2)}) copy-start(f32[32,3,512]{2,0,1:T(8,128)} %param.35) | copy-start | bytes 589828
  128.1 79.5 %copy-start.8 = (f32[32,3,512]{2,0,1:T(8,128)S(1)}, f32[32,3,512]{2,0,1:T(8,128)}, u32[]{:S(2)}) copy-start(f32[32,3,512]{2,0,1:T(8,128)} %param.34) | copy-start | bytes 589828

commit v4 on v3

--- a/solution.py
+++ b/solution.py
@@ -2,6 +2,7 @@
 
 import jax
 import jax.numpy as jnp
+import numpy as np
 from jax import lax
 from jax.experimental import pallas as pl
 from jax.experimental.pallas import tpu as pltpu
@@ -14,6 +15,7 @@
 PATCH_CH = 16
 SEQ = 256
 LATENT = 4096
+SAMPLES = 64
 K = 8
 TGRID = 16
 NBUCKET = 8
@@ -287,6 +289,7 @@
 
 
 TOKENS = 256
+UNROLL = 4
 WIDE = 256
 NT = (((1,), (1,)), ((), ()))
 TN = (((0,), (0,)), ((), ()))
@@ -333,6 +336,9 @@
                 else:
                     spot = (every, back) if axis == "dp_1" else (back, every)
                 go((*spot, side, core, half), base + 4 * half + 2 + side, axis, near[axis][side])
+
+    def across(k, spot):
+        go((*spot[:3], core, spot[3]), k, "dp_3", 1 - core)
 
     def step(k):
         if k == 0:
@@ -348,10 +354,56 @@
             ring_direct(False)
         elif k == 4:
             ring_relay(False)
+            relays.extend(live[-4:])
+            across(17, (y, every, every, 0))
+            across(18, (every, x, every, 1))
+            for n in range(2):
+                across(19 + 2 * n, (near["dp_0"][n], every, every, 0))
+                across(20 + 2 * n, (every, near["dp_1"][n], every, 1))
         elif k == 5:
-            for c in live[-4:]:
+            for c in relays:
                 c.wait_recv()
-            go((every, every, every, core), 17, "dp_3", 1 - core)
+            across(23, (lax.rem(y + 2, 4), every, every, 0))
+            across(24, (every, lax.rem(x + 2, 4), every, 1))
+        else:
+            for c in live[-8:]:
+                c.wait_recv()
+            for c in live:
+                c.wait_send()
+
+    relays = []
+    return step
+
+
+def gather_direct(held, slab, send, recv):
+    y, x, z, core = (lax.axis_index(a) for a in AXES[:4])
+    every = slice(None)
+    live = []
+
+    def ring(spots, base):
+        for half, (axis, spot) in enumerate(spots):
+            me = lax.axis_index(axis)
+            for k in (1, 2, 3):
+                ref = held.at[(slab, *spot, core, half)]
+                n = base + 3 * half + k - 1
+                c = remote(ref, ref, send.at[n], recv.at[n], axis, lax.rem(me + k, 4))
+                c.start()
+                live.append(c)
+
+    def step(k):
+        if k == 0:
+            ring([("dp_1", (y, x, every)), ("dp_0", (y, x, every))], 0)
+        elif k == 1:
+            for c in live:
+                c.wait_recv()
+            ring([("dp_0", (y, every, every)), ("dp_1", (every, x, every))], 6)
+        elif k == 2:
+            for c in live[6:]:
+                c.wait_recv()
+            ref = held.at[slab, :, :, :, core]
+            c = remote(ref, ref, send.at[12], recv.at[12], "dp_3", 1 - core)
+            c.start()
+            live.append(c)
         else:
             live[-1].wait_recv()
             for c in live:
@@ -374,16 +426,26 @@
     return picked.astype(jnp.bfloat16)
 
 
+def picked_level(step, offset, values):
+    out = jnp.float32(0.0)
+    for k in range(1, K + 1):
+        out = jnp.where(step == k, jnp.float32(values[2 * k + offset]), out)
+    return out
+
+
 def step_kernel(
-    coef,
-    latent8,
-    mods,
-    placed,
+    timestep,
+    bucket,
+    bucket_weights,
+    clean8,
+    noise8,
+    tables,
     teacher_embed,
     teacher_final,
+    teacher_mod,
     student_embed,
     student_final,
-    student_back,
+    student_mod,
     teacher_qkv,
     teacher_out,
     student_qkv,
@@ -394,6 +456,7 @@
     loss_part,
     held,
     near_qkv,
+    placed,
     hidden,
     hidden_s,
     mixed,
@@ -406,6 +469,11 @@
     terms,
     inverses,
     d_attn,
+    embed_t,
+    embed_s,
+    back_s,
+    final_t,
+    final_s,
     qkv_sem,
     swap_send,
     swap_recv,
@@ -419,23 +487,54 @@
     load.start()
     held[0:3, y, x, z, core] = student_qkv[...]
     held[3, y, x, z, core] = student_out[...]
-    friends = [("dp_3", 1 - core), ("dp_2", 1 - z), ("mp", 1 - mp)]
-    friends += [("dp_1", lax.rem(x + k, 4)) for k in (1, 3)]
-    friends += [("dp_0", lax.rem(y + k, 4)) for k in (1, 3)]
+    both = ("dp_2", "mp")
+    friends = [("dp_3", 1 - core), ("dp_2", 1 - z), ("mp", 1 - mp), (both, (1 - z, 1 - mp))]
+    friends += [("dp_1", lax.rem(x + k, 4)) for k in (1, 2, 3)]
+    friends += [("dp_0", lax.rem(y + k, 4)) for k in (1, 2, 3)]
     greet(friends)
 
-    def swap(src, dst, k):
-        c = remote(src, dst, swap_send.at[k], swap_recv.at[k], "mp", 1 - mp)
+    def swap(src, dst, k, axis="mp", target=None):
+        target = 1 - mp if target is None else target
+        return remote(src, dst, swap_send.at[k], swap_recv.at[k], axis, target)
+
+    spot = (y, x, z, core)
+    here = teacher_out.at[spot]
+    swaps = [
+        swap(here, held.at[(5, *spot)], 0),
+        swap(here, held.at[(5, *spot)], 1, both, (1 - z, 1 - mp)),
+        swap(student_out, held.at[(4, *spot)], 2),
+    ]
+    for c in swaps:
         c.start()
-        return c
-
-    spot = (y, x, z, core)
-    swaps = [
-        swap(teacher_out.at[spot], held.at[(5, *spot)], 0),
-        swap(student_out, held.at[(4, *spot)], 1),
+    t_step = gather_direct(held, 5, t_send, t_recv)
+    s_step = gather_stream(held, pl.ds(0, 5), s_send, s_recv)
+
+    step = timestep[0]
+    a_f, a_m, a_l = (picked_level(step, -k, ALPHAS) for k in range(3))
+    s_f, s_m, s_l = (picked_level(step, -k, SIGMAS) for k in range(3))
+    row_weight = bucket_weights[jnp.clip(bucket[0], 0, NBUCKET - 1)]
+    places = [
+        (teacher_mod, jnp.clip(2 * step - 1, 0, TGRID - 1)),
+        (teacher_mod, jnp.clip(2 * step - 2, 0, TGRID - 1)),
+        (student_mod, jnp.clip(step - 1, 0, K - 1)),
     ]
-    t_step = gather_stream(held, pl.ds(5, 1), t_send, t_recv)
-    s_step = gather_stream(held, pl.ds(0, 5), s_send, s_recv)
+    modrows = [[mod[j, pl.ds(at, 1), :] for j in range(3)] for mod, at in places]
+
+    def split_rows(ref):
+        v = ref[...]
+        h = v.astype(jnp.bfloat16)
+        rest = v - h.astype(jnp.float32)
+        m = rest.astype(jnp.bfloat16)
+        return h, m, (rest - m.astype(jnp.float32)).astype(jnp.bfloat16)
+
+    def stack(parts, out):
+        h, m, l = parts
+        for k, v in enumerate([h, m, h, l, h, m, jnp.zeros_like(h), jnp.zeros_like(h)]):
+            out[16 * k : 16 * k + 16] = v
+
+    def repeat(parts, out):
+        for k in range(24):
+            out[16 * k : 16 * k + 16] = parts[k // 8]
 
     def columns(k, width):
         return pl.ds(pl.multiple_of(k * width, width), width)
@@ -451,17 +550,26 @@
 
         lax.fori_loop(0, D // WIDE, body, 0)
 
+    def centred(v):
+        c = v - jnp.mean(v, axis=-1, keepdims=True)
+        return c, lax.rsqrt(jnp.mean(c * c, axis=-1, keepdims=True) + LN_EPS)
+
+    def by_rows(body):
+        def group(n, carry):
+            for u in range(UNROLL):
+                body(pl.ds(pl.multiple_of(n * (16 * UNROLL) + 16 * u, 16), 16))
+            return carry
+
+        lax.fori_loop(0, TOKENS // (16 * UNROLL), group, 0)
+
     def shape(hid, which, out):
-        def body(n, carry):
-            rows = columns(n, 16)
-            v = hid[rows]
-            c = v - jnp.mean(v, axis=-1, keepdims=True)
-            inv = lax.rsqrt(jnp.mean(c * c, axis=-1, keepdims=True) + LN_EPS)
-            s = c * inv * (1.0 + mods[which, 1:2]) + mods[which, 0:1]
-            out[rows] = s.astype(jnp.bfloat16)
-            return carry
-
-        lax.fori_loop(0, TOKENS // 16, body, 0)
+        shift, scale = modrows[which][0], 1.0 + modrows[which][1]
+
+        def body(rows):
+            c, inv = centred(hid[rows])
+            out[rows] = (c * inv * scale + shift).astype(jnp.bfloat16)
+
+        by_rows(body)
 
     def project(src, weight):
         def body(j, carry):
@@ -475,9 +583,13 @@
     sides = [low_f.astype(jnp.bfloat16), (1.0 - low_f).astype(jnp.bfloat16)]
     is_low = lax.broadcasted_iota(jnp.int32, (TOKENS, 128), 1) < 64
 
-    def attend(out, keep):
-        def body(hp, carry):
-            cols = columns(hp, 128)
+    def swap_pair(which, hp):
+        cols = pl.ds(128 * hp, 128)
+        return swap(heads.at[which, :, cols], heads_in.at[which, :, cols], 3 + 4 * which + hp)
+
+    def attend(which, keep):
+        for hp in range(4):
+            cols = pl.ds(128 * hp, 128)
             q, k, v = qkv[0, :, cols], qkv[1, :, cols], qkv[2, :, cols]
             outs = []
             for h in range(2):
@@ -487,29 +599,32 @@
                 if keep:
                     weights[2 * hp + h] = w
                 outs.append(dot(w.astype(jnp.bfloat16), v))
-            out[:, cols] = jnp.where(is_low, outs[0], outs[1]).astype(jnp.bfloat16)
-            return carry
-
-        lax.fori_loop(0, 4, body, 0)
+            heads[which, :, cols] = jnp.where(is_low, outs[0], outs[1]).astype(jnp.bfloat16)
+            if hp > 0:
+                swap_pair(which, hp - 1).start()
+        swap_pair(which, 3).start()
+
+    def swapped(which):
+        for hp in range(4):
+            swap_pair(which, hp).wait_recv()
 
     def mix(att, weight, which, base):
+        mod_ref, at = places[which]
+
         def body(n, carry):
             cols = columns(n, 512)
             p = dot(att[...], weight(n), NT)
-            mixed[:, cols] = base[:, cols] + mods[which, 2:3, cols] * p
+            mixed[:, cols] = base[:, cols] + mod_ref[2, pl.ds(at, 1), cols] * p
             return carry
 
         lax.fori_loop(0, 4, body, 0)
 
     def predict(final, keep):
-        def body(n, carry):
-            rows = columns(n, 16)
-            v = mixed[rows]
-            c = v - jnp.mean(v, axis=-1, keepdims=True)
-            inv = lax.rsqrt(jnp.mean(c * c, axis=-1, keepdims=True) + LN_EPS)
+        def body(rows):
+            c, inv = centred(mixed[rows])
             u = c * inv
             if keep:
-                mixed[rows] = u
+                placed[rows] = u
                 inverses[rows] = jnp.broadcast_to(inv, (16, 128))
             high = u.astype(jnp.bfloat16)
             rest = u - high.astype(jnp.float32)
@@ -517,9 +632,8 @@
             terms[0, rows] = high
             terms[1, rows] = middle
             terms[2, rows] = (rest - middle.astype(jnp.float32)).astype(jnp.bfloat16)
-            return carry
-
-        lax.fori_loop(0, TOKENS // 16, body, 0)
+
+        by_rows(body)
         r = dot(terms[0], final[...], NT)
         m = dot(terms[1], final[0:256], NT)
         small = dot(terms[2], final[0:128], NT)
@@ -532,50 +646,8 @@
     def other_rows(slab):
         return lambda n: held[slab, n].reshape(512, 512)
 
-    a_f, s_f, a_m, s_m, a_l, s_l, row_weight = (coef[k] for k in range(7))
-
-    lat0 = latent8[...]
-    spread(lat0, teacher_embed, hidden, placed)
-    shape(hidden, 0, shaped)
-    for c in swaps:
-        c.wait_recv()
-    t_step(0)
-    s_step(0)
-    load.wait()
-    project(shaped, lambda j: near_qkv[j])
-    t_step(1)
-    attend(heads.at[0], False)
-    swaps.append(swap(heads.at[0], heads_in.at[0], 2))
-    t_step(2)
-    spread(lat0, student_embed, hidden_s, placed)
-    t_step(3)
-    s_step(1)
-    shape(hidden_s, 2, shaped_s)
-    t_step(4)
-    s_step(2)
-    mix(heads.at[0], lambda n: teacher_out[n].reshape(512, 512), 0, hidden)
-    t_step(5)
-    s_step(3)
-    t_step(6)
-    swaps[2].wait_recv()
-    mix(heads_in.at[0], other_rows(5), 0, mixed)
-    eps0 = predict(teacher_final, False)
-    lat1 = a_m * (lat0 - s_f * eps0) / a_f + s_m * eps0
-
-    spread(lat1, teacher_embed, hidden, placed)
-    shape(hidden, 1, shaped)
-    project(shaped, lambda j: near_qkv[j])
-    attend(heads.at[1], False)
-    swaps.append(swap(heads.at[1], heads_in.at[1], 3))
-    s_step(4)
-    mix(heads.at[1], lambda n: teacher_out[n].reshape(512, 512), 1, hidden)
-    swaps[3].wait_recv()
-    mix(heads_in.at[1], other_rows(5), 1, mixed)
-    eps1 = predict(teacher_final, False)
-    lat2 = a_l * (lat1 - s_m * eps1) / a_m + s_l * eps1
-    target = (lat0 - a_f / a_l * lat2) / (s_f - a_f * s_l / a_l)
-
-    s_step(5)
+    def near_rows(n):
+        return teacher_out[n].reshape(512, 512)
 
     def turn(src, out):
         def body(n, carry):
@@ -585,32 +657,81 @@
 
         lax.fori_loop(0, D // 128, body, 0)
 
+    half = D // 2
+    for k in range(16):
+        sin_a, cos_a = tables[0, k : k + 1], tables[1, k : k + 1]
+        rows = pl.ds(16 * k, 16)
+        placed[rows, :half] = sin_a * tables[3] + cos_a * tables[2]
+        placed[rows, half:] = cos_a * tables[3] - sin_a * tables[2]
+    stack(split_rows(teacher_embed), embed_t)
+    lat0 = a_f * clean8[...] + s_f * noise8[...]
+    spread(lat0, embed_t, hidden, placed)
+    swaps[0].wait_recv()
+    swaps[1].wait_recv()
+    t_step(0)
+    swaps[2].wait_recv()
+    s_step(0)
+    shape(hidden, 0, shaped)
+    load.wait()
+    project(shaped, lambda j: near_qkv[j])
+    t_step(1)
+    s_step(1)
+    attend(0, False)
+    t_step(2)
+    s_step(2)
+    mix(heads.at[0], near_rows, 0, hidden)
+    stack(split_rows(student_embed), embed_s)
+    repeat(split_rows(teacher_final), final_t)
+    spread(lat0, embed_s, hidden_s, placed)
+    t_step(3)
+    s_step(3)
+    swapped(0)
+    mix(heads_in.at[0], other_rows(5), 0, mixed)
+    eps0 = predict(final_t, False)
+    lat1 = a_m * (lat0 - s_f * eps0) / a_f + s_m * eps0
+
+    spread(lat1, embed_t, hidden, placed)
+    shape(hidden, 1, shaped)
+    project(shaped, lambda j: near_qkv[j])
+    attend(1, False)
+    mix(heads.at[1], near_rows, 1, hidden)
+    shape(hidden_s, 2, shaped_s)
+    s_step(4)
+    swapped(1)
+    mix(heads_in.at[1], other_rows(5), 1, mixed)
+    eps1 = predict(final_t, False)
+    lat2 = a_l * (lat1 - s_m * eps1) / a_m + s_l * eps1
+    target = (lat0 - a_f / a_l * lat2) / (s_f - a_f * s_l / a_l)
+
+    s_step(5)
     turn(shaped_s, shaped_t)
+    student_terms = split_rows(student_final)
+    repeat(student_terms, final_s)
+    stack(student_terms, back_s)
     s_step(6)
     project(shaped_s, lambda j: held[j].reshape(D, 512))
-    attend(heads.at[2], True)
-    swaps.append(swap(heads.at[2], heads_in.at[2], 4))
+    attend(2, True)
     mix(heads.at[2], other_rows(3), 2, hidden_s)
-    swaps[4].wait_recv()
+    swapped(2)
     mix(heads_in.at[2], other_rows(4), 2, mixed)
-    error = predict(student_final, True) - target
+    error = predict(final_s, True) - target
     lanes = lax.broadcasted_iota(jnp.int32, error.shape, 1)
     loss_part[...] = jnp.full(
         (8, 128), 0.5 * row_weight * jnp.sum(jnp.where(lanes < 16, error * error, 0.0))
     )
 
-    spread(2.0 * row_weight * error, student_back, hidden)
-
-    def back(n, carry):
-        rows = columns(n, 16)
-        up, u = hidden[rows], mixed[rows]
+    spread(2.0 * row_weight * error, back_s, hidden)
+
+    gate = modrows[2][2]
+
+    def back(rows):
+        up, u = hidden[rows], placed[rows]
         first_mean = jnp.mean(up, axis=-1, keepdims=True)
         second_mean = jnp.mean(up * u, axis=-1, keepdims=True)
         d = (up - first_mean - u * second_mean) * inverses[rows, 0:1]
-        shaped[rows] = (mods[2, 2:3] * d).astype(jnp.bfloat16)
-        return carry
-
-    lax.fori_loop(0, TOKENS // 16, back, 0)
+        shaped[rows] = (gate * d).astype(jnp.bfloat16)
+
+    by_rows(back)
     d_attn[...] = dot(shaped[...], held[3].reshape(D, 512)).astype(jnp.bfloat16)
 
     def back_heads(hp, carry):
@@ -634,30 +755,34 @@
     turn(shaped, proj_t)
     for c in swaps:
         c.wait_send()
-
-
-def three_parts(values):
-    high = lax.reduce_precision(values, 8, 7)
-    rest = values - high
-    middle = lax.reduce_precision(rest, 8, 7)
-    return high, middle, rest - middle
-
-
-def stacked(values):
-    h, m, l = three_parts(values)
-    zero = jnp.zeros_like(h)
-    return jnp.concatenate([h, m, h, l, h, m, zero, zero], axis=0).astype(jnp.bfloat16)
-
-
-def repeated(values):
-    return jnp.concatenate([jnp.tile(t, (8, 1)) for t in three_parts(values)], axis=0).astype(
-        jnp.bfloat16
-    )
-
-
-def whole_step(coef, latent8, mods, placed, teacher, student, qkv_t, out_t, qkv_s, out_s):
-    vmem = pl.BlockSpec(memory_space=pltpu.VMEM)
+    for which in range(3):
+        for hp in range(4):
+            swap_pair(which, hp).wait_send()
+
+
+def levels():
+    lamb = 6.0 - 12.0 * np.arange(TGRID + 1) / TGRID
+    return [np.sqrt(1.0 / (1.0 + np.exp(sign * lamb))).astype(np.float32) for sign in (-1.0, 1.0)]
+
+
+ALPHAS, SIGMAS = levels()
+
+
+def position_tables():
+    half = D // 2
+    freqs = np.exp(-math.log(10000.0) * np.arange(half) / half)
+    fine = np.arange(16)[:, None] * freqs[None]
+    angles = (np.sin(16.0 * fine), np.cos(16.0 * fine), np.sin(fine), np.cos(fine))
+    return np.stack(angles).astype(np.float32)
+
+
+def whole_step(timestep, bucket, bucket_weights, clean, noise, teacher, student):
+    vmem, smem = (pl.BlockSpec(memory_space=m) for m in (pltpu.VMEM, pltpu.SMEM))
     bf16, f32 = jnp.bfloat16, jnp.float32
+
+    def tiled(v):
+        return jnp.tile(v.reshape(SEQ, PATCH_CH), (1, 8))
+
     return pl.pallas_call(
         step_kernel,
         out_shape=(
@@ -666,14 +791,12 @@
             jax.ShapeDtypeStruct((TOKENS, D), bf16),
             jax.ShapeDtypeStruct((8, 128), f32),
         ),
-        in_specs=[pl.BlockSpec(memory_space=pltpu.SMEM)]
-        + [vmem] * 8
-        + [pl.BlockSpec(memory_space=pl.ANY)]
-        + [vmem] * 3,
+        in_specs=[smem] * 3 + [vmem] * 9 + [pl.BlockSpec(memory_space=pl.ANY)] + [vmem] * 3,
         out_specs=(vmem,) * 4,
         scratch_shapes=[
             pltpu.VMEM((6, 4, 4, 2, 2, 2, 16, 512), bf16),
             pltpu.VMEM((3, D, 512), bf16),
+            pltpu.VMEM((TOKENS, D), f32),
             pltpu.VMEM((TOKENS, D), f32),
             pltpu.VMEM((TOKENS, D), f32),
             pltpu.VMEM((TOKENS, D), f32),
@@ -686,53 +809,71 @@
             pltpu.VMEM((3, TOKENS, D), bf16),
             pltpu.VMEM((TOKENS, 128), f32),
             pltpu.VMEM((TOKENS, 512), bf16),
+            pltpu.VMEM((128, D), bf16),
+            pltpu.VMEM((128, D), bf16),
+            pltpu.VMEM((128, D), bf16),
+            pltpu.VMEM((384, D), bf16),
+            pltpu.VMEM((384, D), bf16),
             pltpu.SemaphoreType.DMA,
-            pltpu.SemaphoreType.DMA((5,)),
-            pltpu.SemaphoreType.DMA((5,)),
-            pltpu.SemaphoreType.DMA((18,)),
-            pltpu.SemaphoreType.DMA((18,)),
-            pltpu.SemaphoreType.DMA((18,)),
-            pltpu.SemaphoreType.DMA((18,)),
+            pltpu.SemaphoreType.DMA((15,)),
+            pltpu.SemaphoreType.DMA((15,)),
+            pltpu.SemaphoreType.DMA((13,)),
+            pltpu.SemaphoreType.DMA((13,)),
+            pltpu.SemaphoreType.DMA((25,)),
+            pltpu.SemaphoreType.DMA((25,)),
         ],
         compiler_params=pltpu.CompilerParams(
             collective_id=2, has_side_effects=True, vmem_limit_bytes=62 * 2**20
         ),
     )(
-        coef,
-        latent8,
-        mods,
-        placed,
-        stacked(teacher[0]),
-        repeated(teacher[1]),
-        stacked(student[0]),
-        repeated(student[1]),
-        stacked(student[1]),
-        jnp.moveaxis(qkv_t, 1, 0),
-        out_t.reshape(4, 4, 2, 2, 2, 16, 512),
-        jnp.moveaxis(qkv_s, 1, 0).reshape(3, 2, 16, 512),
-        out_s.reshape(2, 16, 512),
-    )
-
-
-def plan():
-    grid = jnp.arange(TGRID + 1, dtype=jnp.float32)
-    lamb = 6.0 - 12.0 * grid / TGRID
-    return (jnp.sqrt(jax.nn.sigmoid(lamb)), jnp.sqrt(jax.nn.sigmoid(-lamb)))
-
-
-def positions():
-    half = D // 2
-    freqs = jnp.exp(-math.log(10000.0) * jnp.arange(half, dtype=jnp.float32) / half)
-    steps = jnp.arange(16, dtype=jnp.float32)[:, None]
-    coarse, fine = 16.0 * steps * freqs[None], steps * freqs[None]
-    sin_a, cos_a = jnp.sin(coarse)[:, None], jnp.cos(coarse)[:, None]
-    sin_b, cos_b = jnp.sin(fine)[None], jnp.cos(fine)[None]
-    both = [sin_a * cos_b + cos_a * sin_b, cos_a * cos_b - sin_a * sin_b]
-    return jnp.concatenate(both, axis=2).reshape(SEQ, D)
-
-
-def one_hot_rows(index, width):
-    return (index[:, None] == jnp.arange(width, dtype=jnp.int32)[None, :]).astype(jnp.float32)
+        timestep,
+        bucket,
+        bucket_weights,
+        tiled(clean),
+        tiled(noise),
+        jnp.asarray(position_tables()),
+        teacher[0],
+        teacher[1],
+        jnp.moveaxis(teacher[2], 1, 0),
+        student[0],
+        student[1],
+        jnp.moveaxis(student[2], 1, 0),
+        jnp.moveaxis(teacher[3], 1, 0),
+        teacher[4].reshape(4, 4, 2, 2, 2, 16, 512),
+        jnp.moveaxis(student[3], 1, 0).reshape(3, 2, 16, 512),
+        student[4].reshape(2, 16, 512),
+    )
+
+
+def adam_kernel(grads, totals, mq, vq, mo, vo, new_mq, new_vq, up_q, new_mo, new_vo, up_o, loss):
+    rms = jnp.sqrt(totals[0:1, 0:1] / (4 * D * INNER))
+    factor = 1.0 / jnp.maximum(rms, 1.0)
+
+    def adam(grad, moment, second, new_moment, new_second, update):
+        normed = grad * factor
+        m = BETA_ONE * moment + (1.0 - BETA_ONE) * normed
+        v = BETA_TWO * second + (1.0 - BETA_TWO) * normed * normed
+        new_moment[...] = m
+        new_second[...] = v
+        update[...] = m / (jnp.sqrt(v) + ADAM_EPS)
+
+    for j in range(3):
+        adam(grads[j], mq[j], vq[j], new_mq.at[j], new_vq.at[j], up_q.at[j])
+    adam(grads[3], mo[...], vo[...], new_mo, new_vo, up_o)
+    loss[...] = totals[1:2, 0:1] / (SAMPLES * LATENT)
+
+
+def adam_update(grads, totals, moment_qkv, second_qkv, moment_out, second_out):
+    vmem = pl.BlockSpec(memory_space=pltpu.VMEM)
+    mq, vq = (jnp.moveaxis(v, 1, 0) for v in (moment_qkv, second_qkv))
+    qkv, out = (jax.ShapeDtypeStruct(v.shape, v.dtype) for v in (mq, moment_out))
+    *news, loss = pl.pallas_call(
+        adam_kernel,
+        out_shape=(qkv, qkv, qkv, out, out, out, jax.ShapeDtypeStruct((1, 1), jnp.float32)),
+        in_specs=[vmem] * 6,
+        out_specs=(vmem,) * 7,
+    )(grads, totals, mq, vq, moment_out, second_out)
+    return (*(jnp.moveaxis(v, 0, 1) for v in news[:3]), *news[3:], loss.reshape(()))
 
 
 def per_device(
@@ -756,57 +897,17 @@
     moment_out,
     second_out,
 ):
-    samples = clean_latent.shape[0]
-    alphas, sigmas = plan()
-    table = jnp.stack([alphas, sigmas], axis=1)
-    first = 2 * timestep
-    taus = jnp.concatenate([first, first - 1, first - 2])
-    picked = jnp.dot(one_hot_rows(taus, TGRID + 1), table, precision=lax.Precision.HIGHEST)
-    weight = jnp.dot(
-        one_hot_rows(bucket, NBUCKET), bucket_weights, precision=lax.Precision.HIGHEST
-    )
-    coef = jnp.concatenate([picked.reshape(-1), weight, jnp.zeros((1,), jnp.float32)])
-    steps = one_hot_rows(jnp.concatenate([first - 1, first - 2]), TGRID)
-    mods = jnp.concatenate(
-        [
-            jnp.dot(steps, teacher_mod.reshape(TGRID, 3 * D), precision=lax.Precision.HIGHEST),
-            jnp.dot(
-                one_hot_rows(timestep - 1, K),
-                student_mod.reshape(K, 3 * D),
-                precision=lax.Precision.HIGHEST,
-            ),
-        ]
-    ).reshape(3, 3, D)
-    latent0 = (coef[0] * clean_latent + coef[1] * noise_draw).reshape(SEQ, PATCH_CH)
     shaped, proj, packed, loss_part = whole_step(
-        coef,
-        jnp.tile(latent0, (1, 8)),
-        mods,
-        positions(),
-        (teacher_embed, teacher_final),
-        (student_embed, student_final),
-        teacher_qkv,
-        teacher_out,
-        student_qkv,
-        student_out,
+        timestep,
+        bucket,
+        bucket_weights,
+        clean_latent,
+        noise_draw,
+        (teacher_embed, teacher_final, teacher_mod, teacher_qkv, teacher_out),
+        (student_embed, student_final, student_mod, student_qkv, student_out),
     )
     grads, totals = reduce_gradients(shaped, proj, packed, loss_part)
-    grad_qkv = jnp.moveaxis(grads[:3], 0, 1)
-    grad_out = grads[3]
-    squares, loss_sum = totals[0, 0], totals[1, 0]
-    rms_value = jnp.sqrt(squares / (4 * D * INNER))
-    factor = 1.0 / jnp.maximum(rms_value, 1.0)
-
-    def adam(moment, second, grad):
-        normed_grad = grad * factor
-        new_moment = BETA_ONE * moment + (1.0 - BETA_ONE) * normed_grad
-        new_second = BETA_TWO * second + (1.0 - BETA_TWO) * normed_grad * normed_grad
-        return (new_moment, new_second, new_moment / (jnp.sqrt(new_second) + ADAM_EPS))
-
-    mq, vq, uq = adam(moment_qkv, second_qkv, grad_qkv)
-    mo, vo, uo = adam(moment_out, second_out, grad_out)
-    loss = loss_sum / (samples * lax.axis_size(DP) * LATENT)
-    return (mq, vq, uq, mo, vo, uo, loss)
+    return adam_update(grads, totals, moment_qkv, second_qkv, moment_out, second_out)
 
 
 def solution(mesh):

time: 212 us -> 169 us (0.80)
  Pallas kernels: 186 us -> 160 us
  other arithmetic: 14.1 us -> 2.81 us
  between operations: 4.9 us -> 1.98 us
    pallas_call x1, Pallas kernels: 111 us -> 83 us  [whole_step(): pl.pallas_call(step_kernel, out_shape=(jax.ShapeDtypeStruct((32, 2, 32, T...]
    concatenate x6 -> x0, other arithmetic: 5.43 us -> none  [the longest x1 1.88 us: repeated(): jnp.concatenate([jnp.tile(t, (8, 1)) for t in three_parts(values)], axis=0)]
    div x2 -> x0, other arithmetic: 3.32 us -> none  [adam(): new_moment / (jnp.sqrt(new_second) + ADAM_EPS)]
    unnamed x15 -> x2, other arithmetic: 0.23 us -> 2.81 us
    add x2 -> x0, other arithmetic: 2.38 us -> none  [the longest x1 2.08 us: per_device(): coef[0] * clean_latent + coef[1] * noise_draw]
where the time goes in v4:
time: 169 us; the launch traced here: 167 us
  Pallas kernels  160 us (95%)
  other arithmetic  2.81 us (2%)
  local copies, waits for them, and re-layouts  2.37 us (1%)
  between operations  1.98 us (1%)
    pallas_call x1, Pallas kernels, whole_step(): pl.pallas_call(step_kernel, out_shape=(jax.ShapeDtypeStruct((32, 2, 32, T...  83 us
    pallas_call x1, Pallas kernels, reduce_gradients(): pl.pallas_call(reduce_kernel, out_shape=(jax.ShapeDtypeStruct((4, 32, 512...  75 us

profile of v4, /device:TPU:1, one launch (start us, length us, event | category | flops | bytes accessed | tf_op | source)
XLA Modules:
  0.0 167.2 jit_solution(6206878097873397528)
XLA Ops:
  1.9 0.5 broadcast.10
  2.4 1.4 reduce.6
  3.8 1.4 reduce.7
  5.3 0.1 tile.23
  5.3 0.1 copy.28
  5.4 0.8 copy.30.noise8
  6.2 0.1 tile.20
  6.3 0.1 copy.27
  6.4 0.8 copy.29.clean8
  7.1 83.0 %shard_map.243 = (bf16[32,2,32,256]{3,2,1,0:T(8,128)(2,1)}, bf16[32,2,32,256]{3,2,1,0:T(8,128)(2,1)}, bf16[256,2048]{1,0:T(8,128)(2,1)}, f32[8,128]{1,0:T(8,128)}) custom-call(s32[1]{0:T(128)S(6)} %copy.31.timestep, s32[1]{0:T(128)S(6)} %copy.32.bucket, f32[8]{0:T(128)} %bucket_weights.1, f32[256,128]{1,0:T(8,128)} %copy.29.clean8, f32[256,128]{1,0:T(8,128)} %copy.30.noise8, ...), custom_call_target="tpu_custom_call" | custom-call | tf_op jit(solution)/shard_map/pallas_call | solution.py:786
  90.1 75.0 %shard_map.244 = (f32[4,32,512]{2,1,0:T(8,128)}, f32[8,128]{1,0:T(8,128)}) custom-call(bf16[32,2,32,256]{3,2,1,0:T(8,128)(2,1)} %get-tuple-element.20.shaped, bf16[32,2,32,256]{3,2,1,0:T(8,128)(2,1)} %get-tuple-element.21.proj, bf16[256,2048]{1,0:T(8,128)(2,1)} %get-tuple-element.22.packed, f32[8,128]{1,0:T(8,128)} %get-tuple-element.23.loss_part), custom_call_target="tpu_custom_call" | custom-call | tf_op jit(solution)/shard_map/pallas_call | solution.py:253
  165.1 2.1 %shard_map.245 = (f32[3,32,512]{2,1,0:T(8,128)}, f32[3,32,512]{2,1,0:T(8,128)}, f32[3,32,512]{2,1,0:T(8,128)}, f32[32,512]{1,0:T(8,128)}, f32[32,512]{1,0:T(8,128)}, /*index=5*/f32[32,512]{1,0:T(8,128)}, f32[1,1]{1,0:T(1,128)}) custom-call(f32[4,32,512]{2,1,0:T(8,128)} %get-tuple-element.24.grads, f32[8,128]{1,0:T(8,128)} %get-tuple-element.25.totals, ...), custom_call_target="tpu_custom_call" | custom-call | tf_op jit(solution)/shard_map/pallas_call | solution.py:870
  (2 shorter events, 0.0 us)

commit v5 on v4

--- a/solution.py
+++ b/solution.py
@@ -31,6 +31,7 @@
 
 ROWS = 1024
 HALF = 1024
+CODES = 32767.0
 AXES = ("dp_0", "dp_1", "dp_2", "dp_3", "mp")
 
 
@@ -59,9 +60,12 @@
 
 def all_places():
     y, x, z, core, mp = (lax.axis_index(a) for a in AXES)
+    axes, here = ("mp", "dp_2", "dp_3"), (mp, z, core)
+    cube = []
+    for k in range(1, 8):
+        cube.append((axes, tuple(1 - h if k >> n & 1 else h for n, h in enumerate(here))))
     return [
-        (core, [("dp_3", 1 - core)]),
-        (2 * mp + z, [("dp_2", 1 - z), ("mp", 1 - mp), (("dp_2", "mp"), (1 - z, 1 - mp))]),
+        (4 * mp + 2 * z + core, cube),
         (x, [("dp_1", lax.rem(x + k, 4)) for k in (1, 2, 3)]),
         (y, [("dp_0", lax.rem(y + k, 4)) for k in (1, 2, 3)]),
     ]
@@ -93,50 +97,72 @@
     return value
 
 
-def ring_start(axis, part, relay, direct, send, recv):
+def by_columns(body):
+    def step(n, carry):
+        body(pl.ds(pl.multiple_of(n * 256, 256), 256))
+        return carry
+
+    lax.fori_loop(0, HALF // 256, step, 0)
+
+
+def ring_reduce(axis, part, codes, scales, boxes, box_scales, send, recv):
     me = lax.axis_index(axis)
     right, left, far = (lax.rem(me + k, 4) for k in (1, 3, 2))
     half = part.shape[1] // 2
     top, low = pl.ds(0, half), pl.ds(half, half)
-    copies = [
-        remote(part.at[far, top], relay.at[0], send.at[0], recv.at[0], axis, right),
-        remote(part.at[far, low], relay.at[1], send.at[1], recv.at[1], axis, left),
-        remote(part.at[right, low], direct.at[0], send.at[2], recv.at[2], axis, right),
-        remote(part.at[left, top], direct.at[1], send.at[3], recv.at[3], axis, left),
-    ]
-    for c in copies:
-        c.start()
-    return copies
-
-
-def ring_relay(axis, copies, part, relay, passed, summed, send, recv):
-    me = lax.axis_index(axis)
-    right, left = (lax.rem(me + k, 4) for k in (1, 3))
-    half = part.shape[1] // 2
-    top, low = pl.ds(0, half), pl.ds(half, half)
-    copies[0].wait_recv()
-    passed[0] = relay[0] + part[right, top]
-    first = remote(passed.at[0], summed.at[0], send.at[4], recv.at[4], axis, right)
-    first.start()
-    copies[1].wait_recv()
-    passed[1] = relay[1] + part[left, low]
-    second = remote(passed.at[1], summed.at[1], send.at[5], recv.at[5], axis, left)
-    second.start()
-    return [first, second]
-
-
-def ring_finish(axis, copies, more, part, direct, summed):
-    me = lax.axis_index(axis)
-    half = part.shape[1] // 2
-    copies[3].wait_recv()
-    more[0].wait_recv()
-    upper = part[me, pl.ds(0, half)] + direct[1] + summed[0]
-    copies[2].wait_recv()
-    more[1].wait_recv()
-    lower = part[me, pl.ds(half, half)] + direct[0] + summed[1]
-    for c in [*copies, *more]:
-        c.wait_send()
-    return upper, lower
+
+    def decoded(k, cols):
+        return boxes[k, :, cols].astype(jnp.int32).astype(jnp.float32) * box_scales[k, :, cols]
+
+    def encode(k, value):
+        def body(cols):
+            v = value(cols)
+            peak = jnp.maximum(jnp.max(jnp.abs(v), axis=0, keepdims=True), 1e-30)
+            code = lax.round(v * (CODES / peak), lax.RoundingMethod.TO_NEAREST_EVEN)
+            codes[k, :, cols] = code.astype(jnp.int32).astype(jnp.int16)
+            scales[k, :, cols] = peak * (1.0 / CODES)
+
+        by_columns(body)
+
+    def message(k):
+        target = left if k % 2 else right
+        return [
+            remote(codes.at[k], boxes.at[k], send.at[k, 0], recv.at[k, 0], axis, target),
+            remote(scales.at[k], box_scales.at[k], send.at[k, 1], recv.at[k, 1], axis, target),
+        ]
+
+    def post(k, value):
+        encode(k, value)
+        for c in message(k):
+            c.start()
+
+    def arrived(*which):
+        for k in which:
+            for c in message(k):
+                c.wait_recv()
+
+    def start():
+        post(0, lambda cols: part[far, top, cols])
+        post(1, lambda cols: part[far, low, cols])
+        post(2, lambda cols: part[right, low, cols])
+        post(3, lambda cols: part[left, top, cols])
+
+    def relay():
+        arrived(0)
+        post(4, lambda cols: part[right, top, cols] + decoded(0, cols))
+        arrived(1)
+        post(5, lambda cols: part[left, low, cols] + decoded(1, cols))
+
+    def finish(store):
+        arrived(3, 4)
+        by_columns(lambda cols: store(0, cols, part[me, top, cols] + decoded(3, cols) + decoded(4, cols)))
+        arrived(2, 5)
+        by_columns(lambda cols: store(1, cols, part[me, low, cols] + decoded(2, cols) + decoded(5, cols)))
+        for k in range(6):
+            for c in message(k):
+                c.wait_send()
+
+    return start, relay, finish
 
 
 def reduce_kernel(
@@ -155,7 +181,7 @@
     part_d,
     *rest,
 ):
-    boxes_a, boxes_b, boxes_c, boxes_d = rest[0:4], rest[4:8], rest[8:12], rest[12:16]
+    boxes = [rest[4 * k : 4 * k + 4] for k in range(4)]
     last, last_in, pair_send, pair_recv, send, recv, z_send, z_recv = rest[16:24]
     inbox, sum_send, sum_recv = rest[24:]
     y, x, z, core = (lax.axis_index(a) for a in AXES[:4])
@@ -191,40 +217,37 @@
         c.wait_recv()
     products(shaped_in, proj_in, packed_in, True)
 
-    first_a = ring_start("dp_1", part_a, boxes_a[0], boxes_a[1], send.at[0], recv.at[0])
-    first_b = ring_start("dp_0", part_b, boxes_b[0], boxes_b[1], send.at[1], recv.at[1])
-    more_a = ring_relay(
-        "dp_1", first_a, part_a, boxes_a[0], boxes_a[2], boxes_a[3], send.at[0], recv.at[0]
-    )
-    more_b = ring_relay(
-        "dp_0", first_b, part_b, boxes_b[0], boxes_b[2], boxes_b[3], send.at[1], recv.at[1]
-    )
-    upper, lower = ring_finish("dp_1", first_a, more_a, part_a, boxes_a[1], boxes_a[3])
+    rings = [
+        ring_reduce(axis, part, *boxes[k], send.at[k], recv.at[k])
+        for k, (axis, part) in enumerate(
+            [("dp_1", part_a), ("dp_0", part_b), ("dp_0", part_c), ("dp_1", part_d)]
+        )
+    ]
+
+    def into(part):
+        def store(which, cols, value):
+            part[2 * which, :, cols] = value[:64]
+            part[2 * which + 1, :, cols] = value[64:]
+
+        return store
+
+    rings[0][0]()
+    rings[1][0]()
+    rings[0][1]()
+    rings[1][1]()
+    rings[0][2](into(part_c))
+    rings[2][0]()
+    rings[1][2](into(part_d))
+    rings[3][0]()
+    rings[2][1]()
+    rings[3][1]()
+    z_copies = []
     for k in range(2):
-        part_c[k] = upper[64 * k : 64 * k + 64]
-        part_c[2 + k] = lower[64 * k : 64 * k + 64]
-    first_c = ring_start("dp_0", part_c, boxes_c[0], boxes_c[1], send.at[2], recv.at[2])
-    upper, lower = ring_finish("dp_0", first_b, more_b, part_b, boxes_b[1], boxes_b[3])
-    for k in range(2):
-        part_d[k] = upper[64 * k : 64 * k + 64]
-        part_d[2 + k] = lower[64 * k : 64 * k + 64]
-    first_d = ring_start("dp_1", part_d, boxes_d[0], boxes_d[1], send.at[3], recv.at[3])
-    more_c = ring_relay(
-        "dp_0", first_c, part_c, boxes_c[0], boxes_c[2], boxes_c[3], send.at[2], recv.at[2]
-    )
-    more_d = ring_relay(
-        "dp_1", first_d, part_d, boxes_d[0], boxes_d[2], boxes_d[3], send.at[3], recv.at[3]
-    )
-    z_copies = []
-    for k, (axis, first, more, part, boxes) in enumerate(
-        [
-            ("dp_0", first_c, more_c, part_c, boxes_c),
-            ("dp_1", first_d, more_d, part_d, boxes_d),
-        ]
-    ):
-        upper, lower = ring_finish(axis, first, more, part, boxes[1], boxes[3])
-        last[k, 0] = upper
-        last[k, 1] = lower
+
+        def store(which, cols, value, k=k):
+            last[k, which, :, cols] = value
+
+        rings[2 + k][2](store)
         c = remote(
             last.at[k, 1 - z], last_in.at[k], z_send.at[k], z_recv.at[k], "dp_2", 1 - z
         )
@@ -245,10 +268,9 @@
 
 def reduce_gradients(shaped, proj, packed, loss_part):
     vmem = pl.BlockSpec(memory_space=pltpu.VMEM)
-    wire = jnp.float32
 
     def boxes(half):
-        return [pltpu.VMEM((2, half, HALF), wire)] * 4
+        return [pltpu.VMEM((6, half, HALF), jnp.int16), pltpu.VMEM((6, 1, HALF), jnp.float32)] * 2
 
     return pl.pallas_call(
         reduce_kernel,
@@ -274,13 +296,13 @@
             pltpu.VMEM((2, 32, HALF), jnp.float32),
             pltpu.SemaphoreType.DMA((3,)),
             pltpu.SemaphoreType.DMA((3,)),
-            pltpu.SemaphoreType.DMA((4, 6)),
-            pltpu.SemaphoreType.DMA((4, 6)),
+            pltpu.SemaphoreType.DMA((4, 6, 2)),
+            pltpu.SemaphoreType.DMA((4, 6, 2)),
             pltpu.SemaphoreType.DMA((2,)),
             pltpu.SemaphoreType.DMA((2,)),
-            pltpu.VMEM((4, 4, 8, 128), jnp.float32),
-            pltpu.SemaphoreType.DMA((4, 3)),
-            pltpu.SemaphoreType.DMA((4, 3)),
+            pltpu.VMEM((3, 8, 8, 128), jnp.float32),
+            pltpu.SemaphoreType.DMA((3, 7)),
+            pltpu.SemaphoreType.DMA((3, 7)),
         ],
         compiler_params=pltpu.CompilerParams(
             collective_id=1, has_side_effects=True, vmem_limit_bytes=60 * 2**20

time: 169 us -> 150 us (0.89)
  Pallas kernels: 160 us -> 142 us
    pallas_call x1, Pallas kernels: 75 us -> 56.6 us  [reduce_gradients(): pl.pallas_call(reduce_kernel, out_shape=(jax.ShapeDtypeStruct((4, 32, 512...]
where the time goes in v5:
time: 150 us; the launch traced here: 149 us
  Pallas kernels  142 us (95%)
  other arithmetic  2.81 us (2%)
  local copies, waits for them, and re-layouts  2.37 us (2%)
  between operations  1.98 us (1%)
    pallas_call x1, Pallas kernels, whole_step(): pl.pallas_call(step_kernel, out_shape=(jax.ShapeDtypeStruct((32, 2, 32, T...  83 us
    pallas_call x1, Pallas kernels, reduce_gradients(): pl.pallas_call(reduce_kernel, out_shape=(jax.ShapeDtypeStruct((4, 32, 512...  56.6 us

profile of v5, /device:TPU:1, one launch (start us, length us, event | category | flops | bytes accessed | tf_op | source)
XLA Modules:
  0.0 148.8 jit_solution(11323005724059541428)
XLA Ops:
  1.9 0.5 broadcast.10
  2.4 1.4 reduce.6
  3.8 1.4 reduce.7
  5.3 0.1 tile.23
  5.3 0.1 copy.28
  5.4 0.8 copy.30.noise8
  6.2 0.1 tile.20
  6.3 0.1 copy.27
  6.4 0.8 copy.29.clean8
  7.1 83.0 %shard_map.243 = (bf16[32,2,32,256]{3,2,1,0:T(8,128)(2,1)}, bf16[32,2,32,256]{3,2,1,0:T(8,128)(2,1)}, bf16[256,2048]{1,0:T(8,128)(2,1)}, f32[8,128]{1,0:T(8,128)}) custom-call(s32[1]{0:T(128)S(6)} %copy.31.timestep, s32[1]{0:T(128)S(6)} %copy.32.bucket, f32[8]{0:T(128)} %bucket_weights.1, f32[256,128]{1,0:T(8,128)} %copy.29.clean8, f32[256,128]{1,0:T(8,128)} %copy.30.noise8, ...), custom_call_target="tpu_custom_call" | custom-call | tf_op jit(solution)/shard_map/pallas_call | solution.py:808
  90.1 56.6 %shard_map.244 = (f32[4,32,512]{2,1,0:T(8,128)}, f32[8,128]{1,0:T(8,128)}) custom-call(bf16[32,2,32,256]{3,2,1,0:T(8,128)(2,1)} %get-tuple-element.20.shaped, bf16[32,2,32,256]{3,2,1,0:T(8,128)(2,1)} %get-tuple-element.21.proj, bf16[256,2048]{1,0:T(8,128)(2,1)} %get-tuple-element.22.packed, f32[8,128]{1,0:T(8,128)} %get-tuple-element.23.loss_part), custom_call_target="tpu_custom_call" | custom-call | tf_op jit(solution)/shard_map/pallas_call | solution.py:275
  146.7 2.1 %shard_map.245 = (f32[3,32,512]{2,1,0:T(8,128)}, f32[3,32,512]{2,1,0:T(8,128)}, f32[3,32,512]{2,1,0:T(8,128)}, f32[32,512]{1,0:T(8,128)}, f32[32,512]{1,0:T(8,128)}, /*index=5*/f32[32,512]{1,0:T(8,128)}, f32[1,1]{1,0:T(1,128)}) custom-call(f32[4,32,512]{2,1,0:T(8,128)} %get-tuple-element.24.grads, f32[8,128]{1,0:T(8,128)} %get-tuple-element.25.totals, ...), custom_call_target="tpu_custom_call" | custom-call | tf_op jit(solution)/shard_map/pallas_call | solution.py:892
  (2 shorter events, 0.0 us)

commit v6 on v5

--- a/solution.py
+++ b/solution.py
@@ -165,151 +165,6 @@
     return start, relay, finish
 
 
-def reduce_kernel(
-    shaped,
-    proj,
-    packed,
-    loss_part,
-    out,
-    totals,
-    shaped_in,
-    proj_in,
-    packed_in,
-    part_a,
-    part_b,
-    part_c,
-    part_d,
-    *rest,
-):
-    boxes = [rest[4 * k : 4 * k + 4] for k in range(4)]
-    last, last_in, pair_send, pair_recv, send, recv, z_send, z_recv = rest[16:24]
-    inbox, sum_send, sum_recv = rest[24:]
-    y, x, z, core = (lax.axis_index(a) for a in AXES[:4])
-    greet([friend for _, partners in all_places() for friend in partners])
-    pair = [
-        remote(a, b, pair_send.at[k], pair_recv.at[k], "dp_3", 1 - core)
-        for k, (a, b) in enumerate(
-            [(packed, packed_in), (shaped.at[:, 1 - core], shaped_in), (proj.at[:, 1 - core], proj_in)]
-        )
-    ]
-    for c in pair:
-        c.start()
-
-    def products(s_ref, p_ref, b_ref, add):
-        def step(k, carry):
-            rows = pl.ds(pl.multiple_of(k * 8, 8), 8)
-            s, p = (r[rows].reshape(256, SEQ) for r in (s_ref, p_ref))
-            g = jnp.dot(s, b_ref[:, :HALF], preferred_element_type=jnp.float32)
-            for j in range(4):
-                block = g[64 * j : 64 * j + 64]
-                spot = pl.ds(pl.multiple_of(k * 64, 64), 64)
-                part_a[j, spot] = part_a[j, spot] + block if add else block
-            h = jnp.dot(s, b_ref[:, HALF : HALF + 512], preferred_element_type=jnp.float32)
-            part_b[k, :, 0:512] = part_b[k, :, 0:512] + h if add else h
-            o = jnp.dot(p, b_ref[:, HALF + 512 :], preferred_element_type=jnp.float32)
-            part_b[k, :, 512:1024] = part_b[k, :, 512:1024] + o if add else o
-            return carry
-
-        lax.fori_loop(0, 4, step, 0)
-
-    products(shaped.at[:, core], proj.at[:, core], packed, False)
-    for c in pair:
-        c.wait_recv()
-    products(shaped_in, proj_in, packed_in, True)
-
-    rings = [
-        ring_reduce(axis, part, *boxes[k], send.at[k], recv.at[k])
-        for k, (axis, part) in enumerate(
-            [("dp_1", part_a), ("dp_0", part_b), ("dp_0", part_c), ("dp_1", part_d)]
-        )
-    ]
-
-    def into(part):
-        def store(which, cols, value):
-            part[2 * which, :, cols] = value[:64]
-            part[2 * which + 1, :, cols] = value[64:]
-
-        return store
-
-    rings[0][0]()
-    rings[1][0]()
-    rings[0][1]()
-    rings[1][1]()
-    rings[0][2](into(part_c))
-    rings[2][0]()
-    rings[1][2](into(part_d))
-    rings[3][0]()
-    rings[2][1]()
-    rings[3][1]()
-    z_copies = []
-    for k in range(2):
-
-        def store(which, cols, value, k=k):
-            last[k, which, :, cols] = value
-
-        rings[2 + k][2](store)
-        c = remote(
-            last.at[k, 1 - z], last_in.at[k], z_send.at[k], z_recv.at[k], "dp_2", 1 - z
-        )
-        c.start()
-        z_copies.append(c)
-    for k, c in enumerate(z_copies):
-        c.wait_recv()
-        both = last[k, z] + last_in[k]
-        out[2 * k] = both[:, :512]
-        out[2 * k + 1] = both[:, 512:]
-    for c in [*pair, *z_copies]:
-        c.wait_send()
-    squares = jnp.sum(out[...] * out[...])
-    row = lax.broadcasted_iota(jnp.int32, (8, 128), 0)
-    value = jnp.where(row == 0, squares, loss_part[...])
-    totals[...] = sum_over_all(value, inbox, sum_send, sum_recv)
-
-
-def reduce_gradients(shaped, proj, packed, loss_part):
-    vmem = pl.BlockSpec(memory_space=pltpu.VMEM)
-
-    def boxes(half):
-        return [pltpu.VMEM((6, half, HALF), jnp.int16), pltpu.VMEM((6, 1, HALF), jnp.float32)] * 2
-
-    return pl.pallas_call(
-        reduce_kernel,
-        out_shape=(
-            jax.ShapeDtypeStruct((4, 32, 512), jnp.float32),
-            jax.ShapeDtypeStruct((8, 128), jnp.float32),
-        ),
-        in_specs=[vmem] * 4,
-        out_specs=(vmem, vmem),
-        scratch_shapes=[
-            pltpu.VMEM((32, 32, SEQ), jnp.bfloat16),
-            pltpu.VMEM((32, 32, SEQ), jnp.bfloat16),
-            pltpu.VMEM((SEQ, 2 * HALF), jnp.bfloat16),
-            pltpu.VMEM((4, 256, HALF), jnp.float32),
-            pltpu.VMEM((4, 256, HALF), jnp.float32),
-            pltpu.VMEM((4, 64, HALF), jnp.float32),
-            pltpu.VMEM((4, 64, HALF), jnp.float32),
-            *boxes(128),
-            *boxes(128),
-            *boxes(32),
-            *boxes(32),
-            pltpu.VMEM((2, 2, 32, HALF), jnp.float32),
-            pltpu.VMEM((2, 32, HALF), jnp.float32),
-            pltpu.SemaphoreType.DMA((3,)),
-            pltpu.SemaphoreType.DMA((3,)),
-            pltpu.SemaphoreType.DMA((4, 6, 2)),
-            pltpu.SemaphoreType.DMA((4, 6, 2)),
-            pltpu.SemaphoreType.DMA((2,)),
-            pltpu.SemaphoreType.DMA((2,)),
-            pltpu.VMEM((3, 8, 8, 128), jnp.float32),
-            pltpu.SemaphoreType.DMA((3, 7)),
-            pltpu.SemaphoreType.DMA((3, 7)),
-        ],
-        compiler_params=pltpu.CompilerParams(
-            collective_id=1, has_side_effects=True, vmem_limit_bytes=60 * 2**20
-        ),
-    )(shaped, proj, packed, loss_part)
-
-
 TOKENS = 256
 UNROLL = 4
 WIDE = 256
@@ -321,7 +176,7 @@
     return lax.dot_general(a, b, dims, preferred_element_type=jnp.float32)
 
 
-def gather_stream(held, slabs, send, recv):
+def gather_stream(held, slabs, send, recv, short=False):
     y, x, z, core = (lax.axis_index(a) for a in AXES[:4])
     near = {"dp_0": [lax.rem(y + k, 4) for k in (1, 3)], "dp_1": [lax.rem(x + k, 4) for k in (1, 3)]}
     every = slice(None)
@@ -362,16 +217,23 @@
     def across(k, spot):
         go((*spot[:3], core, spot[3]), k, "dp_3", 1 - core)
 
+    def ring_straight():
+        for half, (axis, me) in enumerate([("dp_1", x), ("dp_0", y)]):
+            for k in (1, 2, 3):
+                go((y, x, every, core, half), 3 * half + k - 1, axis, lax.rem(me + k, 4))
+
     def step(k):
+        if short:
+            k = k + 2
         if k == 0:
             go((y, x, z, core), 0, "dp_2", 1 - z)
         elif k == 1:
             live[-1].wait_recv()
             ring_direct(True)
         elif k == 2:
-            ring_relay(True)
+            ring_straight() if short else ring_relay(True)
         elif k == 3:
-            for c in live[-4:]:
+            for c in live[-6:] if short else live[-4:]:
                 c.wait_recv()
             ring_direct(False)
         elif k == 4:
@@ -397,43 +259,6 @@
     return step
 
 
-def gather_direct(held, slab, send, recv):
-    y, x, z, core = (lax.axis_index(a) for a in AXES[:4])
-    every = slice(None)
-    live = []
-
-    def ring(spots, base):
-        for half, (axis, spot) in enumerate(spots):
-            me = lax.axis_index(axis)
-            for k in (1, 2, 3):
-                ref = held.at[(slab, *spot, core, half)]
-                n = base + 3 * half + k - 1
-                c = remote(ref, ref, send.at[n], recv.at[n], axis, lax.rem(me + k, 4))
-                c.start()
-                live.append(c)
-
-    def step(k):
-        if k == 0:
-            ring([("dp_1", (y, x, every)), ("dp_0", (y, x, every))], 0)
-        elif k == 1:
-            for c in live:
-                c.wait_recv()
-            ring([("dp_0", (y, every, every)), ("dp_1", (every, x, every))], 6)
-        elif k == 2:
-            for c in live[6:]:
-                c.wait_recv()
-            ref = held.at[slab, :, :, :, core]
-            c = remote(ref, ref, send.at[12], recv.at[12], "dp_3", 1 - core)
-            c.start()
-            live.append(c)
-        else:
-            live[-1].wait_recv()
-            for c in live:
-                c.wait_send()
-
-    return step
-
-
 def three_terms(v8):
     high = v8.astype(jnp.bfloat16).astype(jnp.float32)
     rest = v8 - high
@@ -448,6 +273,21 @@
     return picked.astype(jnp.bfloat16)
 
 
+def eightfold(rows):
+    v = jnp.broadcast_to(rows[:, None], (32, 8, 128)).reshape(TOKENS, 128)
+    token = lax.broadcasted_iota(jnp.int32, v.shape, 0) % 8
+    lane = lax.broadcasted_iota(jnp.int32, v.shape, 1)
+    v = jnp.where(lane // 16 == token, v, 0.0)
+    across = lax.broadcasted_iota(jnp.int32, (128, 128), 1) % 16
+    down = lax.broadcasted_iota(jnp.int32, (128, 128), 0) % 16
+    spread = jnp.where(across == down, 1.0, 0.0).astype(jnp.bfloat16)
+    high = v.astype(jnp.bfloat16)
+    rest = v - high.astype(jnp.float32)
+    middle = rest.astype(jnp.bfloat16)
+    low = (rest - middle.astype(jnp.float32)).astype(jnp.bfloat16)
+    return dot(high, spread) + dot(middle, spread) + dot(low, spread)
+
+
 def picked_level(step, offset, values):
     out = jnp.float32(0.0)
     for k in range(1, K + 1):
@@ -459,8 +299,8 @@
     timestep,
     bucket,
     bucket_weights,
-    clean8,
-    noise8,
+    clean,
+    noise,
     tables,
     teacher_embed,
     teacher_final,
@@ -469,19 +309,15 @@
     student_final,
     student_mod,
     teacher_qkv,
-    teacher_out,
+    teacher_out_far,
     student_qkv,
     student_out,
-    shaped_t,
-    proj_t,
-    packed,
-    loss_part,
+    out,
+    totals,
     held,
     near_qkv,
-    placed,
-    hidden,
-    hidden_s,
-    mixed,
+    teacher_out,
+    wide,
     shaped,
     shaped_s,
     qkv,
@@ -493,43 +329,62 @@
     d_attn,
     embed_t,
     embed_s,
-    back_s,
-    final_t,
-    final_s,
+    final_b,
+    lat_rows,
+    shaped_t,
+    proj_t,
+    shaped_in,
+    proj_in,
+    packed_in,
+    part_c,
+    part_d,
     qkv_sem,
+    out_sem,
     swap_send,
     swap_recv,
     t_send,
     t_recv,
     s_send,
     s_recv,
+    o_send,
+    o_recv,
+    *rest,
 ):
+    boxes = [rest[4 * k : 4 * k + 4] for k in range(4)]
+    last, last_in, pair_send, pair_recv, send, recv, z_send, z_recv = rest[16:24]
+    inbox, sum_send, sum_recv = rest[24:]
+    hidden, hidden_s, mixed, placed = (wide.at[k] for k in range(4))
+    part_a, part_b = (wide.at[:, :, pl.ds(HALF * k, HALF)] for k in range(2))
+    packed = near_qkv.at[0, pl.ds(0, 4 * TOKENS)]
     y, x, z, core, mp = (lax.axis_index(a) for a in AXES)
+    load_out = pltpu.make_async_copy(teacher_out_far, teacher_out, out_sem)
+    load_out.start()
     load = pltpu.make_async_copy(teacher_qkv, near_qkv, qkv_sem)
     load.start()
     held[0:3, y, x, z, core] = student_qkv[...]
     held[3, y, x, z, core] = student_out[...]
     both = ("dp_2", "mp")
-    friends = [("dp_3", 1 - core), ("dp_2", 1 - z), ("mp", 1 - mp), (both, (1 - z, 1 - mp))]
-    friends += [("dp_1", lax.rem(x + k, 4)) for k in (1, 2, 3)]
-    friends += [("dp_0", lax.rem(y + k, 4)) for k in (1, 2, 3)]
-    greet(friends)
+    greet([friend for _, partners in all_places() for friend in partners])
 
     def swap(src, dst, k, axis="mp", target=None):
         target = 1 - mp if target is None else target
         return remote(src, dst, swap_send.at[k], swap_recv.at[k], axis, target)
 
+    load_out.wait()
     spot = (y, x, z, core)
     here = teacher_out.at[spot]
     swaps = [
         swap(here, held.at[(5, *spot)], 0),
         swap(here, held.at[(5, *spot)], 1, both, (1 - z, 1 - mp)),
-        swap(student_out, held.at[(4, *spot)], 2),
+        swap(student_out, held.at[(4, *spot)], 15),
+        swap(student_out, held.at[(4, *spot)], 16, both, (1 - z, 1 - mp)),
     ]
     for c in swaps:
         c.start()
-    t_step = gather_direct(held, 5, t_send, t_recv)
-    s_step = gather_stream(held, pl.ds(0, 5), s_send, s_recv)
+    t_step = gather_stream(held, pl.ds(5, 1), t_send, t_recv, short=True)
+    s_step = gather_stream(held, pl.ds(0, 4), s_send, s_recv)
+    o_step = gather_stream(held, pl.ds(4, 1), o_send, o_recv, short=True)
+    s_step(0)
 
     step = timestep[0]
     a_f, a_m, a_l = (picked_level(step, -k, ALPHAS) for k in range(3))
@@ -573,8 +428,9 @@
         lax.fori_loop(0, D // WIDE, body, 0)
 
     def centred(v):
-        c = v - jnp.mean(v, axis=-1, keepdims=True)
-        return c, lax.rsqrt(jnp.mean(c * c, axis=-1, keepdims=True) + LN_EPS)
+        mean = jnp.mean(v, axis=-1, keepdims=True)
+        c = v - mean
+        return c, lax.rsqrt(jnp.mean(c * c, axis=-1, keepdims=True) + LN_EPS), mean
 
     def by_rows(body):
         def group(n, carry):
@@ -588,7 +444,7 @@
         shift, scale = modrows[which][0], 1.0 + modrows[which][1]
 
         def body(rows):
-            c, inv = centred(hid[rows])
+            c, inv, _ = centred(hid[rows])
             out[rows] = (c * inv * scale + shift).astype(jnp.bfloat16)
 
         by_rows(body)
@@ -643,11 +499,11 @@
 
     def predict(final, keep):
         def body(rows):
-            c, inv = centred(mixed[rows])
+            c, inv, mean = centred(mixed[rows])
             u = c * inv
             if keep:
-                placed[rows] = u
-                inverses[rows] = jnp.broadcast_to(inv, (16, 128))
+                inverses[0, rows] = jnp.broadcast_to(inv, (16, 128))
+                inverses[1, rows] = jnp.broadcast_to(mean, (16, 128))
             high = u.astype(jnp.bfloat16)
             rest = u - high.astype(jnp.float32)
             middle = rest.astype(jnp.bfloat16)
@@ -679,6 +535,15 @@
 
         lax.fori_loop(0, D // 128, body, 0)
 
+    def pair(k):
+        if k < 2:
+            src, dst = ((shaped_t, shaped_in), (proj_t, proj_in))[k]
+            src = src.at[:, 1 - core]
+        else:
+            cols = pl.ds(128 * (k - 2), 128)
+            src, dst = packed.at[:, cols], packed_in.at[:, cols]
+        return remote(src, dst, pair_send.at[k], pair_recv.at[k], "dp_3", 1 - core)
+
     half = D // 2
     for k in range(16):
         sin_a, cos_a = tables[0, k : k + 1], tables[1, k : k + 1]
@@ -686,78 +551,90 @@
         placed[rows, :half] = sin_a * tables[3] + cos_a * tables[2]
         placed[rows, half:] = cos_a * tables[3] - sin_a * tables[2]
     stack(split_rows(teacher_embed), embed_t)
-    lat0 = a_f * clean8[...] + s_f * noise8[...]
+    latents = a_f * clean[...] + s_f * noise[...]
+    for k in range(32):
+        lat_rows[k : k + 1] = latents[:, 128 * k : 128 * k + 128]
+    lat0 = eightfold(lat_rows[...])
     spread(lat0, embed_t, hidden, placed)
+    shape(hidden, 0, shaped)
     swaps[0].wait_recv()
     swaps[1].wait_recv()
     t_step(0)
-    swaps[2].wait_recv()
-    s_step(0)
-    shape(hidden, 0, shaped)
+    s_step(1)
     load.wait()
     project(shaped, lambda j: near_qkv[j])
     t_step(1)
-    s_step(1)
     attend(0, False)
+    s_step(2)
     t_step(2)
-    s_step(2)
     mix(heads.at[0], near_rows, 0, hidden)
+    s_step(3)
     stack(split_rows(student_embed), embed_s)
-    repeat(split_rows(teacher_final), final_t)
+    repeat(split_rows(teacher_final), final_b)
     spread(lat0, embed_s, hidden_s, placed)
     t_step(3)
-    s_step(3)
+    shape(hidden_s, 2, shaped_s)
+    turn(shaped_s, shaped_t)
+    t_step(4)
     swapped(0)
     mix(heads_in.at[0], other_rows(5), 0, mixed)
-    eps0 = predict(final_t, False)
+    eps0 = predict(final_b, False)
     lat1 = a_m * (lat0 - s_f * eps0) / a_f + s_m * eps0
 
     spread(lat1, embed_t, hidden, placed)
     shape(hidden, 1, shaped)
     project(shaped, lambda j: near_qkv[j])
+    s_step(4)
+    swaps[2].wait_recv()
+    swaps[3].wait_recv()
+    o_step(0)
     attend(1, False)
     mix(heads.at[1], near_rows, 1, hidden)
-    shape(hidden_s, 2, shaped_s)
-    s_step(4)
     swapped(1)
     mix(heads_in.at[1], other_rows(5), 1, mixed)
-    eps1 = predict(final_t, False)
+    s_step(5)
+    o_step(1)
+    eps1 = predict(final_b, False)
     lat2 = a_l * (lat1 - s_m * eps1) / a_m + s_l * eps1
     target = (lat0 - a_f / a_l * lat2) / (s_f - a_f * s_l / a_l)
 
-    s_step(5)
-    turn(shaped_s, shaped_t)
+    pair(0).start()
     student_terms = split_rows(student_final)
-    repeat(student_terms, final_s)
-    stack(student_terms, back_s)
+    repeat(student_terms, final_b)
+    stack(student_terms, embed_t)
     s_step(6)
     project(shaped_s, lambda j: held[j].reshape(D, 512))
+    o_step(2)
     attend(2, True)
     mix(heads.at[2], other_rows(3), 2, hidden_s)
+    o_step(3)
+    o_step(4)
     swapped(2)
     mix(heads_in.at[2], other_rows(4), 2, mixed)
-    error = predict(final_s, True) - target
+    error = predict(final_b, True) - target
     lanes = lax.broadcasted_iota(jnp.int32, error.shape, 1)
-    loss_part[...] = jnp.full(
-        (8, 128), 0.5 * row_weight * jnp.sum(jnp.where(lanes < 16, error * error, 0.0))
+    loss_part = (
+        0.5 * row_weight * jnp.sum(jnp.where(lanes < 16, error * error, 0.0))
     )
 
-    spread(2.0 * row_weight * error, back_s, hidden)
+    spread(2.0 * row_weight * error, embed_t, hidden)
 
     gate = modrows[2][2]
 
     def back(rows):
-        up, u = hidden[rows], placed[rows]
+        inv, mean = inverses[0, rows, 0:1], inverses[1, rows, 0:1]
+        up, u = hidden[rows], (mixed[rows] - mean) * inv
         first_mean = jnp.mean(up, axis=-1, keepdims=True)
         second_mean = jnp.mean(up * u, axis=-1, keepdims=True)
-        d = (up - first_mean - u * second_mean) * inverses[rows, 0:1]
+        d = (up - first_mean - u * second_mean) * inv
         shaped[rows] = (gate * d).astype(jnp.bfloat16)
 
     by_rows(back)
+    turn(shaped, proj_t)
     d_attn[...] = dot(shaped[...], held[3].reshape(D, 512)).astype(jnp.bfloat16)
-
-    def back_heads(hp, carry):
-        cols = columns(hp, 128)
+    pair(1).start()
+    for hp in range(4):
+        cols = pl.ds(128 * hp, 128)
         q, k, v, da = qkv[0, :, cols], qkv[1, :, cols], qkv[2, :, cols], d_attn[:, cols]
         outs = []
         for h in range(2):
@@ -767,16 +644,86 @@
             ds = ds.astype(jnp.bfloat16)
             outs.append((dot(ds, k), dot(ds, q, TN), dot(w.astype(jnp.bfloat16), da, TN)))
         for j in range(3):
-            spot = pl.ds(pl.multiple_of(j * 512 + hp * 128, 128), 128)
-            both = jnp.where(is_low, outs[0][j], outs[1][j])
-            packed[:, spot] = both.astype(jnp.bfloat16)
-        packed[:, pl.ds(pl.multiple_of(1536 + hp * 128, 128), 128)] = heads[2, :, cols]
-        return carry
-
-    lax.fori_loop(0, 4, back_heads, 0)
-    turn(shaped, proj_t)
+            joined = jnp.where(is_low, outs[0][j], outs[1][j]).astype(jnp.bfloat16)
+            packed[TOKENS * j : TOKENS * (j + 1), cols] = joined
+        packed[3 * TOKENS :, cols] = heads[2, :, cols]
+        if hp > 0:
+            pair(1 + hp).start()
+    pair(5).start()
+
+    def products(s_ref, p_ref, b_ref, add):
+        def body(k, carry):
+            rows = pl.ds(pl.multiple_of(k * 8, 8), 8)
+            s, p = (r[rows].reshape(256, TOKENS) for r in (s_ref, p_ref))
+            spot = pl.ds(pl.multiple_of(k * 64, 64), 64)
+            for j in range(4):
+                g = dot(p if j == 3 else s, b_ref[TOKENS * j : TOKENS * (j + 1)])
+                cols = pl.ds(512 * (j % 2), 512)
+                if j < 2:
+                    for i in range(4):
+                        block = g[64 * i : 64 * i + 64]
+                        part_a[i, spot, cols] = part_a[i, spot, cols] + block if add else block
+                else:
+                    part_b[k, :, cols] = part_b[k, :, cols] + g if add else g
+            return carry
+
+        lax.fori_loop(0, 4, body, 0)
+
+    products(shaped_t.at[:, core], proj_t.at[:, core], packed, False)
+    for k in range(6):
+        pair(k).wait_recv()
+    products(shaped_in, proj_in, packed_in, True)
+    rings = [
+        ring_reduce(axis, part, *boxes[k], send.at[k], recv.at[k])
+        for k, (axis, part) in enumerate(
+            [("dp_1", part_a), ("dp_0", part_b), ("dp_0", part_c), ("dp_1", part_d)]
+        )
+    ]
+
+    def into(part):
+        def store(which, cols, value):
+            part[2 * which, :, cols] = value[:64]
+            part[2 * which + 1, :, cols] = value[64:]
+
+        return store
+
+    rings[0][0]()
+    rings[1][0]()
+    rings[0][1]()
+    rings[1][1]()
+    rings[0][2](into(part_c))
+    rings[2][0]()
+    rings[1][2](into(part_d))
+    rings[3][0]()
+    rings[2][1]()
+    rings[3][1]()
+    z_copies = []
+    for k in range(2):
+
+        def store(which, cols, value, k=k):
+            last[k, which, :, cols] = value
+
+        rings[2 + k][2](store)
+        c = remote(
+            last.at[k, 1 - z], last_in.at[k], z_send.at[k], z_recv.at[k], "dp_2", 1 - z
+        )
+        c.start()
+        z_copies.append(c)
+    for k, c in enumerate(z_copies):
+        c.wait_recv()
+        both = last[k, z] + last_in[k]
+        out[2 * k] = both[:, :512]
+        out[2 * k + 1] = both[:, 512:]
+    for c in z_copies:
+        c.wait_send()
+    squares = jnp.sum(out[...] * out[...])
+    row = lax.broadcasted_iota(jnp.int32, (8, 128), 0)
+    value = jnp.where(row == 0, squares, loss_part)
+    totals[...] = sum_over_all(value, inbox, sum_send, sum_recv)
     for c in swaps:
         c.wait_send()
+    for k in range(6):
+        pair(k).wait_send()
     for which in range(3):
         for hp in range(4):
             swap_pair(which, hp).wait_send()
@@ -802,26 +749,25 @@
     vmem, smem = (pl.BlockSpec(memory_space=m) for m in (pltpu.VMEM, pltpu.SMEM))
     bf16, f32 = jnp.bfloat16, jnp.float32
 
-    def tiled(v):
-        return jnp.tile(v.reshape(SEQ, PATCH_CH), (1, 8))
+    def boxes(half):
+        return [pltpu.VMEM((6, half, HALF), jnp.int16), pltpu.VMEM((6, 1, HALF), f32)] * 2
+
+    def semaphores(*shape):
+        return [pltpu.SemaphoreType.DMA(shape)] * 2
 
     return pl.pallas_call(
         step_kernel,
         out_shape=(
-            jax.ShapeDtypeStruct((32, 2, 32, TOKENS), bf16),
-            jax.ShapeDtypeStruct((32, 2, 32, TOKENS), bf16),
-            jax.ShapeDtypeStruct((TOKENS, D), bf16),
+            jax.ShapeDtypeStruct((4, 32, 512), f32),
             jax.ShapeDtypeStruct((8, 128), f32),
         ),
-        in_specs=[smem] * 3 + [vmem] * 9 + [pl.BlockSpec(memory_space=pl.ANY)] + [vmem] * 3,
-        out_specs=(vmem,) * 4,
+        in_specs=[smem] * 3 + [vmem] * 9 + [pl.BlockSpec(memory_space=pl.ANY)] * 2 + [vmem] * 2,
+        out_specs=(vmem,) * 2,
         scratch_shapes=[
             pltpu.VMEM((6, 4, 4, 2, 2, 2, 16, 512), bf16),
             pltpu.VMEM((3, D, 512), bf16),
-            pltpu.VMEM((TOKENS, D), f32),
-            pltpu.VMEM((TOKENS, D), f32),
-            pltpu.VMEM((TOKENS, D), f32),
-            pltpu.VMEM((TOKENS, D), f32),
+            pltpu.VMEM((4, 4, 2, 2, 2, 16, 512), bf16),
+            pltpu.VMEM((4, TOKENS, D), f32),
             pltpu.VMEM((TOKENS, D), bf16),
             pltpu.VMEM((TOKENS, D), bf16),
             pltpu.VMEM((3, TOKENS, 512), bf16),
@@ -829,30 +775,46 @@
             pltpu.VMEM((3, TOKENS, 512), bf16),
             pltpu.VMEM((8, TOKENS, TOKENS), f32),
             pltpu.VMEM((3, TOKENS, D), bf16),
-            pltpu.VMEM((TOKENS, 128), f32),
+            pltpu.VMEM((2, TOKENS, 128), f32),
             pltpu.VMEM((TOKENS, 512), bf16),
             pltpu.VMEM((128, D), bf16),
             pltpu.VMEM((128, D), bf16),
-            pltpu.VMEM((128, D), bf16),
             pltpu.VMEM((384, D), bf16),
-            pltpu.VMEM((384, D), bf16),
+            pltpu.VMEM((32, 128), f32),
+            pltpu.VMEM((32, 2, 32, TOKENS), bf16),
+            pltpu.VMEM((32, 2, 32, TOKENS), bf16),
+            pltpu.VMEM((32, 32, TOKENS), bf16),
+            pltpu.VMEM((32, 32, TOKENS), bf16),
+            pltpu.VMEM((4 * TOKENS, 512), bf16),
+            pltpu.VMEM((4, 64, HALF), f32),
+            pltpu.VMEM((4, 64, HALF), f32),
             pltpu.SemaphoreType.DMA,
-            pltpu.SemaphoreType.DMA((15,)),
-            pltpu.SemaphoreType.DMA((15,)),
-            pltpu.SemaphoreType.DMA((13,)),
-            pltpu.SemaphoreType.DMA((13,)),
-            pltpu.SemaphoreType.DMA((25,)),
-            pltpu.SemaphoreType.DMA((25,)),
+            pltpu.SemaphoreType.DMA,
+            *semaphores(17),
+            *semaphores(25),
+            *semaphores(25),
+            *semaphores(25),
+            *boxes(128),
+            *boxes(128),
+            *boxes(32),
+            *boxes(32),
+            pltpu.VMEM((2, 2, 32, HALF), f32),
+            pltpu.VMEM((2, 32, HALF), f32),
+            *semaphores(6),
+            *semaphores(4, 6, 2),
+            *semaphores(2),
+            pltpu.VMEM((3, 8, 8, 128), f32),
+            *semaphores(3, 7),
         ],
         compiler_params=pltpu.CompilerParams(
-            collective_id=2, has_side_effects=True, vmem_limit_bytes=62 * 2**20
+            collective_id=2, has_side_effects=True, vmem_limit_bytes=63 * 2**20
         ),
     )(
         timestep,
         bucket,
         bucket_weights,
-        tiled(clean),
-        tiled(noise),
+        clean,
+        noise,
         jnp.asarray(position_tables()),
         teacher[0],
         teacher[1],
@@ -919,7 +881,7 @@
     moment_out,
     second_out,
 ):
-    shaped, proj, packed, loss_part = whole_step(
+    grads, totals = whole_step(
         timestep,
         bucket,
         bucket_weights,
@@ -928,7 +890,6 @@
         (teacher_embed, teacher_final, teacher_mod, teacher_qkv, teacher_out),
         (student_embed, student_final, student_mod, student_qkv, student_out),
     )
-    grads, totals = reduce_gradients(shaped, proj, packed, loss_part)
     return adam_update(grads, totals, moment_qkv, second_qkv, moment_out, second_out)
 
 

time: 150 us -> 133 us (0.89)
  Pallas kernels: 142 us -> 130 us
  other arithmetic: 2.81 us -> 0 us
  local copies, waits for them, and re-layouts: 2.37 us -> 0 us
    pallas_call x2 -> x1, Pallas kernels: 140 us -> 128 us  [whole_step(): pl.pallas_call(step_kernel, out_shape=(jax.ShapeDtypeStruct((4, 32, 512),...]
    unnamed x2 -> x0, other arithmetic: 2.81 us -> none
    another operation x8 -> x0, local copies, waits for them, and re-layouts: 1.86 us -> none  [tiled(): return jnp.tile(v.reshape(SEQ, PATCH_CH), (1, 8))]
where the time goes in v6:
time: 133 us; the launch traced here: 132 us
  Pallas kernels  130 us (98%)
  between operations  1.94 us (1%)
    pallas_call x1, Pallas kernels, whole_step(): pl.pallas_call(step_kernel, out_shape=(jax.ShapeDtypeStruct((4, 32, 512),...  128 us

profile of v6, /device:TPU:1, one launch (start us, length us, event | category | flops | bytes accessed | tf_op | source)
XLA Modules:
  0.0 132.0 jit_solution(17648543193454260761)
XLA Ops:
  1.9 128.0 %shard_map.243 = (f32[4,32,512]{2,1,0:T(8,128)}, f32[8,128]{1,0:T(8,128)}) custom-call(s32[1]{0:T(128)S(6)} %copy.27.timestep, s32[1]{0:T(128)S(6)} %copy.28.bucket, f32[8]{0:T(128)} %bucket_weights.1, f32[1,4096]{1,0:T(1,128)} %clean.1, f32[1,4096]{1,0:T(1,128)} %noise.1, f32[4,16,1024]{2,1,0:T(8,128)} %constant.2.clone.tables, f32[16,2048]{1,0:T(8,128)} %teacher_embed.1, ...), custom_call_target="tpu_custom_call" | custom-call | tf_op jit(solution)/shard_map/pallas_call | solution.py:758
  129.9 2.1 %shard_map.244 = (f32[3,32,512]{2,1,0:T(8,128)}, f32[3,32,512]{2,1,0:T(8,128)}, f32[3,32,512]{2,1,0:T(8,128)}, f32[32,512]{1,0:T(8,128)}, f32[32,512]{1,0:T(8,128)}, /*index=5*/f32[32,512]{1,0:T(8,128)}, f32[1,1]{1,0:T(1,128)}) custom-call(f32[4,32,512]{2,1,0:T(8,128)} %get-tuple-element.16.grads, f32[8,128]{1,0:T(8,128)} %get-tuple-element.17.totals, ...), custom_call_target="tpu_custom_call" | custom-call | tf_op jit(solution)/shard_map/pallas_call | solution.py:854

commit v7 on v6

--- a/solution.py
+++ b/solution.py
@@ -64,11 +64,10 @@
     cube = []
     for k in range(1, 8):
         cube.append((axes, tuple(1 - h if k >> n & 1 else h for n, h in enumerate(here))))
-    return [
-        (4 * mp + 2 * z + core, cube),
-        (x, [("dp_1", lax.rem(x + k, 4)) for k in (1, 2, 3)]),
-        (y, [("dp_0", lax.rem(y + k, 4)) for k in (1, 2, 3)]),
-    ]
+    plane = []
+    for k in range(1, 16):
+        plane.append((("dp_0", "dp_1"), (lax.rem(y + k // 4, 4), lax.rem(x + k % 4, 4))))
+    return [(4 * mp + 2 * z + core, cube), (4 * y + x, plane)]
 
 
 def sum_over_all(value, inbox, send, recv):
@@ -97,23 +96,15 @@
     return value
 
 
-def by_columns(body):
+def by_columns(body, width):
     def step(n, carry):
         body(pl.ds(pl.multiple_of(n * 256, 256), 256))
         return carry
 
-    lax.fori_loop(0, HALF // 256, step, 0)
-
-
-def ring_reduce(axis, part, codes, scales, boxes, box_scales, send, recv):
-    me = lax.axis_index(axis)
-    right, left, far = (lax.rem(me + k, 4) for k in (1, 3, 2))
-    half = part.shape[1] // 2
-    top, low = pl.ds(0, half), pl.ds(half, half)
-
-    def decoded(k, cols):
-        return boxes[k, :, cols].astype(jnp.int32).astype(jnp.float32) * box_scales[k, :, cols]
-
+    lax.fori_loop(0, width // 256, step, 0)
+
+
+def coder(codes, scales, boxes, box_scales):
     def encode(k, value):
         def body(cols):
             v = value(cols)
@@ -122,7 +113,21 @@
             codes[k, :, cols] = code.astype(jnp.int32).astype(jnp.int16)
             scales[k, :, cols] = peak * (1.0 / CODES)
 
-        by_columns(body)
+        by_columns(body, codes.shape[2])
+
+    def decoded(k, cols):
+        return boxes[k, :, cols].astype(jnp.int32).astype(jnp.float32) * box_scales[k, :, cols]
+
+    return encode, decoded
+
+
+def ring_reduce(axis, part, codes, scales, boxes, box_scales, send, recv):
+    me = lax.axis_index(axis)
+    right, left, far = (lax.rem(me + k, 4) for k in (1, 3, 2))
+    half, width = part.shape[1] // 2, part.shape[2]
+    top, low = pl.ds(0, half), pl.ds(half, half)
+
+    encode, decoded = coder(codes, scales, boxes, box_scales)
 
     def message(k):
         target = left if k % 2 else right
@@ -155,9 +160,15 @@
 
     def finish(store):
         arrived(3, 4)
-        by_columns(lambda cols: store(0, cols, part[me, top, cols] + decoded(3, cols) + decoded(4, cols)))
+        by_columns(
+            lambda cols: store(0, cols, part[me, top, cols] + decoded(3, cols) + decoded(4, cols)),
+            width,
+        )
         arrived(2, 5)
-        by_columns(lambda cols: store(1, cols, part[me, low, cols] + decoded(2, cols) + decoded(5, cols)))
+        by_columns(
+            lambda cols: store(1, cols, part[me, low, cols] + decoded(2, cols) + decoded(5, cols)),
+            width,
+        )
         for k in range(6):
             for c in message(k):
                 c.wait_send()
@@ -312,8 +323,9 @@
     teacher_out_far,
     student_qkv,
     student_out,
+    out_far,
+    totals,
     out,
-    totals,
     held,
     near_qkv,
     teacher_out,
@@ -340,6 +352,7 @@
     part_d,
     qkv_sem,
     out_sem,
+    grads_sem,
     swap_send,
     swap_recv,
     t_send,
@@ -350,12 +363,11 @@
     o_recv,
     *rest,
 ):
-    boxes = [rest[4 * k : 4 * k + 4] for k in range(4)]
-    last, last_in, pair_send, pair_recv, send, recv, z_send, z_recv = rest[16:24]
-    inbox, sum_send, sum_recv = rest[24:]
+    boxes = [rest[4 * k : 4 * k + 4] for k in range(10)]
+    last, pair_send, pair_recv, send, recv, z_send, z_recv = rest[40:47]
+    inbox, sum_send, sum_recv = rest[47:]
     hidden, hidden_s, mixed, placed = (wide.at[k] for k in range(4))
-    part_a, part_b = (wide.at[:, :, pl.ds(HALF * k, HALF)] for k in range(2))
-    packed = near_qkv.at[0, pl.ds(0, 4 * TOKENS)]
+    packed = near_qkv.at[0, pl.ds(0, 3 * TOKENS)]
     y, x, z, core, mp = (lax.axis_index(a) for a in AXES)
     load_out = pltpu.make_async_copy(teacher_out_far, teacher_out, out_sem)
     load_out.start()
@@ -419,13 +431,10 @@
     def spread(v8, b_ref, out, base=None):
         terms8 = three_terms(v8)
 
-        def body(n, carry):
-            cols = columns(n, WIDE)
+        for n in range(D // WIDE):
+            cols = pl.ds(n * WIDE, WIDE)
             h = dot(terms8, b_ref[:, cols])
             out[:, cols] = h if base is None else h + base[:, cols]
-            return carry
-
-        lax.fori_loop(0, D // WIDE, body, 0)
 
     def centred(v):
         mean = jnp.mean(v, axis=-1, keepdims=True)
@@ -489,13 +498,10 @@
     def mix(att, weight, which, base):
         mod_ref, at = places[which]
 
-        def body(n, carry):
-            cols = columns(n, 512)
+        for n in range(4):
+            cols = pl.ds(n * 512, 512)
             p = dot(att[...], weight(n), NT)
             mixed[:, cols] = base[:, cols] + mod_ref[2, pl.ds(at, 1), cols] * p
-            return carry
-
-        lax.fori_loop(0, 4, body, 0)
 
     def predict(final, keep):
         def body(rows):
@@ -539,9 +545,11 @@
         if k < 2:
             src, dst = ((shaped_t, shaped_in), (proj_t, proj_in))[k]
             src = src.at[:, 1 - core]
+        elif k == 2:
+            src, dst = heads.at[2], packed_in.at[pl.ds(3 * TOKENS, TOKENS)]
         else:
-            cols = pl.ds(128 * (k - 2), 128)
-            src, dst = packed.at[:, cols], packed_in.at[:, cols]
+            cols = pl.ds(128 * (k - 3), 128)
+            src, dst = packed.at[:, cols], packed_in.at[pl.ds(0, 3 * TOKENS), cols]
         return remote(src, dst, pair_send.at[k], pair_recv.at[k], "dp_3", 1 - core)
 
     half = D // 2
@@ -608,8 +616,8 @@
     attend(2, True)
     mix(heads.at[2], other_rows(3), 2, hidden_s)
     o_step(3)
+    swapped(2)
     o_step(4)
-    swapped(2)
     mix(heads_in.at[2], other_rows(4), 2, mixed)
     error = predict(final_b, True) - target
     lanes = lax.broadcasted_iota(jnp.int32, error.shape, 1)
@@ -631,8 +639,76 @@
 
     by_rows(back)
     turn(shaped, proj_t)
+    pair(2).start()
     d_attn[...] = dot(shaped[...], held[3].reshape(D, 512)).astype(jnp.bfloat16)
     pair(1).start()
+
+    extents = [(0, 3 * WIDE), (3 * WIDE, WIDE)]
+
+    def products(s_ref, b_ref, first, count, add):
+        def body(k, carry):
+            lhs = s_ref[pl.ds(pl.multiple_of(k * 8, 8), 8)].reshape(256, TOKENS)
+            spot = pl.ds(pl.multiple_of(k * 64, 64), 64)
+            for j in range(count):
+                g = dot(lhs, b_ref[TOKENS * j : TOKENS * (j + 1)])
+                cols = pl.ds(WIDE * (first + j), WIDE)
+                for i in range(4):
+                    block = g[64 * i : 64 * i + 64, :WIDE]
+                    wide[i, spot, cols] = wide[i, spot, cols] + block if add else block
+                cols = pl.ds(HALF + WIDE * (first + j), WIDE)
+                right = g[:, WIDE:]
+                wide[k, :, cols] = wide[k, :, cols] + right if add else right
+            return carry
+
+        lax.fori_loop(0, 4, body, 0)
+
+    rings = []
+    for which, (offset, width) in enumerate(extents):
+        for way in range(2):
+            for stage in range(2):
+                n = len(rings)
+                if stage == 0:
+                    part = wide.at[:, :, pl.ds(HALF * way + offset, width)]
+                else:
+                    part = (part_c, part_d)[way].at[:, :, pl.ds(offset, width)]
+                axis = ("dp_1", "dp_0")[(way + stage) % 2]
+                rings.append(ring_reduce(axis, part, *boxes[n], send.at[n], recv.at[n]))
+
+    def ring_step(which, stage, step):
+        offset, width = extents[which]
+        for way in range(2):
+
+            def into(half, cols, value, way=way):
+                if stage == 0:
+                    part = (part_c, part_d)[way].at[:, :, pl.ds(offset, width)]
+                    part[2 * half, :, cols] = value[:64]
+                    part[2 * half + 1, :, cols] = value[64:]
+                else:
+                    last.at[way, half, :, pl.ds(offset, width)][:, cols] = value
+
+            do = rings[4 * which + 2 * way + stage][step]
+            do(into) if step == 2 else do()
+
+    def z_copies(which):
+        codes, scales, codes_in, scales_in = boxes[8 + which]
+        return [
+            remote(a, b, z_send.at[2 * which + k], z_recv.at[2 * which + k], "dp_2", 1 - z)
+            for k, (a, b) in enumerate([(codes, codes_in), (scales, scales_in)])
+        ]
+
+    def z_start(which):
+        encode, _ = coder(*boxes[8 + which])
+        offset, width = extents[which]
+        for way in range(2):
+            encode(way, lambda cols, way=way: last.at[way, 1 - z, :, pl.ds(offset, width)][:, cols])
+        for c in z_copies(which):
+            c.start()
+
+    products(proj_t.at[:, core], heads.at[2], 3, 1, False)
+    pair(1).wait_recv()
+    pair(2).wait_recv()
+    products(proj_in, packed_in.at[pl.ds(3 * TOKENS, TOKENS)], 3, 1, True)
+    ring_step(1, 0, 0)
     for hp in range(4):
         cols = pl.ds(128 * hp, 128)
         q, k, v, da = qkv[0, :, cols], qkv[1, :, cols], qkv[2, :, cols], d_attn[:, cols]
@@ -646,83 +722,46 @@
         for j in range(3):
             joined = jnp.where(is_low, outs[0][j], outs[1][j]).astype(jnp.bfloat16)
             packed[TOKENS * j : TOKENS * (j + 1), cols] = joined
-        packed[3 * TOKENS :, cols] = heads[2, :, cols]
         if hp > 0:
-            pair(1 + hp).start()
-    pair(5).start()
-
-    def products(s_ref, p_ref, b_ref, add):
-        def body(k, carry):
-            rows = pl.ds(pl.multiple_of(k * 8, 8), 8)
-            s, p = (r[rows].reshape(256, TOKENS) for r in (s_ref, p_ref))
-            spot = pl.ds(pl.multiple_of(k * 64, 64), 64)
-            for j in range(4):
-                g = dot(p if j == 3 else s, b_ref[TOKENS * j : TOKENS * (j + 1)])
-                cols = pl.ds(512 * (j % 2), 512)
-                if j < 2:
-                    for i in range(4):
-                        block = g[64 * i : 64 * i + 64]
-                        part_a[i, spot, cols] = part_a[i, spot, cols] + block if add else block
-                else:
-                    part_b[k, :, cols] = part_b[k, :, cols] + g if add else g
-            return carry
-
-        lax.fori_loop(0, 4, body, 0)
-
-    products(shaped_t.at[:, core], proj_t.at[:, core], packed, False)
-    for k in range(6):
+            pair(2 + hp).start()
+    pair(6).start()
+    ring_step(1, 0, 1)
+    products(shaped_t.at[:, core], packed, 0, 3, False)
+    for k in (0, 3, 4, 5, 6):
         pair(k).wait_recv()
-    products(shaped_in, proj_in, packed_in, True)
-    rings = [
-        ring_reduce(axis, part, *boxes[k], send.at[k], recv.at[k])
-        for k, (axis, part) in enumerate(
-            [("dp_1", part_a), ("dp_0", part_b), ("dp_0", part_c), ("dp_1", part_d)]
-        )
-    ]
-
-    def into(part):
-        def store(which, cols, value):
-            part[2 * which, :, cols] = value[:64]
-            part[2 * which + 1, :, cols] = value[64:]
-
-        return store
-
-    rings[0][0]()
-    rings[1][0]()
-    rings[0][1]()
-    rings[1][1]()
-    rings[0][2](into(part_c))
-    rings[2][0]()
-    rings[1][2](into(part_d))
-    rings[3][0]()
-    rings[2][1]()
-    rings[3][1]()
-    z_copies = []
-    for k in range(2):
-
-        def store(which, cols, value, k=k):
-            last[k, which, :, cols] = value
-
-        rings[2 + k][2](store)
-        c = remote(
-            last.at[k, 1 - z], last_in.at[k], z_send.at[k], z_recv.at[k], "dp_2", 1 - z
-        )
-        c.start()
-        z_copies.append(c)
-    for k, c in enumerate(z_copies):
-        c.wait_recv()
-        both = last[k, z] + last_in[k]
-        out[2 * k] = both[:, :512]
-        out[2 * k + 1] = both[:, 512:]
-    for c in z_copies:
-        c.wait_send()
+    products(shaped_in, packed_in, 0, 3, True)
+    ring_step(0, 0, 0)
+    ring_step(1, 0, 2)
+    ring_step(0, 0, 1)
+    ring_step(0, 0, 2)
+    ring_step(0, 1, 0)
+    ring_step(1, 1, 0)
+    ring_step(0, 1, 1)
+    ring_step(1, 1, 1)
+    ring_step(0, 1, 2)
+    z_start(0)
+    ring_step(1, 1, 2)
+    z_start(1)
+    for which, (offset, width) in enumerate(extents):
+        _, decoded = coder(*boxes[8 + which])
+        for c in z_copies(which):
+            c.wait_recv()
+        for way in range(2):
+            for j in range(offset // WIDE, (offset + width) // WIDE):
+                cols, near = pl.ds(WIDE * j, WIDE), pl.ds(WIDE * j - offset, WIDE)
+                out[j, :, pl.ds(WIDE * way, WIDE)] = last[way, z, :, cols] + decoded(way, near)
+    leave = pltpu.make_async_copy(out, out_far, grads_sem)
+    leave.start()
     squares = jnp.sum(out[...] * out[...])
     row = lax.broadcasted_iota(jnp.int32, (8, 128), 0)
     value = jnp.where(row == 0, squares, loss_part)
     totals[...] = sum_over_all(value, inbox, sum_send, sum_recv)
+    leave.wait()
+    for c in [*z_copies(0), *z_copies(1)]:
+        c.wait_send()
     for c in swaps:
         c.wait_send()
-    for k in range(6):
+    for k in range(7):
         pair(k).wait_send()
     for which in range(3):
         for hp in range(4):
@@ -749,8 +788,15 @@
     vmem, smem = (pl.BlockSpec(memory_space=m) for m in (pltpu.VMEM, pltpu.SMEM))
     bf16, f32 = jnp.bfloat16, jnp.float32
 
-    def boxes(half):
-        return [pltpu.VMEM((6, half, HALF), jnp.int16), pltpu.VMEM((6, 1, HALF), f32)] * 2
+    def boxes(width):
+        return [
+            scratch
+            for half in (128, 32, 128, 32)
+            for scratch in [pltpu.VMEM((6, half, width), jnp.int16), pltpu.VMEM((6, 1, width), f32)] * 2
+        ]
+
+    def last_boxes(width):
+        return [pltpu.VMEM((2, 32, width), jnp.int16), pltpu.VMEM((2, 1, width), f32)] * 2
 
     def semaphores(*shape):
         return [pltpu.SemaphoreType.DMA(shape)] * 2
@@ -762,8 +808,9 @@
             jax.ShapeDtypeStruct((8, 128), f32),
         ),
         in_specs=[smem] * 3 + [vmem] * 9 + [pl.BlockSpec(memory_space=pl.ANY)] * 2 + [vmem] * 2,
-        out_specs=(vmem,) * 2,
+        out_specs=(pl.BlockSpec(memory_space=pl.ANY), vmem),
         scratch_shapes=[
+            pltpu.VMEM((4, 32, 512), f32),
             pltpu.VMEM((6, 4, 4, 2, 2, 2, 16, 512), bf16),
             pltpu.VMEM((3, D, 512), bf16),
             pltpu.VMEM((4, 4, 2, 2, 2, 16, 512), bf16),
@@ -790,21 +837,21 @@
             pltpu.VMEM((4, 64, HALF), f32),
             pltpu.SemaphoreType.DMA,
             pltpu.SemaphoreType.DMA,
+            pltpu.SemaphoreType.DMA,
             *semaphores(17),
             *semaphores(25),
             *semaphores(25),
             *semaphores(25),
-            *boxes(128),
-            *boxes(128),
-            *boxes(32),
-            *boxes(32),
+            *boxes(3 * WIDE),
+            *boxes(WIDE),
+            *last_boxes(3 * WIDE),
+            *last_boxes(WIDE),
             pltpu.VMEM((2, 2, 32, HALF), f32),
-            pltpu.VMEM((2, 32, HALF), f32),
-            *semaphores(6),
-            *semaphores(4, 6, 2),
-            *semaphores(2),
-            pltpu.VMEM((3, 8, 8, 128), f32),
-            *semaphores(3, 7),
+            *semaphores(7),
+            *semaphores(8, 6, 2),
+            *semaphores(4),
+            pltpu.VMEM((2, 16, 8, 128), f32),
+            *semaphores(2, 15),
         ],
         compiler_params=pltpu.CompilerParams(
             collective_id=2, has_side_effects=True, vmem_limit_bytes=63 * 2**20

time: 133 us -> 126 us (0.947)
  Pallas kernels: 130 us -> 124 us
    pallas_call x1, Pallas kernels: 128 us -> 121 us  [whole_step(): pl.pallas_call(step_kernel, out_shape=(jax.ShapeDtypeStruct((4, 32, 512),...]
where the time goes in v7:
time: 126 us
  Pallas kernels  124 us (98%)
  between operations  1.94 us (2%)
    pallas_call x1, Pallas kernels, whole_step(): pl.pallas_call(step_kernel, out_shape=(jax.ShapeDtypeStruct((4, 32, 512),...  121 us

profile of v7, /device:TPU:1, one launch (start us, length us, event | category | flops | bytes accessed | tf_op | source)
XLA Modules:
  0.0 125.5 jit_solution(355331628574171081)
XLA Ops:
  1.9 121.5 %shard_map.243 = (f32[4,32,512]{2,1,0:T(8,128)}, f32[8,128]{1,0:T(8,128)}) custom-call(s32[1]{0:T(128)S(6)} %copy.27.timestep, s32[1]{0:T(128)S(6)} %copy.28.bucket, f32[8]{0:T(128)} %bucket_weights.1, f32[1,4096]{1,0:T(1,128)} %clean.1, f32[1,4096]{1,0:T(1,128)} %noise.1, f32[4,16,1024]{2,1,0:T(8,128)} %constant.2.clone.tables, f32[16,2048]{1,0:T(8,128)} %teacher_embed.1, ...), custom_call_target="tpu_custom_call" | custom-call | tf_op jit(solution)/shard_map/pallas_call | solution.py:804
  123.4 2.1 %shard_map.244 = (f32[3,32,512]{2,1,0:T(8,128)}, f32[3,32,512]{2,1,0:T(8,128)}, f32[3,32,512]{2,1,0:T(8,128)}, f32[32,512]{1,0:T(8,128)}, f32[32,512]{1,0:T(8,128)}, /*index=5*/f32[32,512]{1,0:T(8,128)}, f32[1,1]{1,0:T(1,128)}) custom-call(f32[4,32,512]{2,1,0:T(8,128)} %get-tuple-element.16.grads, f32[8,128]{1,0:T(8,128)} %get-tuple-element.17.totals, ...), custom_call_target="tpu_custom_call" | custom-call | tf_op jit(solution)/shard_map/pallas_call | solution.py:901

commit v8 on v7

--- a/solution.py
+++ b/solution.py
@@ -547,9 +547,12 @@
             src = src.at[:, 1 - core]
         elif k == 2:
             src, dst = heads.at[2], packed_in.at[pl.ds(3 * TOKENS, TOKENS)]
+        elif k == 3:
+            rows = pl.ds(2 * TOKENS, TOKENS)
+            src, dst = packed.at[rows], packed_in.at[rows]
         else:
-            cols = pl.ds(128 * (k - 3), 128)
-            src, dst = packed.at[:, cols], packed_in.at[pl.ds(0, 3 * TOKENS), cols]
+            rows, cols = pl.ds(0, 2 * TOKENS), pl.ds(128 * (k - 4), 128)
+            src, dst = packed.at[rows, cols], packed_in.at[rows, cols]
         return remote(src, dst, pair_send.at[k], pair_recv.at[k], "dp_3", 1 - core)
 
     half = D // 2
@@ -577,12 +580,8 @@
     t_step(2)
     mix(heads.at[0], near_rows, 0, hidden)
     s_step(3)
-    stack(split_rows(student_embed), embed_s)
     repeat(split_rows(teacher_final), final_b)
-    spread(lat0, embed_s, hidden_s, placed)
     t_step(3)
-    shape(hidden_s, 2, shaped_s)
-    turn(shaped_s, shaped_t)
     t_step(4)
     swapped(0)
     mix(heads_in.at[0], other_rows(5), 0, mixed)
@@ -598,6 +597,9 @@
     o_step(0)
     attend(1, False)
     mix(heads.at[1], near_rows, 1, hidden)
+    stack(split_rows(student_embed), embed_s)
+    spread(lat0, embed_s, hidden_s, placed)
+    shape(hidden_s, 2, shaped_s)
     swapped(1)
     mix(heads_in.at[1], other_rows(5), 1, mixed)
     s_step(5)
@@ -606,7 +608,6 @@
     lat2 = a_l * (lat1 - s_m * eps1) / a_m + s_l * eps1
     target = (lat0 - a_f / a_l * lat2) / (s_f - a_f * s_l / a_l)
 
-    pair(0).start()
     student_terms = split_rows(student_final)
     repeat(student_terms, final_b)
     stack(student_terms, embed_t)
@@ -616,9 +617,11 @@
     attend(2, True)
     mix(heads.at[2], other_rows(3), 2, hidden_s)
     o_step(3)
+    turn(shaped_s, shaped_t)
     swapped(2)
     o_step(4)
     mix(heads_in.at[2], other_rows(4), 2, mixed)
+    pair(0).start()
     error = predict(final_b, True) - target
     lanes = lax.broadcasted_iota(jnp.int32, error.shape, 1)
     loss_part = (
@@ -643,7 +646,7 @@
     d_attn[...] = dot(shaped[...], held[3].reshape(D, 512)).astype(jnp.bfloat16)
     pair(1).start()
 
-    extents = [(0, 3 * WIDE), (3 * WIDE, WIDE)]
+    extents = [(0, 2 * WIDE), (2 * WIDE, 2 * WIDE)]
 
     def products(s_ref, b_ref, first, count, add):
         def body(k, carry):
@@ -704,10 +707,20 @@
         for c in z_copies(which):
             c.start()
 
+    for hp in range(4):
+        cols = pl.ds(128 * hp, 128)
+        da = d_attn[:, cols]
+        outs = [dot(weights[2 * hp + h].astype(jnp.bfloat16), da, TN) for h in range(2)]
+        packed[2 * TOKENS :, cols] = jnp.where(is_low, outs[0], outs[1]).astype(jnp.bfloat16)
     products(proj_t.at[:, core], heads.at[2], 3, 1, False)
+    pair(3).start()
     pair(1).wait_recv()
     pair(2).wait_recv()
     products(proj_in, packed_in.at[pl.ds(3 * TOKENS, TOKENS)], 3, 1, True)
+    products(shaped_t.at[:, core], packed.at[pl.ds(2 * TOKENS, TOKENS)], 2, 1, False)
+    pair(0).wait_recv()
+    pair(3).wait_recv()
+    products(shaped_in, packed_in.at[pl.ds(2 * TOKENS, TOKENS)], 2, 1, True)
     ring_step(1, 0, 0)
     for hp in range(4):
         cols = pl.ds(128 * hp, 128)
@@ -718,18 +731,18 @@
             dp = dot(da * sides[h], v, NT)
             ds = w * (dp - jnp.sum(w * dp, axis=-1, keepdims=True)) * 0.125
             ds = ds.astype(jnp.bfloat16)
-            outs.append((dot(ds, k), dot(ds, q, TN), dot(w.astype(jnp.bfloat16), da, TN)))
-        for j in range(3):
+            outs.append((dot(ds, k), dot(ds, q, TN)))
+        for j in range(2):
             joined = jnp.where(is_low, outs[0][j], outs[1][j]).astype(jnp.bfloat16)
             packed[TOKENS * j : TOKENS * (j + 1), cols] = joined
         if hp > 0:
-            pair(2 + hp).start()
-    pair(6).start()
+            pair(3 + hp).start()
+    pair(7).start()
+    products(shaped_t.at[:, core], packed, 0, 2, False)
     ring_step(1, 0, 1)
-    products(shaped_t.at[:, core], packed, 0, 3, False)
-    for k in (0, 3, 4, 5, 6):
+    for k in (4, 5, 6, 7):
         pair(k).wait_recv()
-    products(shaped_in, packed_in, 0, 3, True)
+    products(shaped_in, packed_in, 0, 2, True)
     ring_step(0, 0, 0)
     ring_step(1, 0, 2)
     ring_step(0, 0, 1)
@@ -761,7 +774,7 @@
         c.wait_send()
     for c in swaps:
         c.wait_send()
-    for k in range(7):
+    for k in range(8):
         pair(k).wait_send()
     for which in range(3):
         for hp in range(4):
@@ -842,12 +855,12 @@
             *semaphores(25),
             *semaphores(25),
             *semaphores(25),
-            *boxes(3 * WIDE),
-            *boxes(WIDE),
-            *last_boxes(3 * WIDE),
-            *last_boxes(WIDE),
+            *boxes(2 * WIDE),
+            *boxes(2 * WIDE),
+            *last_boxes(2 * WIDE),
+            *last_boxes(2 * WIDE),
             pltpu.VMEM((2, 2, 32, HALF), f32),
-            *semaphores(7),
+            *semaphores(8),
             *semaphores(8, 6, 2),
             *semaphores(4),
             pltpu.VMEM((2, 16, 8, 128), f32),

time: 126 us -> 124 us (0.984)
  Pallas kernels: 124 us -> 121 us
    pallas_call x1, Pallas kernels: 121 us -> 119 us  [whole_step(): pl.pallas_call(step_kernel, out_shape=(jax.ShapeDtypeStruct((4, 32, 512),...]
where the time goes in v8:
time: 124 us; the launch traced here: 123 us
  Pallas kernels  121 us (98%)
  between operations  1.94 us (2%)
    pallas_call x1, Pallas kernels, whole_step(): pl.pallas_call(step_kernel, out_shape=(jax.ShapeDtypeStruct((4, 32, 512),...  119 us

profile of v8, /device:TPU:1, one launch (start us, length us, event | category | flops | bytes accessed | tf_op | source)
XLA Modules:
  0.0 123.3 jit_solution(13604652948974979349)
XLA Ops:
  1.9 119.3 %shard_map.243 = (f32[4,32,512]{2,1,0:T(8,128)}, f32[8,128]{1,0:T(8,128)}) custom-call(s32[1]{0:T(128)S(6)} %copy.27.timestep, s32[1]{0:T(128)S(6)} %copy.28.bucket, f32[8]{0:T(128)} %bucket_weights.1, f32[1,4096]{1,0:T(1,128)} %clean.1, f32[1,4096]{1,0:T(1,128)} %noise.1, f32[4,16,1024]{2,1,0:T(8,128)} %constant.2.clone.tables, f32[16,2048]{1,0:T(8,128)} %teacher_embed.1, ...), custom_call_target="tpu_custom_call" | custom-call | tf_op jit(solution)/shard_map/pallas_call | solution.py:817
  121.2 2.1 %shard_map.244 = (f32[3,32,512]{2,1,0:T(8,128)}, f32[3,32,512]{2,1,0:T(8,128)}, f32[3,32,512]{2,1,0:T(8,128)}, f32[32,512]{1,0:T(8,128)}, f32[32,512]{1,0:T(8,128)}, /*index=5*/f32[32,512]{1,0:T(8,128)}, f32[1,1]{1,0:T(1,128)}) custom-call(f32[4,32,512]{2,1,0:T(8,128)} %get-tuple-element.16.grads, f32[8,128]{1,0:T(8,128)} %get-tuple-element.17.totals, ...), custom_call_target="tpu_custom_call" | custom-call | tf_op jit(solution)/shard_map/pallas_call | solution.py:914

commit v9 on v8

--- a/solution.py
+++ b/solution.py
@@ -745,16 +745,16 @@
     products(shaped_in, packed_in, 0, 2, True)
     ring_step(0, 0, 0)
     ring_step(1, 0, 2)
+    ring_step(1, 1, 0)
     ring_step(0, 0, 1)
+    ring_step(1, 1, 1)
     ring_step(0, 0, 2)
     ring_step(0, 1, 0)
-    ring_step(1, 1, 0)
+    ring_step(1, 1, 2)
+    z_start(1)
     ring_step(0, 1, 1)
-    ring_step(1, 1, 1)
     ring_step(0, 1, 2)
     z_start(0)
-    ring_step(1, 1, 2)
-    z_start(1)
     for which, (offset, width) in enumerate(extents):
         _, decoded = coder(*boxes[8 + which])
         for c in z_copies(which):

time: 124 us -> 124 us (level)
  no operation moved by 1% of the time
where the time goes in v9:
time: 124 us
  Pallas kernels  122 us (98%)
  between operations  1.94 us (2%)
    pallas_call x1, Pallas kernels, whole_step(): pl.pallas_call(step_kernel, out_shape=(jax.ShapeDtypeStruct((4, 32, 512),...  120 us

profile of v9, /device:TPU:1, one launch (start us, length us, event | category | flops | bytes accessed | tf_op | source)
XLA Modules:
  0.0 123.8 jit_solution(2075296183156061295)
XLA Ops:
  1.9 119.7 %shard_map.243 = (f32[4,32,512]{2,1,0:T(8,128)}, f32[8,128]{1,0:T(8,128)}) custom-call(s32[1]{0:T(128)S(6)} %copy.27.timestep, s32[1]{0:T(128)S(6)} %copy.28.bucket, f32[8]{0:T(128)} %bucket_weights.1, f32[1,4096]{1,0:T(1,128)} %clean.1, f32[1,4096]{1,0:T(1,128)} %noise.1, f32[4,16,1024]{2,1,0:T(8,128)} %constant.2.clone.tables, f32[16,2048]{1,0:T(8,128)} %teacher_embed.1, ...), custom_call_target="tpu_custom_call" | custom-call | tf_op jit(solution)/shard_map/pallas_call | solution.py:817
  121.7 2.1 %shard_map.244 = (f32[3,32,512]{2,1,0:T(8,128)}, f32[3,32,512]{2,1,0:T(8,128)}, f32[3,32,512]{2,1,0:T(8,128)}, f32[32,512]{1,0:T(8,128)}, f32[32,512]{1,0:T(8,128)}, /*index=5*/f32[32,512]{1,0:T(8,128)}, f32[1,1]{1,0:T(1,128)}) custom-call(f32[4,32,512]{2,1,0:T(8,128)} %get-tuple-element.16.grads, f32[8,128]{1,0:T(8,128)} %get-tuple-element.17.totals, ...), custom_call_target="tpu_custom_call" | custom-call | tf_op jit(solution)/shard_map/pallas_call | solution.py:914

commit v10 on v8

--- a/solution.py
+++ b/solution.py
@@ -535,11 +535,13 @@
 
     def turn(src, out):
         def body(n, carry):
-            t = src[:, columns(n, 128)].astype(jnp.float32).T.astype(jnp.bfloat16)
-            out[pl.ds(2 * n, 2)] = t.reshape(2, 2, 32, TOKENS)
+            for u in range(4):
+                m = 4 * n + u
+                t = src[:, columns(m, 128)].astype(jnp.float32).T.astype(jnp.bfloat16)
+                out[pl.ds(2 * m, 2)] = t.reshape(2, 2, 32, TOKENS)
             return carry
 
-        lax.fori_loop(0, D // 128, body, 0)
+        lax.fori_loop(0, D // 512, body, 0)
 
     def pair(k):
         if k < 2:
@@ -649,9 +651,9 @@
     extents = [(0, 2 * WIDE), (2 * WIDE, 2 * WIDE)]
 
     def products(s_ref, b_ref, first, count, add):
-        def body(k, carry):
-            lhs = s_ref[pl.ds(pl.multiple_of(k * 8, 8), 8)].reshape(256, TOKENS)
-            spot = pl.ds(pl.multiple_of(k * 64, 64), 64)
+        for k in range(4):
+            lhs = s_ref[pl.ds(8 * k, 8)].reshape(256, TOKENS)
+            spot = pl.ds(64 * k, 64)
             for j in range(count):
                 g = dot(lhs, b_ref[TOKENS * j : TOKENS * (j + 1)])
                 cols = pl.ds(WIDE * (first + j), WIDE)
@@ -661,9 +663,6 @@
                 cols = pl.ds(HALF + WIDE * (first + j), WIDE)
                 right = g[:, WIDE:]
                 wide[k, :, cols] = wide[k, :, cols] + right if add else right
-            return carry
-
-        lax.fori_loop(0, 4, body, 0)
 
     rings = []
     for which, (offset, width) in enumerate(extents):

time: 124 us -> 120 us (0.968)
  Pallas kernels: 121 us -> 118 us
    pallas_call x1, Pallas kernels: 119 us -> 116 us  [whole_step(): pl.pallas_call(step_kernel, out_shape=(jax.ShapeDtypeStruct((4, 32, 512),...]
where the time goes in v10:
time: 120 us
  Pallas kernels  118 us (98%)
  between operations  1.94 us (2%)
    pallas_call x1, Pallas kernels, whole_step(): pl.pallas_call(step_kernel, out_shape=(jax.ShapeDtypeStruct((4, 32, 512),...  116 us

profile of v10, /device:TPU:1, one launch (start us, length us, event | category | flops | bytes accessed | tf_op | source)
XLA Modules:
  0.0 119.8 jit_solution(9668611411662441589)
XLA Ops:
  1.9 115.7 %shard_map.243 = (f32[4,32,512]{2,1,0:T(8,128)}, f32[8,128]{1,0:T(8,128)}) custom-call(s32[1]{0:T(128)S(6)} %copy.27.timestep, s32[1]{0:T(128)S(6)} %copy.28.bucket, f32[8]{0:T(128)} %bucket_weights.1, f32[1,4096]{1,0:T(1,128)} %clean.1, f32[1,4096]{1,0:T(1,128)} %noise.1, f32[4,16,1024]{2,1,0:T(8,128)} %constant.2.clone.tables, f32[16,2048]{1,0:T(8,128)} %teacher_embed.1, ...), custom_call_target="tpu_custom_call" | custom-call | tf_op jit(solution)/shard_map/pallas_call | solution.py:816
  117.6 2.1 %shard_map.244 = (f32[3,32,512]{2,1,0:T(8,128)}, f32[3,32,512]{2,1,0:T(8,128)}, f32[3,32,512]{2,1,0:T(8,128)}, f32[32,512]{1,0:T(8,128)}, f32[32,512]{1,0:T(8,128)}, /*index=5*/f32[32,512]{1,0:T(8,128)}, f32[1,1]{1,0:T(1,128)}) custom-call(f32[4,32,512]{2,1,0:T(8,128)} %get-tuple-element.16.grads, f32[8,128]{1,0:T(8,128)} %get-tuple-element.17.totals, ...), custom_call_target="tpu_custom_call" | custom-call | tf_op jit(solution)/shard_map/pallas_call | solution.py:913
